TPU v7x, 256 devices: a whole 4x4x8 slice. The times are simulated.
256 devices in a mesh: rows: 32 (over y, x, core), grp: 8 (over z).
Axes of the slice: x: 4, y: 4, z: 8, core: 2. Of those that a mesh axis runs over, the one named last changes fastest.
Arguments:
- matrix: bfloat16 [131072, 2048], P(('rows', 'grp')), may hold values from -0.0625 to 0.0625
- right_side: bfloat16 [131072, 128], P(('rows', 'grp')), may hold values from -6 to 6
- precond: bfloat16 [2048, 2048], replicated, may hold values from -1 to 3
- row_counts: int32 [256], P(('rows', 'grp')), may hold values from 64 to 512, as said below
Outputs:
- solution: float32 [2048, 128], P(None, 'grp')
- coeffs: float32 [2048, 128], P(None, 'grp')
- rel_residual: float32 [128], P('grp')
Inputs may be any that keep to these rules, and one draw needn't show every extreme that they name: Device d holds A's rows in its first row_counts[d] slots of 512; some device is full in every draw.
All inputs are finite; a program needn't handle non-finite values.
Results may differ from a plain program's by a relative error of at most 0.0128.
Values may be sent and summed in bfloat16 or wider, within the bound.
No kernel may reach another device: no remote copies, remote signals or barrier semaphores. Data moves between devices by JAX's collectives and lax.ppermute only.
A program may use at most 64 MiB of HBM per device.

v0:
```python
import jax
import jax.numpy as jnp
from jax import lax
from jax.sharding import PartitionSpec as P

ITERS = 3


floor_sq = 0.01


def cut_along(value, dim, peers):
    lengths = value.shape
    tiles = value.reshape(*lengths[:dim], peers, lengths[dim] // peers, *lengths[dim + 1 :])
    return jnp.moveaxis(tiles, dim, 0)


def sent_and_summed(value, axis, dim):
    peers = lax.axis_size(axis)
    tiles = lax.all_to_all(cut_along(value, dim, peers), axis, 0, 0, tiled=True)
    return jnp.sum(tiles, axis=0)


def sent_together(arrays, axis, dim, along):
    both = jnp.concatenate(arrays, axis=along)
    filled, at, gathered = (sent_and_summed(both, axis, dim), 0, [])
    for a in arrays:
        gathered.append(lax.slice_in_dim(filled, at, at + a.shape[along], axis=along))
        at += a.shape[along]
    return tuple(gathered)


def rows_for(lines, peers):
    spare = -lines.shape[0] % peers
    if not spare:
        return lines
    return jnp.concatenate([lines, jnp.zeros((spare, *lines.shape[1:]), lines.dtype)])


def joined_along(tiles, dim):
    lengths = list(tiles.shape[1:])
    lengths[dim] *= tiles.shape[0]
    return jnp.moveaxis(tiles, 0, dim).reshape(lengths)


def copy_for_each(value, axis):
    copies = jnp.broadcast_to(value, (lax.axis_size(axis), *value.shape))
    return lax.all_to_all(copies, axis, split_axis=0, concat_axis=0, tiled=True)


def gathered_copies(value, axis, dim):
    return joined_along(copy_for_each(value, axis), dim)


def sum_by_parts(value, axes):
    own = sent_and_summed(rows_for(value, lax.axis_size(axes)), axes, 0)
    whole = gathered_copies(own, axes, 0)
    return whole[: len(value)].reshape(value.shape)


def in_one(arrays, axis):
    ravelled, at, gathered = (jnp.concatenate([a.reshape(-1) for a in arrays]), 0, [])
    subtotal = sum_by_parts(ravelled, axis)
    for a in arrays:
        gathered.append(subtotal[at : at + a.size].reshape(a.shape))
        at += a.size
    return tuple(gathered)


def pull_partial(matrix, residue):
    partial_value = lax.dot_general(
        matrix,
        residue.astype(jnp.bfloat16),
        (((0,), (0,)), ((), ())),
        preferred_element_type=jnp.float32,
    )
    squares = jnp.sum(residue * residue, axis=0, keepdims=True)
    return (partial_value, squares)


def column_section(precond, partial_value, squares, right_vec):
    u_norm = jnp.sqrt(squares + floor_sq)
    pulled = lax.dot_general(
        precond,
        (partial_value / u_norm).astype(jnp.bfloat16),
        (((0,), (0,)), ((), ())),
        preferred_element_type=jnp.float32,
    )
    raw_vec = pulled - u_norm * right_vec
    v_norm = jnp.sqrt(jnp.sum(raw_vec * raw_vec, axis=0, keepdims=True) + floor_sq)
    return (u_norm, raw_vec / v_norm, v_norm)


def shards(matrix, right_side, precond, row_counts):
    local_rows, width = matrix.shape
    count = row_counts[0]
    live_rows = (lax.broadcasted_iota(jnp.int32, (local_rows, 1), 0) < count).astype(jnp.float32)

    def row_pass(pushed, v_norm_all, left_vec):
        if pushed is None:
            residue = live_rows * right_side.astype(jnp.float32)
        else:
            residue = live_rows * (
                jnp.dot(matrix, pushed, preferred_element_type=jnp.float32) - v_norm_all * left_vec
            )
        partial_value, squares = pull_partial(matrix, residue)
        return (residue, partial_value, squares)

    def reduce_cols(partial_value, squares):
        shared, shared_sq = sent_together((partial_value, squares), "grp", 1, 0)
        return in_one((shared, shared_sq), "rows")

    def share_cols(right_vec, v_norm, u_norm):
        pushed = jnp.dot(
            precond, right_vec.astype(jnp.bfloat16), preferred_element_type=jnp.float32
        ).astype(jnp.bfloat16)
        pushed = gathered_copies(pushed, "grp", 1)
        norms = gathered_copies(jnp.concatenate([v_norm, u_norm], axis=0), "grp", 1)
        return (pushed, norms[0:1], norms[1:2])

    residue, partial_value, squares = row_pass(None, None, None)
    partial_value, squares = reduce_cols(partial_value, squares)
    u_norm, right_vec, v_norm = column_section(
        precond, partial_value, squares, jnp.zeros((width, partial_value.shape[1]), jnp.float32)
    )
    phi_bar = u_norm
    rho_bar = v_norm
    search = right_vec
    coeffs = jnp.zeros(right_vec.shape, jnp.float32)
    start_norm = u_norm
    pushed, v_norm_all, u_norm_all = share_cols(right_vec, v_norm, u_norm)
    left_vec = residue / u_norm_all
    for turn_index in range(ITERS):
        residue, partial_value, squares = row_pass(pushed, v_norm_all, left_vec)
        partial_value, squares = reduce_cols(partial_value, squares)
        u_norm, next_vec, next_norm = column_section(precond, partial_value, squares, right_vec)
        radius = jnp.sqrt(rho_bar * rho_bar + u_norm * u_norm)
        cosine = rho_bar / radius
        sine_part = u_norm / radius
        coupling = sine_part * next_norm
        rho_bar = -cosine * next_norm
        phi_step = cosine * phi_bar
        phi_bar = sine_part * phi_bar
        coeffs = coeffs + phi_step / radius * search
        search = next_vec - coupling / radius * search
        right_vec = next_vec
        v_norm = next_norm
        if turn_index + 1 < ITERS:
            pushed, v_norm_all, u_norm_all = share_cols(right_vec, v_norm, u_norm)
            left_vec = residue / u_norm_all
    ratio = phi_bar / start_norm
    solution = jnp.dot(precond, coeffs.astype(jnp.bfloat16), preferred_element_type=jnp.float32)
    return (solution, coeffs, ratio[0])


def solution(mesh):
    return jax.shard_map(
        shards,
        mesh=mesh,
        in_specs=(P(("rows", "grp"), None), P(("rows", "grp"), None), P(), P(("rows", "grp"))),
        out_specs=(P(None, "grp"), P(None, "grp"), P("grp")),
        check_vma=False,
    )
```

profile of v0, /device:TPU:1, one launch (start us, length us, event | category | flops | bytes accessed | tf_op | source)
XLA Modules:
  0.0 400.8 jit_solution(16813123153177191530)
XLA Ops:
  1.5 1.0 copy.47
  3.3 37.6 %all_to_all.110 = f32[8,2049,16]{1,2,0:T(8,128)S(1)} all-to-all(f32[8,2049,16]{1,2,0:T(8,128)S(1)} %maximum_bitcast_fusion), channel_id=1, replica_groups=mesh['rows'=32,'grp'=8] {'grp'}, dimensions={0} | all-to-all | bytes 2098176 | tf_op jit(solution)/shard_map/all_to_all | solution.py:20
  40.9 0.7 reduce_sum.136
  41.6 0.8 slice_reduce_fusion.3
  42.4 0.9 slice.113
  44.4 16.9 %all_to_all.111 = f32[32,1,1025]{2,1,0:T(1,128)S(1)} all-to-all(f32[32,1,1025]{2,1,0:T(1,128)S(1)} %all_to_all.71), channel_id=1, replica_groups=mesh['rows'=32,'grp'=8] {'rows'}, dimensions={0} | all-to-all | bytes 262400 | tf_op jit(solution)/shard_map/all_to_all | solution.py:20
  61.5 11.4 %all_to_all.112 = f32[32,1,1025]{2,1,0:T(1,128)S(1)} all-to-all(f32[32,1,1025]{2,1,0:T(1,128)S(1)} %broadcast_in_dim.38), channel_id=1, replica_groups=mesh['rows'=32,'grp'=8] {'rows'}, dimensions={0} | all-to-all | bytes 262400 | tf_op jit(solution)/shard_map/all_to_all | solution.py:48
  73.2 0.8 reshape.238
  74.7 0.7 broadcast_multiply_fusion
  75.4 4.7 %multiply_reduce_fusion.6 = (f32[16]{0:T(128)S(1)}, f32[16,2048]{1,0:T(8,128)S(1)}) fusion(f32[16]{0:T(128)S(1)} %get-tuple-element.16, bf16[2048,2048]{1,0:T(8,128)(2,1)} %param.6, f32[2050,16]{1,0:T(8,128)S(1)} %slice.91, f32[16]{0:T(128)S(1)} %get-tuple-element.17), kind=kOutput, calls=%fused_computation.48 | convolution fusion | flops 134381552 | bytes 9569344 | tf_op jit(solution)/shard_map/dot_general | solution.py:83
  80.7 3.3 all-to-all-start.4
  84.1 5.7 %fusion = bf16[2048,16]{0,1:T(8,128)(2,1)S(1)} fusion(bf16[2048,2048]{1,0:T(8,128)(2,1)} %param.6, f32[16,2048]{1,0:T(8,128)S(1)} %get-tuple-element.34, f32[16]{0:T(128)S(1)} %get-tuple-element.32), kind=kOutput, calls=%fused_computation.7 | convolution fusion | flops 134316032 | bytes 8585280 | tf_op jit(solution)/shard_map/dot_general | solution.py:114
  89.7 0.9 all-to-all-done.4
  90.6 0.8 broadcast_in_dim.39
  91.4 5.7 %all-to-all-start.3 = ((bf16[8,2048,16]{1,2,0:T(8,128)(2,1)}), bf16[8,2048,16]{1,2,0:T(8,128)(2,1)S(1)}, u32[]{:S(2)}, u32[]{:S(2)}) async-start(bf16[8,2048,16]{1,2,0:T(8,128)(2,1)} %broadcast_in_dim.39), calls=%async_computation.3 | async-start | bytes 1048576 | tf_op jit(solution)/shard_map/all_to_all | solution.py:48
  97.3 17.8 %all-to-all-done.3 = bf16[8,2048,16]{1,2,0:T(8,128)(2,1)S(1)} async-done(((bf16[8,2048,16]{1,2,0:T(8,128)(2,1)}), bf16[8,2048,16]{1,2,0:T(8,128)(2,1)S(1)}, u32[]{:S(2)}, u32[]{:S(2)}) %all-to-all-start.3) | async-done | bytes 524320 | tf_op jit(solution)/shard_map/all_to_all | solution.py:48
  115.1 0.9 multiply_reduce_fusion.2
  116.8 32.3 %all_to_all.113 = f32[8,2049,16]{1,2,0:T(8,128)S(1)} all-to-all(f32[8,2049,16]{1,2,0:T(8,128)S(1)} %maximum_bitcast_fusion.1), channel_id=1, replica_groups=mesh['rows'=32,'grp'=8] {'grp'}, dimensions={0} | all-to-all | bytes 2098176 | tf_op jit(solution)/shard_map/all_to_all | solution.py:20
  149.9 1.2 copy.52
  151.8 12.1 %all_to_all.114 = f32[32,1,1025]{2,1,0:T(1,128)S(1)} all-to-all(f32[32,1,1025]{2,1,0:T(1,128)S(1)} %all_to_all.77), channel_id=1, replica_groups=mesh['rows'=32,'grp'=8] {'rows'}, dimensions={0} | all-to-all | bytes 262400 | tf_op jit(solution)/shard_map/all_to_all | solution.py:20
  164.1 11.4 %all_to_all.115 = f32[32,1,1025]{2,1,0:T(1,128)S(1)} all-to-all(f32[32,1,1025]{2,1,0:T(1,128)S(1)} %broadcast_in_dim.41), channel_id=1, replica_groups=mesh['rows'=32,'grp'=8] {'rows'}, dimensions={0} | all-to-all | bytes 262400 | tf_op jit(solution)/shard_map/all_to_all | solution.py:48
  175.8 0.8 reshape.242
  177.3 0.7 fusion.42
  178.0 4.7 %multiply_reduce_fusion.5 = (f32[16]{0:T(128)S(1)}, f32[16,2048]{1,0:T(8,128)S(1)}) fusion(f32[16,2048]{1,0:T(8,128)S(1)} %get-tuple-element.34, f32[16]{0:T(128)S(1)} %get-tuple-element.32, f32[16]{0:T(128)S(1)} %get-tuple-element.21, bf16[2048,2048]{1,0:T(8,128)(2,1)} %param.6, f32[2050,16]{1,0:T(8,128)S(1)} %slice.99), kind=kOutput, calls=%fused_computation.41 | convolution fusion | flops 134447088 | bytes 9700928 | tf_op jit(solution)/shard_map/dot_general | solution.py:83
  183.3 3.3 all-to-all-start.9
  186.7 5.7 %fusion.1 = bf16[2048,16]{0,1:T(8,128)(2,1)S(1)} fusion(bf16[2048,2048]{1,0:T(8,128)(2,1)} %param.6, f32[16,2048]{1,0:T(8,128)S(1)} %get-tuple-element.38, f32[16]{0:T(128)S(1)} %get-tuple-element.30), kind=kOutput, calls=%fused_computation.8 | convolution fusion | flops 134316032 | bytes 8585280 | tf_op jit(solution)/shard_map/dot_general | solution.py:114
  192.4 0.8 all-to-all-done.9
  193.2 0.8 broadcast_in_dim.42
  194.0 5.8 %all-to-all-start.8 = ((bf16[8,2048,16]{1,2,0:T(8,128)(2,1)}), bf16[8,2048,16]{1,2,0:T(8,128)(2,1)S(1)}, u32[]{:S(2)}, u32[]{:S(2)}) async-start(bf16[8,2048,16]{1,2,0:T(8,128)(2,1)} %broadcast_in_dim.42), calls=%async_computation.8 | async-start | bytes 1048576 | tf_op jit(solution)/shard_map/all_to_all | solution.py:48
  200.0 17.8 %all-to-all-done.8 = bf16[8,2048,16]{1,2,0:T(8,128)(2,1)S(1)} async-done(((bf16[8,2048,16]{1,2,0:T(8,128)(2,1)}), bf16[8,2048,16]{1,2,0:T(8,128)(2,1)S(1)}, u32[]{:S(2)}, u32[]{:S(2)}) %all-to-all-start.8) | async-done | bytes 524320 | tf_op jit(solution)/shard_map/all_to_all | solution.py:48
  217.7 0.9 multiply_reduce_fusion.1
  219.5 32.0 %all_to_all.116 = f32[8,2049,16]{1,2,0:T(8,128)S(1)} all-to-all(f32[8,2049,16]{1,2,0:T(8,128)S(1)} %maximum_bitcast_fusion.2), channel_id=1, replica_groups=mesh['rows'=32,'grp'=8] {'grp'}, dimensions={0} | all-to-all | bytes 2098176 | tf_op jit(solution)/shard_map/all_to_all | solution.py:20
  251.5 0.7 reduce_sum.144
  252.2 0.8 slice_reduce_fusion.1
  253.0 1.6 slice.125
  254.6 1.2 copy.55
  255.8 1.0 reshape.244
  256.8 1.0 concatenate.66
  258.0 12.3 %all_to_all.117 = f32[32,1,1025]{2,1,0:T(1,128)S(1)} all-to-all(f32[32,1,1025]{2,1,0:T(1,128)S(1)} %all_to_all.83), channel_id=1, replica_groups=mesh['rows'=32,'grp'=8] {'rows'}, dimensions={0} | all-to-all | bytes 262400 | tf_op jit(solution)/shard_map/all_to_all | solution.py:20
  270.5 11.4 %all_to_all.118 = f32[32,1,1025]{2,1,0:T(1,128)S(1)} all-to-all(f32[32,1,1025]{2,1,0:T(1,128)S(1)} %broadcast_in_dim.44), channel_id=1, replica_groups=mesh['rows'=32,'grp'=8] {'rows'}, dimensions={0} | all-to-all | bytes 262400 | tf_op jit(solution)/shard_map/all_to_all | solution.py:48
  281.9 1.0 reduce.18
  282.9 1.7 reshape.246
  284.6 1.6 slice.106
  286.3 0.7 fusion.45
  287.0 5.4 %multiply_reduce_fusion.4 = (f32[16]{0:T(128)S(1)}, f32[16,2048]{1,0:T(8,128)}) fusion(f32[16,2048]{1,0:T(8,128)S(1)} %get-tuple-element.38, f32[16]{0:T(128)S(1)} %get-tuple-element.30, f32[16]{0:T(128)S(1)} %get-tuple-element.19, bf16[2048,2048]{1,0:T(8,128)(2,1)} %param.6, f32[2050,16]{1,0:T(8,128)S(1)} %slice.106), kind=kOutput, calls=%fused_computation.40 | convolution fusion | flops 134447088 | bytes 9700928 | tf_op jit(solution)/shard_map/dot_general | solution.py:83
  293.0 3.3 all-to-all-start.14
  296.3 5.8 %fusion.2 = bf16[2048,16]{0,1:T(8,128)(2,1)S(1)} fusion(bf16[2048,2048]{1,0:T(8,128)(2,1)} %param.6, f32[16,2048]{1,0:T(8,128)} %get-tuple-element.42, f32[16]{0:T(128)S(1)} %get-tuple-element.28), kind=kOutput, calls=%fused_computation.9 | convolution fusion | flops 134316032 | bytes 8585280 | tf_op jit(solution)/shard_map/dot_general | solution.py:114
  302.1 0.7 all-to-all-done.14
  302.8 0.8 broadcast_in_dim.45
  303.7 5.8 %all-to-all-start.13 = ((bf16[8,2048,16]{1,2,0:T(8,128)(2,1)}), bf16[8,2048,16]{1,2,0:T(8,128)(2,1)S(1)}, u32[]{:S(2)}, u32[]{:S(2)}) async-start(bf16[8,2048,16]{1,2,0:T(8,128)(2,1)} %broadcast_in_dim.45), calls=%async_computation.13 | async-start | bytes 1048576 | tf_op jit(solution)/shard_map/all_to_all | solution.py:48
  309.7 17.8 %all-to-all-done.13 = bf16[8,2048,16]{1,2,0:T(8,128)(2,1)S(1)} async-done(((bf16[8,2048,16]{1,2,0:T(8,128)(2,1)}), bf16[8,2048,16]{1,2,0:T(8,128)(2,1)S(1)}, u32[]{:S(2)}, u32[]{:S(2)}) %all-to-all-start.13) | async-done | bytes 524320 | tf_op jit(solution)/shard_map/all_to_all | solution.py:48
  327.5 0.9 multiply_reduce_fusion
  329.2 32.0 %all_to_all.119 = f32[8,2049,16]{1,2,0:T(8,128)S(1)} all-to-all(f32[8,2049,16]{1,2,0:T(8,128)S(1)} %maximum_bitcast_fusion.3), channel_id=1, replica_groups=mesh['rows'=32,'grp'=8] {'grp'}, dimensions={0} | all-to-all | bytes 2098176 | tf_op jit(solution)/shard_map/all_to_all | solution.py:20
  361.2 0.7 reduce_sum.148
  361.9 0.8 slice_reduce_fusion
  362.7 1.6 slice.131
  364.3 1.2 copy.58
  365.5 1.0 reshape.248
  366.5 1.0 concatenate.71
  367.7 12.3 %all_to_all.120 = f32[32,1,1025]{2,1,0:T(1,128)S(1)} all-to-all(f32[32,1,1025]{2,1,0:T(1,128)S(1)} %all_to_all.89), channel_id=1, replica_groups=mesh['rows'=32,'grp'=8] {'rows'}, dimensions={0} | all-to-all | bytes 262400 | tf_op jit(solution)/shard_map/all_to_all | solution.py:20
  380.2 11.4 %all_to_all.121 = f32[32,1,1025]{2,1,0:T(1,128)S(1)} all-to-all(f32[32,1,1025]{2,1,0:T(1,128)S(1)} %broadcast_in_dim.47), channel_id=1, replica_groups=mesh['rows'=32,'grp'=8] {'rows'}, dimensions={0} | all-to-all | bytes 262400 | tf_op jit(solution)/shard_map/all_to_all | solution.py:48
  392.1 1.3 multiply_divide_fusion
  393.4 1.0 add_bitcast_fusion
  394.5 6.4 %convolution_bitcast_fusion = f32[2048,16]{0,1:T(8,128)} fusion(bf16[2048,2048]{1,0:T(8,128)(2,1)} %param.6, f32[2048,16]{0,1:T(8,128)S(1)} %add_bitcast_fusion), kind=kOutput, calls=%fused_computation | convolution fusion | flops 134250496 | bytes 8650752 | tf_op jit(solution)/shard_map/dot_general | solution.py:152
  (72 shorter events, 11.7 us)
Async XLA Ops:
  0.6 2.2 copy-start
  80.7 9.9 %all-to-all-start.4 = ((f32[8,2,16]{2,1,0:T(2,128)}), f32[8,2,16]{2,1,0:T(2,128)S(1)}, u32[]{:S(2)}, u32[]{:S(2)}) async-start(f32[8,2,16]{2,1,0:T(2,128)} %broadcast_in_dim.40), calls=%async_computation.4 | async-start | bytes 16384 | tf_op jit(solution)/shard_map/all_to_all | solution.py:48
  91.4 23.7 %all-to-all-start.3 = ((bf16[8,2048,16]{1,2,0:T(8,128)(2,1)}), bf16[8,2048,16]{1,2,0:T(8,128)(2,1)S(1)}, u32[]{:S(2)}, u32[]{:S(2)}) async-start(bf16[8,2048,16]{1,2,0:T(8,128)(2,1)} %broadcast_in_dim.39), calls=%async_computation.3 | async-start | bytes 1048576 | tf_op jit(solution)/shard_map/all_to_all | solution.py:48
  116.0 0.7 copy-start.4
  183.3 9.9 %all-to-all-start.9 = ((f32[8,2,16]{2,1,0:T(2,128)}), f32[8,2,16]{2,1,0:T(2,128)S(1)}, u32[]{:S(2)}, u32[]{:S(2)}) async-start(f32[8,2,16]{2,1,0:T(2,128)} %broadcast_in_dim.43), calls=%async_computation.9 | async-start | bytes 16384 | tf_op jit(solution)/shard_map/all_to_all | solution.py:48
  186.7 31.1 %copy-start.5 = (f32[512,128]{0,1:T(8,128)S(1)}, f32[512,128]{0,1:T(8,128)}, u32[]{:S(2)}) copy-start(f32[512,128]{0,1:T(8,128)} %copy-done.4) | copy-start | bytes 786436
  194.0 23.7 %all-to-all-start.8 = ((bf16[8,2048,16]{1,2,0:T(8,128)(2,1)}), bf16[8,2048,16]{1,2,0:T(8,128)(2,1)S(1)}, u32[]{:S(2)}, u32[]{:S(2)}) async-start(bf16[8,2048,16]{1,2,0:T(8,128)(2,1)} %broadcast_in_dim.42), calls=%async_computation.8 | async-start | bytes 1048576 | tf_op jit(solution)/shard_map/all_to_all | solution.py:48
  218.7 0.7 copy-start.2
  293.0 9.9 %all-to-all-start.14 = ((f32[8,2,16]{2,1,0:T(2,128)}), f32[8,2,16]{2,1,0:T(2,128)S(1)}, u32[]{:S(2)}, u32[]{:S(2)}) async-start(f32[8,2,16]{2,1,0:T(2,128)} %broadcast_in_dim.46), calls=%async_computation.14 | async-start | bytes 16384 | tf_op jit(solution)/shard_map/all_to_all | solution.py:48
  296.3 31.2 %copy-start.3 = (f32[512,128]{0,1:T(8,128)S(1)}, f32[512,128]{0,1:T(8,128)}, u32[]{:S(2)}) copy-start(f32[512,128]{0,1:T(8,128)} %copy-done.2) | copy-start | bytes 786436
  303.7 23.8 %all-to-all-start.13 = ((bf16[8,2048,16]{1,2,0:T(8,128)(2,1)}), bf16[8,2048,16]{1,2,0:T(8,128)(2,1)S(1)}, u32[]{:S(2)}, u32[]{:S(2)}) async-start(bf16[8,2048,16]{1,2,0:T(8,128)(2,1)} %broadcast_in_dim.45), calls=%async_computation.13 | async-start | bytes 1048576 | tf_op jit(solution)/shard_map/all_to_all | solution.py:48
  394.5 6.4 %copy-start.1 = (f32[2048,16]{0,1:T(8,128)}, f32[2048,16]{0,1:T(8,128)S(1)}, u32[]{:S(2)}) copy-start(f32[2048,16]{0,1:T(8,128)S(1)} %add_bitcast_fusion) | copy-start | bytes 393220
where the time goes:
time: 402 us; the launch traced here: 401 us
  blocking collectives  233 us (58%)
  waiting for transfers between devices  55.7 us (14%)
  matrix products  42.8 us (11%)
  local copies, waits for them, and re-layouts  30.4 us (8%)
  starting transfers between devices  27.3 us (7%)
  other arithmetic  9.51 us (2%)
    all_to_all x8, blocking collectives, sent_and_summed(): tiles = lax.all_to_all(cut_along(value, dim, peers), axis, 0, 0, tiled=True)  188 us
    all_to_all x6, waiting for transfers between devices, copy_for_each(): return lax.all_to_all(copies, axis, split_axis=0, concat_axis=0, tiled=True)  55.7 us
    all_to_all x4, blocking collectives, copy_for_each(): return lax.all_to_all(copies, axis, split_axis=0, concat_axis=0, tiled=True)  45.6 us
    all_to_all x6, starting transfers between devices, copy_for_each(): return lax.all_to_all(copies, axis, split_axis=0, concat_axis=0, tiled=True)  27.3 us
    dot_general x3, matrix products, share_cols(): jnp.dot(precond, right_vec.astype(jnp.bfloat16), preferred_element_type=j...  17.1 us
    dot_general x3, matrix products, column_section(): lax.dot_general(precond, (partial_value / u_norm).astype(jnp.bfloat16), (...  14.8 us
    slice x12, local copies, waits for them, and re-layouts, sent_together(): lax.slice_in_dim(filled, at, at + a.shape[along], axis=along)  11.3 us
  transfers between devices with their start and end apart: 6, of which 6 were waited for; matrix products, arithmetic and copies ran while one was open for 4% of the time, Pallas kernels for 0%

commit v1 on v0

v1 whole, which is shorter than its diff:
```python
import jax
import jax.numpy as jnp
from jax import lax
from jax.sharding import Mesh, PartitionSpec as P

ITERS = 3

floor_sq = 0.01
plane = ("y", "x")
every = ("y", "x", "core", "grp")
SQ_ROWS = 8


def split_terms(value):
    first = value.astype(jnp.bfloat16)
    rest = value - first.astype(jnp.float32)
    second = rest.astype(jnp.bfloat16)
    third = (rest - second.astype(jnp.float32)).astype(jnp.bfloat16)
    blank = jnp.zeros((SQ_ROWS - 3, value.shape[1]), jnp.bfloat16)
    return jnp.concatenate([first, second, third, blank])


def swap_cores(value):
    return lax.ppermute(value, "core", [(0, 1), (1, 0)])


def exchange(tiles, axis):
    return lax.all_to_all(tiles, axis, 0, 0, tiled=True)


def copies_from_all(value, axis):
    return exchange(jnp.broadcast_to(value, (lax.axis_size(axis), *value.shape)), axis)


def summed(tiles):
    return jnp.sum(tiles.astype(jnp.float32), axis=0)


def with_squares(tiles, squares):
    extra = jnp.broadcast_to(split_terms(squares), (tiles.shape[0], SQ_ROWS, tiles.shape[2]))
    return jnp.concatenate([tiles.astype(jnp.bfloat16), extra], axis=1)


def apart(block):
    return (block[:-SQ_ROWS], jnp.sum(block[-SQ_ROWS:], axis=0, keepdims=True))


def sum_everywhere(partial_value, squares):
    core = lax.axis_index("core")
    width, cols = partial_value.shape
    peers = lax.axis_size(plane)
    halves = partial_value.reshape(2, peers, width // 2 // peers, cols)
    mine = lax.dynamic_index_in_dim(halves, core, 0, keepdims=False)
    other = lax.dynamic_index_in_dim(halves, 1 - core, 0, keepdims=False)
    came = swap_cores(with_squares(other, squares)).astype(jnp.float32)
    came_rows, came_sq = (came[:, :-SQ_ROWS], jnp.sum(came[0, -SQ_ROWS:], axis=0, keepdims=True))
    block = summed(exchange(with_squares(mine + came_rows, squares + came_sq), plane))
    rows, squares = apart(block)
    block = summed(copies_from_all(with_squares(rows[None], squares)[0], "grp"))
    rows, squares = apart(block)
    half = copies_from_all(rows.astype(jnp.bfloat16), plane).reshape(width // 2, cols)
    twin = swap_cores(half)
    low = jnp.where(core == 0, half, twin)
    high = jnp.where(core == 0, twin, half)
    return (jnp.concatenate([low, high]), squares)


def sum_squares(squares):
    tiles = copies_from_all(squares, every)
    return jnp.sum(tiles, axis=0)


def pull(precond, total, squares):
    u_norm = jnp.sqrt(squares + floor_sq)
    pulled = lax.dot_general(
        precond, total, (((0,), (0,)), ((), ())), preferred_element_type=jnp.float32
    )
    return (u_norm, pulled / u_norm)


def shards(matrix, right_side, precond, row_counts):
    local_rows, width = matrix.shape
    count = row_counts[0]
    live_rows = (lax.broadcasted_iota(jnp.int32, (local_rows, 1), 0) < count).astype(jnp.float32)

    def partials(residue):
        partial_value = lax.dot_general(
            matrix,
            residue.astype(jnp.bfloat16),
            (((0,), (0,)), ((), ())),
            preferred_element_type=jnp.float32,
        )
        return (partial_value, jnp.sum(residue * residue, axis=0, keepdims=True))

    residue = live_rows * right_side.astype(jnp.float32)
    total, squares = sum_everywhere(*partials(residue))
    u_norm, raw_vec = pull(precond, total, squares)
    v_norm = jnp.sqrt(jnp.sum(raw_vec * raw_vec, axis=0, keepdims=True) + floor_sq)
    right_vec = raw_vec / v_norm
    phi_bar = u_norm
    rho_bar = v_norm
    search = right_vec
    coeffs = jnp.zeros(right_vec.shape, jnp.float32)
    solution = jnp.zeros(right_vec.shape, jnp.float32)
    search_image = None
    start_norm = u_norm
    for turn_index in range(ITERS):
        image = jnp.dot(
            precond, right_vec.astype(jnp.bfloat16), preferred_element_type=jnp.float32
        )
        search_image = image if search_image is None else image - step_back * search_image
        residue = live_rows * (
            jnp.dot(matrix, image.astype(jnp.bfloat16), preferred_element_type=jnp.float32)
            - v_norm * (residue / u_norm)
        )
        partial_value, squares = partials(residue)
        total, total_squares = sum_everywhere(partial_value, squares)
        if turn_index + 1 == ITERS:
            total_squares = sum_squares(squares)
        u_norm, pulled = pull(precond, total, total_squares)
        raw_vec = pulled - u_norm * right_vec
        next_norm = jnp.sqrt(jnp.sum(raw_vec * raw_vec, axis=0, keepdims=True) + floor_sq)
        next_vec = raw_vec / next_norm
        radius = jnp.sqrt(rho_bar * rho_bar + u_norm * u_norm)
        cosine = rho_bar / radius
        sine_part = u_norm / radius
        coupling = sine_part * next_norm
        rho_bar = -cosine * next_norm
        phi_step = cosine * phi_bar
        phi_bar = sine_part * phi_bar
        coeffs = coeffs + phi_step / radius * search
        solution = solution + phi_step / radius * search_image
        step_back = coupling / radius
        search = next_vec - step_back * search
        right_vec = next_vec
        v_norm = next_norm
    ratio = phi_bar / start_norm

    def own_columns(value):
        cols = value.shape[1] // lax.axis_size("grp")
        return lax.dynamic_slice_in_dim(value, lax.axis_index("grp") * cols, cols, axis=1)

    return (own_columns(solution), own_columns(coeffs), own_columns(ratio)[0])


def solution(mesh):
    fine = Mesh(mesh.devices.reshape(4, 4, 2, 8), every)
    return jax.shard_map(
        shards,
        mesh=fine,
        in_specs=(P(every, None), P(every, None), P(), P(every)),
        out_specs=(P(None, "grp"), P(None, "grp"), P("grp")),
        check_vma=False,
    )
```

time: 402 us -> 203 us (0.50)
  blocking collectives: 233 us -> 93.7 us
  waiting for transfers between devices: 55.7 us -> 27.5 us
  local copies, waits for them, and re-layouts: 30.4 us -> 16.5 us
  matrix products: 42.8 us -> 29.8 us
    all_to_all x12 -> x8, blocking collectives: 233 us -> 93.7 us  [exchange(): return lax.all_to_all(tiles, axis, 0, 0, tiled=True)]
    all_to_all x6 -> x2, waiting for transfers between devices: 55.7 us -> 20.4 us  [exchange(): return lax.all_to_all(tiles, axis, 0, 0, tiled=True)]
    all_to_all x6 -> x2, starting transfers between devices: 27.3 us -> 8.91 us  [exchange(): return lax.all_to_all(tiles, axis, 0, 0, tiled=True)]
    ppermute x0 -> x6, starting transfers between devices: none -> 15.9 us  [swap_cores(): return lax.ppermute(value, 'core', [(0, 1), (1, 0)])]
    slice x18 -> x3, local copies, waits for them, and re-layouts: 14.3 us -> 0.01 us  [apart(): return (block[:-SQ_ROWS], jnp.sum(block[-SQ_ROWS:], axis=0, keepdims=True))]
    dot_general x14 -> x12, matrix products: 42.8 us -> 29.8 us  [the longest x3 15 us: pull(): lax.dot_general(precond, total, (((0,), (0,)), ((), ())), preferred_eleme...]
    ppermute x0 -> x6, waiting for transfers between devices: none -> 7.03 us  [swap_cores(): return lax.ppermute(value, 'core', [(0, 1), (1, 0)])]
    dot_general x0 -> x3, local copies, waits for them, and re-layouts: none -> 6.41 us  [partials(): lax.dot_general(matrix, residue.astype(jnp.bfloat16), (((0,), (0,)), ((),...]
  transfers between devices with their start and end apart: 6 -> 8, of which waited for: 6 -> 8; matrix products, arithmetic and copies ran while one was open for 4% -> 0% of each run, Pallas kernels for 0% -> 0%
where the time goes in v1:
time: 203 us; the launch traced here: 202 us
  blocking collectives  93.7 us (46%)
  matrix products  29.8 us (15%)
  waiting for transfers between devices  27.5 us (14%)
  starting transfers between devices  24.8 us (12%)
  local copies, waits for them, and re-layouts  16.5 us (8%)
  other arithmetic  7.79 us (4%)
    all_to_all x8, blocking collectives, exchange(): return lax.all_to_all(tiles, axis, 0, 0, tiled=True)  93.7 us
    all_to_all x2, waiting for transfers between devices, exchange(): return lax.all_to_all(tiles, axis, 0, 0, tiled=True)  20.4 us
    ppermute x6, starting transfers between devices, swap_cores(): return lax.ppermute(value, 'core', [(0, 1), (1, 0)])  15.9 us
    dot_general x3, matrix products, pull(): lax.dot_general(precond, total, (((0,), (0,)), ((), ())), preferred_eleme...  15 us
    all_to_all x2, starting transfers between devices, exchange(): return lax.all_to_all(tiles, axis, 0, 0, tiled=True)  8.91 us
    dot_general x3, matrix products, shards(): jnp.dot(precond, right_vec.astype(jnp.bfloat16), preferred_element_type=j...  8.68 us
    ppermute x6, waiting for transfers between devices, swap_cores(): return lax.ppermute(value, 'core', [(0, 1), (1, 0)])  7.03 us
    dot_general x3, local copies, waits for them, and re-layouts, partials(): lax.dot_general(matrix, residue.astype(jnp.bfloat16), (((0,), (0,)), ((),...  6.41 us
  transfers between devices with their start and end apart: 8, of which 8 were waited for; matrix products, arithmetic and copies ran while one was open for 0% of the time, Pallas kernels for 0%

profile of v1, /device:TPU:1, one launch (start us, length us, event | category | flops | bytes accessed | tf_op | source)
XLA Modules:
  0.0 202.1 jit_solution(6421945301910035279)
XLA Ops:
  1.5 1.0 copy.46
  2.5 0.1 multiply_reduce_fusion.5
  2.6 0.4 convolution_bitcast_fusion.2
  3.1 1.3 copy.47
  4.4 0.1 pad.59.clone
  4.5 1.1 fusion.32
  5.7 3.3 %collective-permute-start = (bf16[16,72,128]{2,1,0:T(8,128)(2,1)S(1)}, bf16[16,72,128]{2,1,0:T(8,128)(2,1)S(1)}, u32[]{:S(2)}, u32[]{:S(2)}) collective-permute-start(bf16[16,72,128]{2,1,0:T(8,128)(2,1)S(1)} %pad_maximum_fusion), channel_id=1, source_target_pairs={{0,8},{8,0},{1,9},{9,1},{2,10},{10,2},{3,11},{11,3},{4,12},{12,4},... | collective-permute-start | bytes 884744 | tf_op jit(solution)/shard_map/ppermute | solution.py:24
  9.0 1.2 collective-permute-done
  10.2 1.1 fusion.12
  11.4 0.1 maximum_maximum_fusion.1
  11.5 13.3 %all_to_all.50 = bf16[16,72,128]{2,1,0:T(8,128)(2,1)S(1)} all-to-all(bf16[16,72,128]{2,1,0:T(8,128)(2,1)S(1)} %pad_maximum_fusion.1), channel_id=1, replica_groups=mesh['y'=4,'x'=4,'core'=2,'grp'=8] {'y','x'}, dimensions={0} | all-to-all | bytes 589824 | tf_op jit(solution)/shard_map/all_to_all | solution.py:28
  24.9 0.1 maximum_bitcast_fusion.3
  25.0 16.1 %all_to_all.51 = bf16[8,72,128]{2,1,0:T(8,128)(2,1)S(1)} all-to-all(bf16[8,72,128]{2,1,0:T(8,128)(2,1)S(1)} %broadcast_in_dim.70), channel_id=1, replica_groups=mesh['y'=4,'x'=4,'core'=2,'grp'=8] {'grp'}, dimensions={0} | all-to-all | bytes 294912 | tf_op jit(solution)/shard_map/all_to_all | solution.py:28
  41.1 0.7 broadcast_in_dim.71
  41.9 3.5 %all-to-all-start.2 = ((bf16[16,64,128]{2,1,0:T(8,128)(2,1)}), bf16[16,64,128]{2,1,0:T(8,128)(2,1)S(1)}, u32[]{:S(2)}, u32[]{:S(2)}) async-start(bf16[16,64,128]{2,1,0:T(8,128)(2,1)} %broadcast_in_dim.71), calls=%async_computation.2 | async-start | bytes 524288 | tf_op jit(solution)/shard_map/all_to_all | solution.py:28
  45.4 7.5 %all-to-all-done.2 = bf16[16,64,128]{2,1,0:T(8,128)(2,1)S(1)} async-done(((bf16[16,64,128]{2,1,0:T(8,128)(2,1)}), bf16[16,64,128]{2,1,0:T(8,128)(2,1)S(1)}, u32[]{:S(2)}, u32[]{:S(2)}) %all-to-all-start.2) | async-done | bytes 262176 | tf_op jit(solution)/shard_map/all_to_all | solution.py:28
  52.9 4.1 %collective-permute-start.1 = (bf16[1024,128]{1,0:T(8,128)(2,1)S(1)}, bf16[1024,128]{1,0:T(8,128)(2,1)S(1)}, u32[]{:S(2)}, u32[]{:S(2)}) collective-permute-start(bf16[1024,128]{1,0:T(8,128)(2,1)S(1)} %bitcast.291), channel_id=1, source_target_pairs={{0,8},{8,0},{1,9},{9,1},{2,10},{10,2},{3,11},{11,3},{4,12},{12,4},... | collective-permute-start | bytes 786440 | tf_op jit(solution)/shard_map/ppermute | solution.py:24
  57.0 1.1 collective-permute-done.1
  58.2 4.9 %multiply_reduce_fusion.2 = (f32[128]{0:T(128)S(1)}, f32[128,2048]{1,0:T(8,128)S(1)}) fusion(f32[128]{0:T(128)S(1)} %add_sqrt_fusion.7, bf16[2048,2048]{1,0:T(8,128)(2,1)} %param.6, bf16[1024,128]{1,0:T(8,128)(2,1)S(1)} %get-tuple-element.13, bf16[1024,128]{1,0:T(8,128)(2,1)S(1)} %get-tuple-element.12), kind=kOutput, calls=%fused_computation.20 | convolution fusion | flops 1075576704 | bytes 9962496 | tf_op jit(solution)/shard_map/dot_general | solution.py:75
  63.1 0.2 broadcast_divide_fusion.2
  63.3 0.7 slice-done.1
  64.0 2.9 %fusion.30 = f32[128,2048]{1,0:T(8,128)S(1)} fusion(bf16[2048,2048]{1,0:T(8,128)(2,1)S(1)} %bitcast.280, f32[128,2048]{1,0:T(8,128)S(1)} %broadcast_divide_fusion.2), kind=kOutput, calls=%fused_computation.51 | convolution fusion | flops 1074003968 | bytes 10485760 | tf_op jit(solution)/shard_map/dot_general | solution.py:108
  67.0 1.0 copy-done.4
  67.9 0.9 multiply_reduce_fusion.4
  68.9 0.7 copy-done.6
  69.6 1.5 convolution_bitcast_fusion.1
  71.1 2.5 %copy.48 = f32[2048,128]{1,0:T(8,128)} copy(f32[2048,128]{0,1:T(8,128)} %convolution_bitcast_fusion.1) | data formatting | bytes 2097152 | tf_op jit(solution)/shard_map/dot_general | solution.py:87
  73.6 1.1 fusion.33
  74.8 0.5 collective-permute-start.2
  75.3 1.2 collective-permute-done.2
  76.5 1.1 fusion.11
  77.8 11.1 %all_to_all.52 = bf16[16,72,128]{2,1,0:T(8,128)(2,1)S(1)} all-to-all(bf16[16,72,128]{2,1,0:T(8,128)(2,1)S(1)} %pad_maximum_fusion.3), channel_id=1, replica_groups=mesh['y'=4,'x'=4,'core'=2,'grp'=8] {'y','x'}, dimensions={0} | all-to-all | bytes 589824 | tf_op jit(solution)/shard_map/all_to_all | solution.py:28
  89.0 0.1 maximum_bitcast_fusion.4
  89.1 10.6 %all_to_all.53 = bf16[8,72,128]{2,1,0:T(8,128)(2,1)S(1)} all-to-all(bf16[8,72,128]{2,1,0:T(8,128)(2,1)S(1)} %broadcast_in_dim.75), channel_id=1, replica_groups=mesh['y'=4,'x'=4,'core'=2,'grp'=8] {'grp'}, dimensions={0} | all-to-all | bytes 294912 | tf_op jit(solution)/shard_map/all_to_all | solution.py:28
  99.8 10.3 %all_to_all.54 = bf16[16,64,128]{2,1,0:T(8,128)(2,1)S(1)} all-to-all(bf16[16,64,128]{2,1,0:T(8,128)(2,1)S(1)} %broadcast_in_dim.76), channel_id=1, replica_groups=mesh['y'=4,'x'=4,'core'=2,'grp'=8] {'y','x'}, dimensions={0} | all-to-all | bytes 524288 | tf_op jit(solution)/shard_map/all_to_all | solution.py:28
  110.1 3.8 %collective-permute-start.3 = (bf16[1024,128]{1,0:T(8,128)(2,1)S(1)}, bf16[1024,128]{1,0:T(8,128)(2,1)S(1)}, u32[]{:S(2)}, u32[]{:S(2)}) collective-permute-start(bf16[1024,128]{1,0:T(8,128)(2,1)S(1)} %bitcast.293), channel_id=1, source_target_pairs={{0,8},{8,0},{1,9},{9,1},{2,10},{10,2},{3,11},{11,3},{4,12},{12,4},... | collective-permute-start | bytes 786440 | tf_op jit(solution)/shard_map/ppermute | solution.py:24
  113.9 1.1 collective-permute-done.3
  115.2 4.9 %multiply_reduce_fusion.1 = (f32[128]{0:T(128)S(1)}, f32[128,2048]{1,0:T(8,128)S(1)}) fusion(f32[128,2048]{1,0:T(8,128)S(1)} %broadcast_divide_fusion.2, f32[128]{0:T(128)S(1)} %add_sqrt_fusion.5, bf16[2048,2048]{1,0:T(8,128)(2,1)} %param.6, bf16[1024,128]{1,0:T(8,128)(2,1)S(1)} %get-tuple-element.11, bf16[1024,128]{1,0:T(8,128)(2,1)S(1)} %get-tuple-element.10), kind=kOutput, calls=%fused_computation.19 | convolution fusion | flops 1076100992 | bytes 11011072 | tf_op jit(solution)/shard_map/dot_general | solution.py:75
  120.1 0.2 broadcast_divide_fusion.1
  120.3 0.6 slice-done.3
  121.0 2.9 %fusion.25 = f32[128,2048]{1,0:T(8,128)S(1)} fusion(bf16[2048,2048]{1,0:T(8,128)(2,1)S(1)} %bitcast.282, f32[128,2048]{1,0:T(8,128)S(1)} %broadcast_divide_fusion.1), kind=kOutput, calls=%fused_computation.43 | convolution fusion | flops 1074003968 | bytes 10485760 | tf_op jit(solution)/shard_map/dot_general | solution.py:108
  123.9 0.9 multiply_reduce_fusion.3
  124.9 1.4 convolution_bitcast_fusion
  126.3 2.5 %copy.49 = f32[2048,128]{1,0:T(8,128)} copy(f32[2048,128]{0,1:T(8,128)} %convolution_bitcast_fusion) | data formatting | bytes 2097152 | tf_op jit(solution)/shard_map/dot_general | solution.py:87
  128.8 1.1 fusion.34
  130.0 0.5 collective-permute-start.4
  130.5 1.2 collective-permute-done.4
  131.7 1.1 fusion.10
  133.0 11.1 %all_to_all.55 = bf16[16,72,128]{2,1,0:T(8,128)(2,1)S(1)} all-to-all(bf16[16,72,128]{2,1,0:T(8,128)(2,1)S(1)} %pad_maximum_fusion.5), channel_id=1, replica_groups=mesh['y'=4,'x'=4,'core'=2,'grp'=8] {'y','x'}, dimensions={0} | all-to-all | bytes 589824 | tf_op jit(solution)/shard_map/all_to_all | solution.py:28
  144.3 10.6 %all_to_all.56 = bf16[8,72,128]{2,1,0:T(8,128)(2,1)S(1)} all-to-all(bf16[8,72,128]{2,1,0:T(8,128)(2,1)S(1)} %broadcast_in_dim.80), channel_id=1, replica_groups=mesh['y'=4,'x'=4,'core'=2,'grp'=8] {'grp'}, dimensions={0} | all-to-all | bytes 294912 | tf_op jit(solution)/shard_map/all_to_all | solution.py:28
  155.0 10.6 %all_to_all.57 = bf16[16,64,128]{2,1,0:T(8,128)(2,1)S(1)} all-to-all(bf16[16,64,128]{2,1,0:T(8,128)(2,1)S(1)} %broadcast_in_dim.81), channel_id=1, replica_groups=mesh['y'=4,'x'=4,'core'=2,'grp'=8] {'y','x'}, dimensions={0} | all-to-all | bytes 524288 | tf_op jit(solution)/shard_map/all_to_all | solution.py:28
  165.6 3.8 %collective-permute-start.5 = (bf16[1024,128]{1,0:T(8,128)(2,1)S(1)}, bf16[1024,128]{1,0:T(8,128)(2,1)S(1)}, u32[]{:S(2)}, u32[]{:S(2)}) collective-permute-start(bf16[1024,128]{1,0:T(8,128)(2,1)S(1)} %bitcast.292), channel_id=1, source_target_pairs={{0,8},{8,0},{1,9},{9,1},{2,10},{10,2},{3,11},{11,3},{4,12},{12,4},... | collective-permute-start | bytes 786440 | tf_op jit(solution)/shard_map/ppermute | solution.py:24
  169.4 1.1 collective-permute-done.5
  170.6 5.2 %multiply_reduce_fusion = (f32[128]{0:T(128)S(1)}, f32[128,2048]{1,0:T(8,128)S(1)}) fusion(f32[128,2048]{1,0:T(8,128)} %copy-done.1, f32[128]{0:T(128)S(1)} %add_sqrt_fusion.3, bf16[2048,2048]{1,0:T(8,128)(2,1)} %param.6, bf16[1024,128]{1,0:T(8,128)(2,1)S(1)} %get-tuple-element.9, bf16[1024,128]{1,0:T(8,128)(2,1)S(1)} %get-tuple-element.8), kind=kOutput, calls=%fused_computation.18 | convolution fusion | flops 1076100992 | bytes 11011072 | tf_op jit(solution)/shard_map/dot_general | solution.py:75
  175.8 0.2 broadcast_divide_fusion
  176.0 2.9 %fusion.23 = f32[128,2048]{1,0:T(8,128)S(1)} fusion(bf16[2048,2048]{1,0:T(8,128)(2,1)S(1)} %bitcast.284, f32[128,2048]{1,0:T(8,128)S(1)} %broadcast_divide_fusion), kind=kOutput, calls=%fused_computation.40 | convolution fusion | flops 1074003968 | bytes 10485760 | tf_op jit(solution)/shard_map/dot_general | solution.py:108
  178.9 0.9 fusion.9
  179.9 0.7 broadcast_in_dim.82
  180.6 5.4 %all-to-all-start.9 = ((f32[256,1,128]{2,1,0:T(1,128)}), f32[256,1,128]{2,1,0:T(1,128)S(1)}, u32[]{:S(2)}, u32[]{:S(2)}) async-start(f32[256,1,128]{2,1,0:T(1,128)} %broadcast_in_dim.82), calls=%async_computation.9 | async-start | bytes 262144 | tf_op jit(solution)/shard_map/all_to_all | solution.py:28
  186.0 0.1 dynamic-slice.6
  186.2 12.9 %all-to-all-done.9 = f32[256,1,128]{2,1,0:T(1,128)S(1)} async-done(((f32[256,1,128]{2,1,0:T(1,128)}), f32[256,1,128]{2,1,0:T(1,128)S(1)}, u32[]{:S(2)}, u32[]{:S(2)}) %all-to-all-start.9) | async-done | bytes 131104 | tf_op jit(solution)/shard_map/all_to_all | solution.py:28
  199.2 0.6 fusion.50
  199.9 0.1 dynamic-slice.5
  200.1 2.0 fusion.39
  (110 shorter events, 2.2 us)
Async XLA Ops:
  0.6 2.0 copy-start
  5.7 4.5 %collective-permute-start = (bf16[16,72,128]{2,1,0:T(8,128)(2,1)S(1)}, bf16[16,72,128]{2,1,0:T(8,128)(2,1)S(1)}, u32[]{:S(2)}, u32[]{:S(2)}) collective-permute-start(bf16[16,72,128]{2,1,0:T(8,128)(2,1)S(1)} %pad_maximum_fusion), channel_id=1, source_target_pairs={{0,8},{8,0},{1,9},{9,1},{2,10},{10,2},{3,11},{11,3},{4,12},{12,4},... | collective-permute-start | bytes 884744 | tf_op jit(solution)/shard_map/ppermute | solution.py:24
  41.9 11.0 %all-to-all-start.2 = ((bf16[16,64,128]{2,1,0:T(8,128)(2,1)}), bf16[16,64,128]{2,1,0:T(8,128)(2,1)S(1)}, u32[]{:S(2)}, u32[]{:S(2)}) async-start(bf16[16,64,128]{2,1,0:T(8,128)(2,1)} %broadcast_in_dim.71), calls=%async_computation.2 | async-start | bytes 524288 | tf_op jit(solution)/shard_map/all_to_all | solution.py:28
  52.9 5.2 %collective-permute-start.1 = (bf16[1024,128]{1,0:T(8,128)(2,1)S(1)}, bf16[1024,128]{1,0:T(8,128)(2,1)S(1)}, u32[]{:S(2)}, u32[]{:S(2)}) collective-permute-start(bf16[1024,128]{1,0:T(8,128)(2,1)S(1)} %bitcast.291), channel_id=1, source_target_pairs={{0,8},{8,0},{1,9},{9,1},{2,10},{10,2},{3,11},{11,3},{4,12},{12,4},... | collective-permute-start | bytes 786440 | tf_op jit(solution)/shard_map/ppermute | solution.py:24
  58.2 5.2 %slice-start = ((s8[8388608]{0:T(1024)(128)(4,1)}), s8[4194304]{0:T(1024)(128)(4,1)S(1)}, s32[]{:S(2)}) async-start(s8[8388608]{0:T(1024)(128)(4,1)} %bitcast.279), calls=%async_computation.10 | async-start | bytes 8388608
  58.2 5.8 %slice-start.1 = ((s8[8388608]{0:T(1024)(128)(4,1)}), s8[4194304]{0:T(1024)(128)(4,1)S(1)}, s32[]{:S(2)}) async-start(s8[8388608]{0:T(1024)(128)(4,1)} %bitcast.279), calls=%async_computation.11 | async-start | bytes 8388608
  67.0 1.0 copy-start.4
  68.9 0.7 copy-start.6
  74.8 1.7 collective-permute-start.2
  110.1 5.0 %collective-permute-start.3 = (bf16[1024,128]{1,0:T(8,128)(2,1)S(1)}, bf16[1024,128]{1,0:T(8,128)(2,1)S(1)}, u32[]{:S(2)}, u32[]{:S(2)}) collective-permute-start(bf16[1024,128]{1,0:T(8,128)(2,1)S(1)} %bitcast.293), channel_id=1, source_target_pairs={{0,8},{8,0},{1,9},{9,1},{2,10},{10,2},{3,11},{11,3},{4,12},{12,4},... | collective-permute-start | bytes 786440 | tf_op jit(solution)/shard_map/ppermute | solution.py:24
  115.1 5.2 %slice-start.2 = ((s8[8388608]{0:T(1024)(128)(4,1)}), s8[4194304]{0:T(1024)(128)(4,1)S(1)}, s32[]{:S(2)}) async-start(s8[8388608]{0:T(1024)(128)(4,1)} %bitcast.281), calls=%async_computation.12 | async-start | bytes 8388608
  115.1 5.8 %slice-start.3 = ((s8[8388608]{0:T(1024)(128)(4,1)}), s8[4194304]{0:T(1024)(128)(4,1)S(1)}, s32[]{:S(2)}) async-start(s8[8388608]{0:T(1024)(128)(4,1)} %bitcast.281), calls=%async_computation.13 | async-start | bytes 8388608
  120.1 3.8 %copy-start.7 = (f32[512,128]{0,1:T(8,128)S(1)}, f32[512,128]{0,1:T(8,128)}, u32[]{:S(2)}) copy-start(f32[512,128]{0,1:T(8,128)} %copy-done.6) | copy-start | bytes 786436
  121.0 2.9 %copy-start.1 = (f32[128,2048]{1,0:T(8,128)}, f32[128,2048]{1,0:T(8,128)S(1)}, u32[]{:S(2)}) copy-start(f32[128,2048]{1,0:T(8,128)S(1)} %broadcast_divide_fusion.1) | copy-start | bytes 3145732
  123.9 1.0 copy-start.5
  130.0 1.7 collective-permute-start.4
  155.0 21.0 %slice-start.4 = ((s8[8388608]{0:T(1024)(128)(4,1)}), s8[4194304]{0:T(1024)(128)(4,1)S(1)}, s32[]{:S(2)}) async-start(s8[8388608]{0:T(1024)(128)(4,1)} %bitcast.283), calls=%async_computation.14 | async-start | bytes 8388608
  165.6 5.0 %collective-permute-start.5 = (bf16[1024,128]{1,0:T(8,128)(2,1)S(1)}, bf16[1024,128]{1,0:T(8,128)(2,1)S(1)}, u32[]{:S(2)}, u32[]{:S(2)}) collective-permute-start(bf16[1024,128]{1,0:T(8,128)(2,1)S(1)} %bitcast.292), channel_id=1, source_target_pairs={{0,8},{8,0},{1,9},{9,1},{2,10},{10,2},{3,11},{11,3},{4,12},{12,4},... | collective-permute-start | bytes 786440 | tf_op jit(solution)/shard_map/ppermute | solution.py:24
  170.6 5.4 %slice-start.5 = ((s8[8388608]{0:T(1024)(128)(4,1)}), s8[4194304]{0:T(1024)(128)(4,1)S(1)}, s32[]{:S(2)}) async-start(s8[8388608]{0:T(1024)(128)(4,1)} %bitcast.283), calls=%async_computation.15 | async-start | bytes 8388608
  176.0 2.9 %copy-start.2 = (f32[128,2048]{1,0:T(8,128)}, f32[128,2048]{1,0:T(8,128)S(1)}, u32[]{:S(2)}) copy-start(f32[128,2048]{1,0:T(8,128)S(1)} %broadcast_divide_fusion) | copy-start | bytes 3145732
  178.9 1.0 copy-start.3
  180.6 18.5 %all-to-all-start.9 = ((f32[256,1,128]{2,1,0:T(1,128)}), f32[256,1,128]{2,1,0:T(1,128)S(1)}, u32[]{:S(2)}, u32[]{:S(2)}) async-start(f32[256,1,128]{2,1,0:T(1,128)} %broadcast_in_dim.82), calls=%async_computation.9 | async-start | bytes 262144 | tf_op jit(solution)/shard_map/all_to_all | solution.py:28

commit v2 on v1

v2 whole, which is shorter than its diff:
```python
import functools

import jax
import jax.numpy as jnp
from jax import lax
from jax.experimental import pallas as pl
from jax.experimental.pallas import tpu as pltpu
from jax.sharding import Mesh, PartitionSpec as P

ITERS = 3

floor_sq = 0.01
plane = ("y", "x")
every = ("y", "x", "core", "grp")
SQ_ROWS = 8
LANES = 128
bf16, f32 = jnp.bfloat16, jnp.float32
VMEM = pl.BlockSpec(memory_space=pltpu.VMEM)
SMEM = pl.BlockSpec(memory_space=pltpu.SMEM)


def run(body, shapes, operands, specs, name, scratch=(), limit=None):
    return pl.pallas_call(
        body,
        out_shape=[jax.ShapeDtypeStruct(s, t) for s, t in shapes],
        in_specs=specs,
        out_specs=[VMEM] * len(shapes),
        scratch_shapes=list(scratch),
        compiler_params=pltpu.CompilerParams(vmem_limit_bytes=limit),
        name=name,
    )(*operands)


def terms_of(row):
    first = row.astype(bf16).astype(f32)
    second = (row - first).astype(bf16).astype(f32)
    third = (row - first - second).astype(bf16).astype(f32)
    at = lax.broadcasted_iota(jnp.int32, (SQ_ROWS, row.shape[1]), 0)
    return jnp.where(at == 0, first, jnp.where(at == 1, second, jnp.where(at == 2, third, 0.0)))


def to_lanes(column):
    square = jnp.broadcast_to(column, (column.shape[0], LANES))
    spare = jnp.zeros((LANES - column.shape[0], LANES), f32)
    return jnp.concatenate([square, spare]).T[0:1]


def to_column(row, count):
    return jnp.broadcast_to(row, (LANES, LANES)).T[:count, 0:1]


def nn(left, right):
    return jnp.dot(left, right, preferred_element_type=f32)


def nt(left, right):
    return lax.dot_general(left, right, (((1,), (1,)), ((), ())), preferred_element_type=f32)


def write_tiles(residue, own_ref, twin_ref, tiles_ref, squares_ref):
    rows = own_ref.shape[0]
    rounded = residue.astype(bf16)
    partial_value = nn(rounded[:, :rows], own_ref[...]) + nn(rounded[:, rows:], twin_ref[...])
    kept = residue.shape[0]
    squares = to_lanes(jnp.sum(residue * residue, axis=1, keepdims=True))
    squares_ref[...] = jnp.broadcast_to(squares.reshape(1, 1, LANES), squares_ref.shape)
    extra = terms_of(squares).astype(bf16)
    for j in range(tiles_ref.shape[0]):
        tiles_ref[j, :kept, :] = partial_value[:, j * LANES : (j + 1) * LANES].astype(bf16)
        tiles_ref[j, kept:, :] = extra


def masked(residue, own_count, twin_count):
    rows = residue.shape[1] // 2
    slot = lax.broadcasted_iota(jnp.int32, residue.shape, 1)
    live = (slot < own_count) | ((slot >= rows) & (slot < rows + twin_count))
    return jnp.where(live, residue, 0.0)


def start_body(own_count, twin_count, b_own, b_twin, a_own, a_twin, tiles_ref, squares_ref, residue_ref, turned):
    cols = residue_ref.shape[0]
    rows = b_own.shape[0]
    turned[:, :rows] = b_own[...].astype(f32).T
    turned[:, rows:] = b_twin[...].astype(f32).T
    mine = turned[pl.ds(pl.multiple_of(lax.axis_index("core") * cols, cols), cols), :]
    residue = masked(mine, own_count[0], twin_count[0])
    residue_ref[...] = residue
    write_tiles(residue, a_own, a_twin, tiles_ref, squares_ref)


def turn_body(first, own_count, twin_count, half_ref, sq_ref, n_ref, a_own, a_twin, old_ref, *refs):
    right_ref = None if first else refs[0]
    tiles_ref, squares_ref, residue_ref, next_ref, image_ref, norms_ref = refs[-6:]
    cols = half_ref.shape[1]
    u_norm = to_column(jnp.sqrt(sq_ref[0:1] + floor_sq), cols)
    total = jnp.concatenate([half_ref[j] for j in range(half_ref.shape[0])], axis=1)
    raw_vec = nn(total, n_ref[...]) / u_norm
    if not first:
        raw_vec = raw_vec - u_norm * right_ref[...]
    v_norm = jnp.sqrt(jnp.sum(raw_vec * raw_vec, axis=1, keepdims=True) + floor_sq)
    next_vec = raw_vec / v_norm
    next_ref[...] = next_vec
    image = nt(next_vec.astype(bf16), n_ref[...])
    image_ref[...] = image
    pushed = image.astype(bf16)
    ahead = jnp.concatenate([nt(pushed, a_own[...]), nt(pushed, a_twin[...])], axis=1)
    residue = masked(ahead - v_norm * (old_ref[...] / u_norm), own_count[0], twin_count[0])
    residue_ref[...] = residue
    norms_ref[:, :LANES] = jnp.broadcast_to(u_norm, (cols, LANES))
    norms_ref[:, LANES:] = jnp.broadcast_to(v_norm, (cols, LANES))
    write_tiles(residue, a_own, a_twin, tiles_ref, squares_ref)


def block_sum(tiles_ref, kept):
    total = jnp.sum(tiles_ref[...].astype(f32), axis=0)
    return (total[:kept], jnp.sum(total[kept:], axis=0, keepdims=True))


def plane_sum_body(tiles_ref, out_ref):
    kept = tiles_ref.shape[1] - SQ_ROWS
    rows, squares = block_sum(tiles_ref, kept)
    extra = terms_of(squares).astype(bf16)
    for j in range(out_ref.shape[0]):
        out_ref[j, :kept, :] = rows.astype(bf16)
        out_ref[j, kept:, :] = extra


def line_sum_body(tiles_ref, out_ref, sq_ref):
    rows, squares = block_sum(tiles_ref, out_ref.shape[1])
    for j in range(out_ref.shape[0]):
        out_ref[j] = rows.astype(bf16)
    sq_ref[...] = jnp.broadcast_to(squares, sq_ref.shape)


def own_place(cols, share):
    group = lax.axis_index("grp")
    per_half = cols // share
    return (group // per_half, pl.multiple_of(group % per_half * share, share))


def pack_body(*refs):
    *sources, out_ref, work = refs
    rights, images, norms = (sources[:ITERS], sources[ITERS : 2 * ITERS], sources[2 * ITERS :])
    width = rights[0].shape[1]
    start_norm = norms[0][:, 0:1]
    phi_bar, rho_bar = (start_norm, norms[0][:, LANES : LANES + 1])
    search, search_image = (rights[0][...], images[0][...])
    coeffs, solution = (jnp.zeros_like(search), jnp.zeros_like(search))
    for k in range(1, ITERS):
        u_norm, next_norm = (norms[k][:, 0:1], norms[k][:, LANES : LANES + 1])
        radius = jnp.sqrt(rho_bar * rho_bar + u_norm * u_norm)
        cosine = rho_bar / radius
        sine_part = u_norm / radius
        coupling = sine_part * next_norm
        rho_bar = -cosine * next_norm
        step = cosine * phi_bar / radius
        phi_bar = sine_part * phi_bar
        coeffs = coeffs + step * search
        solution = solution + step * search_image
        search = rights[k][...] - coupling / radius * search
        search_image = images[k][...] - coupling / radius * search_image
    for j, value in enumerate((coeffs, solution, search, search_image)):
        work[:, j * width : (j + 1) * width] = value
    for j, value in enumerate((phi_bar, rho_bar, start_norm)):
        work[:, 4 * width + j * LANES : 4 * width + (j + 1) * LANES] = jnp.broadcast_to(value, (value.shape[0], LANES))
    share = out_ref.shape[0]
    _, at = own_place(work.shape[0], share)
    out_ref[...] = work[pl.ds(at, share), :]


def final_body(everyone_ref, mine_ref, twin_ref, out_ref, coeffs_ref, ratio_ref, column):
    share = mine_ref.shape[0]
    width = out_ref.shape[1]
    tiles = everyone_ref[...].reshape(everyone_ref.shape[0], LANES)
    sender = lax.broadcasted_iota(jnp.int32, tiles.shape, 0)
    cols = column.shape[0]
    owner, at = own_place(cols, share)
    wanted = sender // lax.axis_size("grp") % 2 == owner
    squares = jnp.sum(jnp.where(wanted, tiles, 0.0), axis=0, keepdims=True)
    column[...] = jnp.broadcast_to(to_column(jnp.sqrt(squares + floor_sq), cols), column.shape)
    u_norm = column[pl.ds(at, share), :][:, 0:1]
    own = owner == lax.axis_index("core")

    def piece(start, length):
        return jnp.where(own, mine_ref[:, start : start + length], twin_ref[:, start : start + length])

    phi_bar, rho_bar, start_norm = (piece(4 * width + j * LANES, LANES)[:, 0:1] for j in range(3))
    radius = jnp.sqrt(rho_bar * rho_bar + u_norm * u_norm)
    step = rho_bar / radius * phi_bar / radius
    phi_bar = u_norm / radius * phi_bar
    coeffs_ref[...] = piece(0, width) + step * piece(2 * width, width)
    out_ref[...] = piece(width, width) + step * piece(3 * width, width)
    ratio_ref[...] = to_lanes(phi_bar / start_norm)


def exchange(tiles, axis):
    return lax.all_to_all(tiles, axis, 0, 0, tiled=True)


def swap_cores(value):
    return lax.ppermute(value, "core", [(0, 1), (1, 0)])


SMALL = 4 * 1024 * 1024


def sum_everywhere(tiles):
    peers, tall, _ = tiles.shape
    kept = tall - SQ_ROWS
    lines = lax.axis_size("grp")
    (block,) = run(plane_sum_body, [((lines, tall, LANES), bf16)], [exchange(tiles, plane)], [VMEM], "plane_sum", limit=SMALL)
    half, squares = run(
        line_sum_body,
        [((peers, kept, LANES), bf16), ((SQ_ROWS, LANES), f32)],
        [exchange(block, "grp")],
        [VMEM],
        "line_sum",
        limit=SMALL,
    )
    return (exchange(half, plane), squares)


def shards(matrix, right_side, precond, row_counts):
    local_rows, width = matrix.shape
    cols = right_side.shape[1] // 2
    twin_matrix = swap_cores(matrix)
    twin_side = swap_cores(right_side)
    twin_counts = swap_cores(row_counts)
    counts = [row_counts, twin_counts]
    blocks = [matrix, twin_matrix]
    tiles_shape = (width // LANES, cols + SQ_ROWS, LANES)
    tiles, _, residue = run(
        start_body,
        [(tiles_shape, bf16), ((1, 1, LANES), f32), ((cols, 2 * local_rows), f32)],
        [*counts, right_side, twin_side, *blocks],
        [SMEM] * 2 + [VMEM] * 4,
        "start",
        scratch=[pltpu.VMEM((2 * cols, 2 * local_rows), f32)],
        limit=12 * 1024 * 1024,
    )

    def turn(first, half, squares, right_vec, residue, copies=1):
        return run(
            functools.partial(turn_body, first),
            [
                (tiles_shape, bf16),
                ((copies, 1, LANES), f32),
                (residue.shape, f32),
                ((cols, width), f32),
                ((cols, width), f32),
                ((cols, 2 * LANES), f32),
            ],
            [*counts, half, squares, precond, *blocks, residue] + ([] if first else [right_vec]),
            [SMEM] * 2 + [VMEM] * (6 if first else 7),
            "turn",
            limit=20 * 1024 * 1024,
        )

    right_vec = None
    rights, images, norms = ([], [], [])
    for turn_index in range(ITERS):
        half, squares = sum_everywhere(tiles)
        tiles, local_squares, residue, right_vec, image, norm_pair = turn(
            turn_index == 0,
            half,
            squares,
            right_vec,
            residue,
            lax.axis_size(every) if turn_index + 1 == ITERS else 1,
        )
        rights.append(right_vec)
        images.append(image)
        norms.append(norm_pair)
    half, squares = sum_everywhere(tiles)
    turn(False, half, squares, right_vec, residue)
    everyone = exchange(local_squares, every)

    share = 2 * cols // lax.axis_size("grp")
    packed = run(
        pack_body,
        [((share, 4 * width + 3 * LANES), f32)],
        [*rights, *images, *norms],
        [VMEM] * (3 * ITERS),
        "pack",
        scratch=[pltpu.VMEM((cols, 4 * width + 3 * LANES), f32)],
        limit=12 * 1024 * 1024,
    )[0]
    twin_packed = swap_cores(packed)
    out, coeffs, ratio = run(
        final_body,
        [((share, width), f32), ((share, width), f32), ((1, LANES), f32)],
        [everyone, packed, twin_packed],
        [VMEM] * 3,
        "final",
        scratch=[pltpu.VMEM((cols, LANES), f32)],
        limit=12 * 1024 * 1024,
    )
    return (out.T, coeffs.T, ratio[0, :share])


def solution(mesh):
    fine = Mesh(mesh.devices.reshape(4, 4, 2, 8), every)
    return jax.shard_map(
        shards,
        mesh=fine,
        in_specs=(P(every, None), P(every, None), P(), P(every)),
        out_specs=(P(None, "grp"), P(None, "grp"), P("grp")),
        check_vma=False,
    )
```

time: 203 us -> 173 us (0.85)
  matrix products: 29.8 us -> 0 us
  blocking collectives: 93.7 us -> 120 us
  Pallas kernels: 0 us -> 26 us
  waiting for transfers between devices: 27.5 us -> 3.03 us
  local copies, waits for them, and re-layouts: 16.5 us -> 6.4 us
  starting transfers between devices: 24.8 us -> 15.9 us
  other arithmetic: 7.79 us -> 0 us
    dot_general x12 -> x0, matrix products: 29.8 us -> none  [the longest x3 15 us: pull(): lax.dot_general(precond, total, (((0,), (0,)), ((), ())), preferred_eleme...]
    all_to_all x8 -> x10, blocking collectives: 93.7 us -> 120 us  [exchange(): return lax.all_to_all(tiles, axis, 0, 0, tiled=True)]
    pallas_call x0 -> x12, Pallas kernels: none -> 26 us  [run(): pl.pallas_call(body, out_shape=[jax.ShapeDtypeStruct(s, t) for s, t in sh...]
    all_to_all x2 -> x0, waiting for transfers between devices: 20.4 us -> none  [exchange(): return lax.all_to_all(tiles, axis, 0, 0, tiled=True)]
    all_to_all x2 -> x0, starting transfers between devices: 8.91 us -> none  [exchange(): return lax.all_to_all(tiles, axis, 0, 0, tiled=True)]
    dot_general x3 -> x0, local copies, waits for them, and re-layouts: 6.41 us -> none  [partials(): lax.dot_general(matrix, residue.astype(jnp.bfloat16), (((0,), (0,)), ((),...]
    ppermute x6 -> x4, waiting for transfers between devices: 7.03 us -> 3.03 us  [swap_cores(): return lax.ppermute(value, 'core', [(0, 1), (1, 0)])]
    convert_element_type x22 -> x0, other arithmetic: 3.58 us -> none  [the longest x3 3.36 us: with_squares(): return jnp.concatenate([tiles.astype(jnp.bfloat16), extra], axis=1)]
  transfers between devices with their start and end apart: 8 -> 4, of which waited for: 8 -> 1; matrix products, arithmetic and copies ran while one was open for 0% -> 0% of each run, Pallas kernels for 0% -> 0%
where the time goes in v2:
time: 173 us
  blocking collectives  120 us (69%)
  Pallas kernels  26 us (15%)
  starting transfers between devices  15.9 us (9%)
  local copies, waits for them, and re-layouts  6.4 us (4%)
  waiting for transfers between devices  3.03 us (2%)
    all_to_all x10, blocking collectives, exchange(): return lax.all_to_all(tiles, axis, 0, 0, tiled=True)  120 us
    pallas_call x12, Pallas kernels, run(): pl.pallas_call(body, out_shape=[jax.ShapeDtypeStruct(s, t) for s, t in sh...  26 us
    ppermute x4, starting transfers between devices, swap_cores(): return lax.ppermute(value, 'core', [(0, 1), (1, 0)])  15.9 us
    unnamed x10, local copies, waits for them, and re-layouts  5.89 us
  transfers between devices with their start and end apart: 4, of which 1 were waited for; matrix products, arithmetic and copies ran while one was open for 0% of the time, Pallas kernels for 0%

profile of v2, /device:TPU:1, one launch (start us, length us, event | category | flops | bytes accessed | tf_op | source)
XLA Modules:
  0.0 172.5 jit_solution(14459194425184632352)
XLA Ops:
  0.6 3.3 %collective-permute-start.2 = (bf16[512,2048]{1,0:T(8,128)(2,1)}, bf16[512,2048]{1,0:T(8,128)(2,1)S(1)}, u32[]{:S(2)}, u32[]{:S(2)}) collective-permute-start(bf16[512,2048]{1,0:T(8,128)(2,1)} %a_own.7), channel_id=1, source_target_pairs={{0,8},{8,0},{1,9},{9,1},{2,10},{10,2},{3,11},{11,3},{4,12},{12,4},... | collective-permute-start | bytes 6291464 | tf_op jit(solution)/shard_map/ppermute | solution.py:201
  3.9 0.1 collective-permute-start.1
  4.0 0.4 collective-permute-start
  5.1 3.0 %collective-permute-done.twin_count = s32[1]{0:T(128)} collective-permute-done((s32[1]{0:T(128)}, s32[1]{0:T(128)}, u32[]{:S(2)}, u32[]{:S(2)}) %collective-permute-start) | collective-permute-done | bytes 36 | tf_op jit(solution)/shard_map/ppermute | solution.py:201
  8.1 0.0 collective-permute-done.1.b_twin
  8.1 0.0 collective-permute-done.2.a_twin
  8.1 0.0 copy-start.2
  8.1 1.6 copy-done.2
  9.7 0.0 copy-start.4
  9.7 0.9 copy-done.4
  10.6 0.0 copy-start.3
  10.6 1.9 %start.1 = (bf16[16,72,128]{2,1,0:T(8,128)(2,1)S(1)}, f32[1,1,128]{2,1,0:T(1,128)}, f32[64,1024]{1,0:T(8,128)S(1)}) custom-call(s32[1]{0:T(128)S(6)} %copy.7.own_count, s32[1]{0:T(128)} %collective-permute-done.twin_count, bf16[512,128]{1,0:T(8,128)(2,1)S(1)} %copy-done.4, bf16[512,128]{1,0:T(8,128)(2,1)S(1)} %collective-permute-done.1.b_twin, ...), custom_call_target="tpu_custom_call" | custom-call | tf_op jit(solution)/shard_map/start/pallas_call | solution.py:23
  12.5 13.3 %all_to_all.53.tiles_ref = bf16[16,72,128]{2,1,0:T(8,128)(2,1)S(1)} all-to-all(bf16[16,72,128]{2,1,0:T(8,128)(2,1)S(1)} %get-tuple-element.28), channel_id=1, replica_groups=mesh['y'=4,'x'=4,'core'=2,'grp'=8] {'y','x'}, dimensions={0} | all-to-all | bytes 589824 | tf_op jit(solution)/shard_map/all_to_all | solution.py:197
  25.9 16.1 %all_to_all.54.tiles_ref = bf16[8,72,128]{2,1,0:T(8,128)(2,1)S(1)} all-to-all(bf16[8,72,128]{2,1,0:T(8,128)(2,1)S(1)} %plane_sum.3), channel_id=1, replica_groups=mesh['y'=4,'x'=4,'core'=2,'grp'=8] {'grp'}, dimensions={0} | all-to-all | bytes 294912 | tf_op jit(solution)/shard_map/all_to_all | solution.py:197
  42.0 10.4 %all_to_all.55.half_ref = bf16[16,64,128]{2,1,0:T(8,128)(2,1)S(1)} all-to-all(bf16[16,64,128]{2,1,0:T(8,128)(2,1)S(1)} %get-tuple-element.29), channel_id=1, replica_groups=mesh['y'=4,'x'=4,'core'=2,'grp'=8] {'y','x'}, dimensions={0} | all-to-all | bytes 524288 | tf_op jit(solution)/shard_map/all_to_all | solution.py:197
  52.4 0.0 copy-done.3
  52.4 0.0 copy-start
  52.4 3.4 %copy-done = bf16[2048,2048]{1,0:T(8,128)(2,1)S(1)} copy-done((bf16[2048,2048]{1,0:T(8,128)(2,1)S(1)}, bf16[2048,2048]{1,0:T(8,128)(2,1)}, u32[]{:S(2)}) %copy-start) | copy-done | bytes 8388632
  55.8 0.0 copy-start.1
  55.8 7.3 %turn.3 = (bf16[16,72,128]{2,1,0:T(8,128)(2,1)S(1)}, f32[1,1,128]{2,1,0:T(1,128)}, f32[64,1024]{1,0:T(8,128)S(1)}, f32[64,2048]{1,0:T(8,128)S(1)}, f32[64,2048]{1,0:T(8,128)S(1)}, /*index=5*/f32[64,256]{1,0:T(8,128)S(1)}) custom-call(s32[1]{0:T(128)S(6)} %copy.7.own_count, s32[1]{0:T(128)} %collective-permute-done.twin_count, ...), custom_call_target="tpu_custom_call" | custom-call | tf_op jit(solution)/shard_map/turn/pallas_call | solution.py:23
  63.1 10.3 %all_to_all.56.tiles_ref = bf16[16,72,128]{2,1,0:T(8,128)(2,1)S(1)} all-to-all(bf16[16,72,128]{2,1,0:T(8,128)(2,1)S(1)} %get-tuple-element.32), channel_id=1, replica_groups=mesh['y'=4,'x'=4,'core'=2,'grp'=8] {'y','x'}, dimensions={0} | all-to-all | bytes 589824 | tf_op jit(solution)/shard_map/all_to_all | solution.py:197
  73.4 10.5 %all_to_all.57.tiles_ref = bf16[8,72,128]{2,1,0:T(8,128)(2,1)S(1)} all-to-all(bf16[8,72,128]{2,1,0:T(8,128)(2,1)S(1)} %plane_sum.4), channel_id=1, replica_groups=mesh['y'=4,'x'=4,'core'=2,'grp'=8] {'grp'}, dimensions={0} | all-to-all | bytes 294912 | tf_op jit(solution)/shard_map/all_to_all | solution.py:197
  84.0 10.1 %all_to_all.58.half_ref = bf16[16,64,128]{2,1,0:T(8,128)(2,1)S(1)} all-to-all(bf16[16,64,128]{2,1,0:T(8,128)(2,1)S(1)} %get-tuple-element.33), channel_id=1, replica_groups=mesh['y'=4,'x'=4,'core'=2,'grp'=8] {'y','x'}, dimensions={0} | all-to-all | bytes 524288 | tf_op jit(solution)/shard_map/all_to_all | solution.py:197
  94.1 0.0 copy-done.1
  94.1 7.1 %turn.4 = (bf16[16,72,128]{2,1,0:T(8,128)(2,1)S(1)}, f32[1,1,128]{2,1,0:T(1,128)}, f32[64,1024]{1,0:T(8,128)S(1)}, f32[64,2048]{1,0:T(8,128)S(1)}, f32[64,2048]{1,0:T(8,128)S(1)}, /*index=5*/f32[64,256]{1,0:T(8,128)S(1)}) custom-call(s32[1]{0:T(128)S(6)} %copy.7.own_count, s32[1]{0:T(128)} %collective-permute-done.twin_count, ...), custom_call_target="tpu_custom_call" | custom-call | tf_op jit(solution)/shard_map/turn/pallas_call | solution.py:23
  101.2 10.5 %all_to_all.59.tiles_ref = bf16[16,72,128]{2,1,0:T(8,128)(2,1)S(1)} all-to-all(bf16[16,72,128]{2,1,0:T(8,128)(2,1)S(1)} %get-tuple-element.37), channel_id=1, replica_groups=mesh['y'=4,'x'=4,'core'=2,'grp'=8] {'y','x'}, dimensions={0} | all-to-all | bytes 589824 | tf_op jit(solution)/shard_map/all_to_all | solution.py:197
  111.8 10.5 %all_to_all.60.tiles_ref = bf16[8,72,128]{2,1,0:T(8,128)(2,1)S(1)} all-to-all(bf16[8,72,128]{2,1,0:T(8,128)(2,1)S(1)} %plane_sum.5), channel_id=1, replica_groups=mesh['y'=4,'x'=4,'core'=2,'grp'=8] {'grp'}, dimensions={0} | all-to-all | bytes 294912 | tf_op jit(solution)/shard_map/all_to_all | solution.py:197
  122.3 10.2 %all_to_all.61.half_ref = bf16[16,64,128]{2,1,0:T(8,128)(2,1)S(1)} all-to-all(bf16[16,64,128]{2,1,0:T(8,128)(2,1)S(1)} %get-tuple-element.38), channel_id=1, replica_groups=mesh['y'=4,'x'=4,'core'=2,'grp'=8] {'y','x'}, dimensions={0} | all-to-all | bytes 524288 | tf_op jit(solution)/shard_map/all_to_all | solution.py:197
  132.5 7.7 %turn.5 = (bf16[16,72,128]{2,1,0:T(8,128)(2,1)}, f32[256,1,128]{2,1,0:T(1,128)S(1)}, f32[64,1024]{1,0:T(8,128)}, f32[64,2048]{1,0:T(8,128)S(1)}, f32[64,2048]{1,0:T(8,128)S(1)}, /*index=5*/f32[64,256]{1,0:T(8,128)S(1)}) custom-call(s32[1]{0:T(128)S(6)} %copy.7.own_count, s32[1]{0:T(128)} %collective-permute-done.twin_count, ...), custom_call_target="tpu_custom_call" | custom-call | tf_op jit(solution)/shard_map/turn/pallas_call | solution.py:23
  140.3 0.6 pack.1.mine_ref
  140.9 12.1 %collective-permute-start.3 = (f32[16,8576]{1,0:T(8,128)S(1)}, f32[16,8576]{1,0:T(8,128)S(1)}, u32[]{:S(2)}, u32[]{:S(2)}) collective-permute-start(f32[16,8576]{1,0:T(8,128)S(1)} %pack.1.mine_ref), channel_id=1, source_target_pairs={{0,8},{8,0},{1,9},{9,1},{2,10},{10,2},{3,11},{11,3},{4,12},{12,4},... | collective-permute-start | bytes 1646600 | tf_op jit(solution)/shard_map/ppermute | solution.py:201
  153.0 17.9 %all_to_all.62.everyone_ref = f32[256,1,128]{2,1,0:T(1,128)S(1)} all-to-all(f32[256,1,128]{2,1,0:T(1,128)S(1)} %get-tuple-element.42), channel_id=1, replica_groups=mesh['y'=4,'x'=4,'core'=2,'grp'=8] {'y','x','core','grp'}, dimensions={0} | all-to-all | bytes 262144 | tf_op jit(solution)/shard_map/all_to_all | solution.py:197
  170.9 0.0 collective-permute-done.3.twin_ref
  170.9 1.1 final.1
  172.0 0.5 slice_bitcast_fusion
  (6 shorter events, 0.2 us)
Async XLA Ops:
  0.6 7.5 %collective-permute-start.2 = (bf16[512,2048]{1,0:T(8,128)(2,1)}, bf16[512,2048]{1,0:T(8,128)(2,1)S(1)}, u32[]{:S(2)}, u32[]{:S(2)}) collective-permute-start(bf16[512,2048]{1,0:T(8,128)(2,1)} %a_own.7), channel_id=1, source_target_pairs={{0,8},{8,0},{1,9},{9,1},{2,10},{10,2},{3,11},{11,3},{4,12},{12,4},... | collective-permute-start | bytes 6291464 | tf_op jit(solution)/shard_map/ppermute | solution.py:201
  3.9 4.2 %collective-permute-start.1 = (bf16[512,128]{1,0:T(8,128)(2,1)}, bf16[512,128]{1,0:T(8,128)(2,1)S(1)}, u32[]{:S(2)}, u32[]{:S(2)}) collective-permute-start(bf16[512,128]{1,0:T(8,128)(2,1)} %b_own.1), channel_id=1, source_target_pairs={{0,8},{8,0},{1,9},{9,1},{2,10},{10,2},{3,11},{11,3},{4,12},{12,4},... | collective-permute-start | bytes 393224 | tf_op jit(solution)/shard_map/ppermute | solution.py:201
  4.0 4.1 %collective-permute-start = (s32[1]{0:T(128)}, s32[1]{0:T(128)}, u32[]{:S(2)}, u32[]{:S(2)}) collective-permute-start(s32[1]{0:T(128)} %param.7), channel_id=1, source_target_pairs={{0,8},{8,0},{1,9},{9,1},{2,10},{10,2},{3,11},{11,3},{4,12},{12,4},... | collective-permute-start | bytes 20 | tf_op jit(solution)/shard_map/ppermute | solution.py:201
  8.1 1.6 copy-start.2
  9.7 0.9 copy-start.4
  10.6 41.8 %copy-start.3 = (bf16[512,2048]{1,0:T(8,128)(2,1)S(1)}, bf16[512,2048]{1,0:T(8,128)(2,1)}, u32[]{:S(2)}) copy-start(bf16[512,2048]{1,0:T(8,128)(2,1)} %a_own.7) | copy-start | bytes 6291460
  52.4 3.4 %copy-start = (bf16[2048,2048]{1,0:T(8,128)(2,1)S(1)}, bf16[2048,2048]{1,0:T(8,128)(2,1)}, u32[]{:S(2)}) copy-start(bf16[2048,2048]{1,0:T(8,128)(2,1)} %n_ref.5) | copy-start | bytes 25165828
  55.8 38.3 %copy-start.1 = (bf16[2048,2048]{1,0:T(8,128)(2,1)S(1)}, bf16[2048,2048]{1,0:T(8,128)(2,1)}, u32[]{:S(2)}) copy-start(bf16[2048,2048]{1,0:T(8,128)(2,1)} %n_ref.5) | copy-start | bytes 25165828
  140.9 30.0 %collective-permute-start.3 = (f32[16,8576]{1,0:T(8,128)S(1)}, f32[16,8576]{1,0:T(8,128)S(1)}, u32[]{:S(2)}, u32[]{:S(2)}) collective-permute-start(f32[16,8576]{1,0:T(8,128)S(1)} %pack.1.mine_ref), channel_id=1, source_target_pairs={{0,8},{8,0},{1,9},{9,1},{2,10},{10,2},{3,11},{11,3},{4,12},{12,4},... | collective-permute-start | bytes 1646600 | tf_op jit(solution)/shard_map/ppermute | solution.py:201

commit v3 on v2

--- a/solution.py
+++ b/solution.py
@@ -14,6 +14,7 @@
 every = ("y", "x", "core", "grp")
 SQ_ROWS = 8
 LANES = 128
+LOAD_ROWS = 256
 bf16, f32 = jnp.bfloat16, jnp.float32
 VMEM = pl.BlockSpec(memory_space=pltpu.VMEM)
 SMEM = pl.BlockSpec(memory_space=pltpu.SMEM)
@@ -77,6 +78,19 @@
     return jnp.where(live, residue, 0.0)
 
 
+def load_body(n_in, a_in, n_ref, turned_n, a_ref, turned_a, arrived):
+    jobs = []
+    for source, target, turned in ((a_in, a_ref, turned_a), (n_in, n_ref, turned_n)):
+        for at in range(0, source.shape[0], LOAD_ROWS):
+            block = pl.ds(at, LOAD_ROWS)
+            copy = pltpu.make_async_copy(source.at[block], target.at[block], arrived.at[len(jobs)])
+            copy.start()
+            jobs.append((copy, target, turned, at))
+    for copy, target, turned, at in jobs:
+        copy.wait()
+        turned[:, at : at + LOAD_ROWS] = target[at : at + LOAD_ROWS, :].T
+
+
 def start_body(own_count, twin_count, b_own, b_twin, a_own, a_twin, tiles_ref, squares_ref, residue_ref, turned):
     cols = residue_ref.shape[0]
     rows = b_own.shape[0]
@@ -88,7 +102,7 @@
     write_tiles(residue, a_own, a_twin, tiles_ref, squares_ref)
 
 
-def turn_body(first, own_count, twin_count, half_ref, sq_ref, n_ref, a_own, a_twin, old_ref, *refs):
+def turn_body(first, own_count, twin_count, half_ref, sq_ref, n_ref, turned_n, a_own, a_twin, turned_a, old_ref, *refs):
     right_ref = None if first else refs[0]
     tiles_ref, squares_ref, residue_ref, next_ref, image_ref, norms_ref = refs[-6:]
     cols = half_ref.shape[1]
@@ -100,10 +114,10 @@
     v_norm = jnp.sqrt(jnp.sum(raw_vec * raw_vec, axis=1, keepdims=True) + floor_sq)
     next_vec = raw_vec / v_norm
     next_ref[...] = next_vec
-    image = nt(next_vec.astype(bf16), n_ref[...])
+    image = nn(next_vec.astype(bf16), turned_n[...])
     image_ref[...] = image
     pushed = image.astype(bf16)
-    ahead = jnp.concatenate([nt(pushed, a_own[...]), nt(pushed, a_twin[...])], axis=1)
+    ahead = jnp.concatenate([nn(pushed, turned_a[...]), nt(pushed, a_twin[...])], axis=1)
     residue = masked(ahead - v_norm * (old_ref[...] / u_norm), own_count[0], twin_count[0])
     residue_ref[...] = residue
     norms_ref[:, :LANES] = jnp.broadcast_to(u_norm, (cols, LANES))
@@ -139,7 +153,10 @@
 
 
 def pack_body(*refs):
-    *sources, out_ref, work = refs
+    *sources, out_ref = refs
+    share = out_ref.shape[0]
+    _, at = own_place(sources[0].shape[0], share)
+    sources = [ref.at[pl.ds(at, share)] for ref in sources]
     rights, images, norms = (sources[:ITERS], sources[ITERS : 2 * ITERS], sources[2 * ITERS :])
     width = rights[0].shape[1]
     start_norm = norms[0][:, 0:1]
@@ -160,12 +177,9 @@
         search = rights[k][...] - coupling / radius * search
         search_image = images[k][...] - coupling / radius * search_image
     for j, value in enumerate((coeffs, solution, search, search_image)):
-        work[:, j * width : (j + 1) * width] = value
+        out_ref[:, j * width : (j + 1) * width] = value
     for j, value in enumerate((phi_bar, rho_bar, start_norm)):
-        work[:, 4 * width + j * LANES : 4 * width + (j + 1) * LANES] = jnp.broadcast_to(value, (value.shape[0], LANES))
-    share = out_ref.shape[0]
-    _, at = own_place(work.shape[0], share)
-    out_ref[...] = work[pl.ds(at, share), :]
+        out_ref[:, 4 * width + j * LANES : 4 * width + (j + 1) * LANES] = jnp.broadcast_to(value, (share, LANES))
 
 
 def final_body(everyone_ref, mine_ref, twin_ref, out_ref, coeffs_ref, ratio_ref, column):
@@ -190,7 +204,7 @@
     phi_bar = u_norm / radius * phi_bar
     coeffs_ref[...] = piece(0, width) + step * piece(2 * width, width)
     out_ref[...] = piece(width, width) + step * piece(3 * width, width)
-    ratio_ref[...] = to_lanes(phi_bar / start_norm)
+    ratio_ref[...] = to_lanes(phi_bar / start_norm)[:, :share]
 
 
 def exchange(tiles, axis):
@@ -227,7 +241,17 @@
     twin_side = swap_cores(right_side)
     twin_counts = swap_cores(row_counts)
     counts = [row_counts, twin_counts]
-    blocks = [matrix, twin_matrix]
+    anywhere = pl.BlockSpec(memory_space=pltpu.HBM)
+    held, turned, own, turned_own = run(
+        load_body,
+        [(precond.shape, bf16), (precond.shape[::-1], bf16), (matrix.shape, bf16), (matrix.shape[::-1], bf16)],
+        [precond, matrix],
+        [anywhere] * 2,
+        "load",
+        scratch=[pltpu.SemaphoreType.DMA(((width + local_rows) // LOAD_ROWS,))],
+        limit=24 * 1024 * 1024,
+    )
+    blocks = [own, twin_matrix]
     tiles_shape = (width // LANES, cols + SQ_ROWS, LANES)
     tiles, _, residue = run(
         start_body,
@@ -250,8 +274,8 @@
                 ((cols, width), f32),
                 ((cols, 2 * LANES), f32),
             ],
-            [*counts, half, squares, precond, *blocks, residue] + ([] if first else [right_vec]),
-            [SMEM] * 2 + [VMEM] * (6 if first else 7),
+            [*counts, half, squares, held, turned, *blocks, turned_own, residue] + ([] if first else [right_vec]),
+            [SMEM] * 2 + [VMEM] * (8 if first else 9),
             "turn",
             limit=20 * 1024 * 1024,
         )
@@ -282,20 +306,19 @@
         [*rights, *images, *norms],
         [VMEM] * (3 * ITERS),
         "pack",
-        scratch=[pltpu.VMEM((cols, 4 * width + 3 * LANES), f32)],
         limit=12 * 1024 * 1024,
     )[0]
     twin_packed = swap_cores(packed)
     out, coeffs, ratio = run(
         final_body,
-        [((share, width), f32), ((share, width), f32), ((1, LANES), f32)],
+        [((share, width), f32), ((share, width), f32), ((1, share), f32)],
         [everyone, packed, twin_packed],
         [VMEM] * 3,
         "final",
         scratch=[pltpu.VMEM((cols, LANES), f32)],
         limit=12 * 1024 * 1024,
     )
-    return (out.T, coeffs.T, ratio[0, :share])
+    return (out.T, coeffs.T, ratio[0])
 
 
 def solution(mesh):

time: 173 us -> 164 us (0.948)
  local copies, waits for them, and re-layouts: 6.4 us -> 1.59 us
  waiting for transfers between devices: 3.03 us -> 0.01 us
    unnamed x10 -> x4, local copies, waits for them, and re-layouts: 5.89 us -> 1.59 us
    ppermute x4, waiting for transfers between devices: 3.03 us -> 0.01 us  [swap_cores(): return lax.ppermute(value, 'core', [(0, 1), (1, 0)])]
    pallas_call x12 -> x13, Pallas kernels: 26 us -> 25.4 us  [run(): pl.pallas_call(body, out_shape=[jax.ShapeDtypeStruct(s, t) for s, t in sh...]
  transfers between devices with their start and end apart: 4 -> 4, of which waited for: 1 -> 0; matrix products, arithmetic and copies ran while one was open for 0% -> 0% of each run, Pallas kernels for 0% -> 3%
where the time goes in v3:
time: 164 us
  blocking collectives  120 us (73%)
  Pallas kernels  25.4 us (15%)
  starting transfers between devices  15.5 us (9%)
    all_to_all x10, blocking collectives, exchange(): return lax.all_to_all(tiles, axis, 0, 0, tiled=True)  120 us
    pallas_call x13, Pallas kernels, run(): pl.pallas_call(body, out_shape=[jax.ShapeDtypeStruct(s, t) for s, t in sh...  25.4 us
    ppermute x4, starting transfers between devices, swap_cores(): return lax.ppermute(value, 'core', [(0, 1), (1, 0)])  15.5 us
  transfers between devices with their start and end apart: 4, of which 0 were waited for; matrix products, arithmetic and copies ran while one was open for 0% of the time, Pallas kernels for 3%

profile of v3, /device:TPU:1, one launch (start us, length us, event | category | flops | bytes accessed | tf_op | source)
XLA Modules:
  0.0 163.9 jit_solution(17697824895767962967)
XLA Ops:
  0.6 3.3 %collective-permute-start.2 = (bf16[512,2048]{1,0:T(8,128)(2,1)}, bf16[512,2048]{1,0:T(8,128)(2,1)S(1)}, u32[]{:S(2)}, u32[]{:S(2)}) collective-permute-start(bf16[512,2048]{1,0:T(8,128)(2,1)} %a_in.1), channel_id=1, source_target_pairs={{0,8},{8,0},{1,9},{9,1},{2,10},{10,2},{3,11},{11,3},{4,12},{12,4},... | collective-permute-start | bytes 6291464 | tf_op jit(solution)/shard_map/ppermute | solution.py:215
  3.9 0.1 collective-permute-start.1
  4.0 0.4 collective-permute-start
  5.1 0.0 copy-start
  5.1 1.6 copy-done
  6.7 0.0 copy-start.1
  6.7 4.3 %load.1 = (bf16[2048,2048]{1,0:T(8,128)(2,1)S(1)}, bf16[2048,2048]{1,0:T(8,128)(2,1)S(1)}, bf16[512,2048]{1,0:T(8,128)(2,1)S(1)}, bf16[2048,512]{1,0:T(8,128)(2,1)S(1)}) custom-call(bf16[2048,2048]{1,0:T(8,128)(2,1)} %n_in.1, bf16[512,2048]{1,0:T(8,128)(2,1)S(1)} %copy-done), custom_call_target="tpu_custom_call" | custom-call | tf_op jit(solution)/shard_map/load/pallas_call | solution.py:24
  11.0 0.0 collective-permute-done.twin_count
  11.0 0.0 collective-permute-done.1.b_twin
  11.0 0.0 collective-permute-done.2.a_twin
  11.0 0.0 copy-done.1
  11.0 1.7 %start.1 = (bf16[16,72,128]{2,1,0:T(8,128)(2,1)S(1)}, f32[1,1,128]{2,1,0:T(1,128)}, f32[64,1024]{1,0:T(8,128)S(1)}) custom-call(s32[1]{0:T(128)S(6)} %copy.7.own_count, s32[1]{0:T(128)} %collective-permute-done.twin_count, bf16[512,128]{1,0:T(8,128)(2,1)S(1)} %copy-done.1, bf16[512,128]{1,0:T(8,128)(2,1)S(1)} %collective-permute-done.1.b_twin, ...), custom_call_target="tpu_custom_call" | custom-call | tf_op jit(solution)/shard_map/start/pallas_call | solution.py:24
  12.7 13.6 %all_to_all.53.tiles_ref = bf16[16,72,128]{2,1,0:T(8,128)(2,1)S(1)} all-to-all(bf16[16,72,128]{2,1,0:T(8,128)(2,1)S(1)} %get-tuple-element.33), channel_id=1, replica_groups=mesh['y'=4,'x'=4,'core'=2,'grp'=8] {'y','x'}, dimensions={0} | all-to-all | bytes 589824 | tf_op jit(solution)/shard_map/all_to_all | solution.py:211
  26.3 16.2 %all_to_all.54.tiles_ref = bf16[8,72,128]{2,1,0:T(8,128)(2,1)S(1)} all-to-all(bf16[8,72,128]{2,1,0:T(8,128)(2,1)S(1)} %plane_sum.3), channel_id=1, replica_groups=mesh['y'=4,'x'=4,'core'=2,'grp'=8] {'grp'}, dimensions={0} | all-to-all | bytes 294912 | tf_op jit(solution)/shard_map/all_to_all | solution.py:211
  42.5 10.2 %all_to_all.55.half_ref = bf16[16,64,128]{2,1,0:T(8,128)(2,1)S(1)} all-to-all(bf16[16,64,128]{2,1,0:T(8,128)(2,1)S(1)} %get-tuple-element.34), channel_id=1, replica_groups=mesh['y'=4,'x'=4,'core'=2,'grp'=8] {'y','x'}, dimensions={0} | all-to-all | bytes 524288 | tf_op jit(solution)/shard_map/all_to_all | solution.py:211
  52.8 5.8 %turn.3 = (bf16[16,72,128]{2,1,0:T(8,128)(2,1)S(1)}, f32[1,1,128]{2,1,0:T(1,128)}, f32[64,1024]{1,0:T(8,128)S(1)}, f32[64,2048]{1,0:T(8,128)S(1)}, f32[64,2048]{1,0:T(8,128)S(1)}, /*index=5*/f32[64,256]{1,0:T(8,128)S(1)}) custom-call(s32[1]{0:T(128)S(6)} %copy.7.own_count, s32[1]{0:T(128)} %collective-permute-done.twin_count, ...), custom_call_target="tpu_custom_call" | custom-call | tf_op jit(solution)/shard_map/turn/pallas_call | solution.py:24
  58.5 10.6 %all_to_all.56.tiles_ref = bf16[16,72,128]{2,1,0:T(8,128)(2,1)S(1)} all-to-all(bf16[16,72,128]{2,1,0:T(8,128)(2,1)S(1)} %get-tuple-element.40), channel_id=1, replica_groups=mesh['y'=4,'x'=4,'core'=2,'grp'=8] {'y','x'}, dimensions={0} | all-to-all | bytes 589824 | tf_op jit(solution)/shard_map/all_to_all | solution.py:211
  69.1 10.5 %all_to_all.57.tiles_ref = bf16[8,72,128]{2,1,0:T(8,128)(2,1)S(1)} all-to-all(bf16[8,72,128]{2,1,0:T(8,128)(2,1)S(1)} %plane_sum.4), channel_id=1, replica_groups=mesh['y'=4,'x'=4,'core'=2,'grp'=8] {'grp'}, dimensions={0} | all-to-all | bytes 294912 | tf_op jit(solution)/shard_map/all_to_all | solution.py:211
  79.7 10.1 %all_to_all.58.half_ref = bf16[16,64,128]{2,1,0:T(8,128)(2,1)S(1)} all-to-all(bf16[16,64,128]{2,1,0:T(8,128)(2,1)S(1)} %get-tuple-element.41), channel_id=1, replica_groups=mesh['y'=4,'x'=4,'core'=2,'grp'=8] {'y','x'}, dimensions={0} | all-to-all | bytes 524288 | tf_op jit(solution)/shard_map/all_to_all | solution.py:211
  89.8 5.8 %turn.4 = (bf16[16,72,128]{2,1,0:T(8,128)(2,1)S(1)}, f32[1,1,128]{2,1,0:T(1,128)}, f32[64,1024]{1,0:T(8,128)S(1)}, f32[64,2048]{1,0:T(8,128)S(1)}, f32[64,2048]{1,0:T(8,128)S(1)}, /*index=5*/f32[64,256]{1,0:T(8,128)S(1)}) custom-call(s32[1]{0:T(128)S(6)} %copy.7.own_count, s32[1]{0:T(128)} %collective-permute-done.twin_count, ...), custom_call_target="tpu_custom_call" | custom-call | tf_op jit(solution)/shard_map/turn/pallas_call | solution.py:24
  95.6 10.3 %all_to_all.59.tiles_ref = bf16[16,72,128]{2,1,0:T(8,128)(2,1)S(1)} all-to-all(bf16[16,72,128]{2,1,0:T(8,128)(2,1)S(1)} %get-tuple-element.45), channel_id=1, replica_groups=mesh['y'=4,'x'=4,'core'=2,'grp'=8] {'y','x'}, dimensions={0} | all-to-all | bytes 589824 | tf_op jit(solution)/shard_map/all_to_all | solution.py:211
  105.9 10.5 %all_to_all.60.tiles_ref = bf16[8,72,128]{2,1,0:T(8,128)(2,1)S(1)} all-to-all(bf16[8,72,128]{2,1,0:T(8,128)(2,1)S(1)} %plane_sum.5), channel_id=1, replica_groups=mesh['y'=4,'x'=4,'core'=2,'grp'=8] {'grp'}, dimensions={0} | all-to-all | bytes 294912 | tf_op jit(solution)/shard_map/all_to_all | solution.py:211
  116.5 10.1 %all_to_all.61.half_ref = bf16[16,64,128]{2,1,0:T(8,128)(2,1)S(1)} all-to-all(bf16[16,64,128]{2,1,0:T(8,128)(2,1)S(1)} %get-tuple-element.46), channel_id=1, replica_groups=mesh['y'=4,'x'=4,'core'=2,'grp'=8] {'y','x'}, dimensions={0} | all-to-all | bytes 524288 | tf_op jit(solution)/shard_map/all_to_all | solution.py:211
  126.6 6.4 %turn.5 = (bf16[16,72,128]{2,1,0:T(8,128)(2,1)}, f32[256,1,128]{2,1,0:T(1,128)S(1)}, f32[64,1024]{1,0:T(8,128)}, f32[64,2048]{1,0:T(8,128)S(1)}, f32[64,2048]{1,0:T(8,128)S(1)}, /*index=5*/f32[64,256]{1,0:T(8,128)S(1)}) custom-call(s32[1]{0:T(128)S(6)} %copy.7.own_count, s32[1]{0:T(128)} %collective-permute-done.twin_count, ...), custom_call_target="tpu_custom_call" | custom-call | tf_op jit(solution)/shard_map/turn/pallas_call | solution.py:24
  133.0 0.2 pack.1.mine_ref
  133.2 11.7 %collective-permute-start.3 = (f32[16,8576]{1,0:T(8,128)S(1)}, f32[16,8576]{1,0:T(8,128)S(1)}, u32[]{:S(2)}, u32[]{:S(2)}) collective-permute-start(f32[16,8576]{1,0:T(8,128)S(1)} %pack.1.mine_ref), channel_id=1, source_target_pairs={{0,8},{8,0},{1,9},{9,1},{2,10},{10,2},{3,11},{11,3},{4,12},{12,4},... | collective-permute-start | bytes 1646600 | tf_op jit(solution)/shard_map/ppermute | solution.py:215
  144.9 17.9 %all_to_all.62.everyone_ref = f32[256,1,128]{2,1,0:T(1,128)S(1)} all-to-all(f32[256,1,128]{2,1,0:T(1,128)S(1)} %get-tuple-element.50), channel_id=1, replica_groups=mesh['y'=4,'x'=4,'core'=2,'grp'=8] {'y','x','core','grp'}, dimensions={0} | all-to-all | bytes 262144 | tf_op jit(solution)/shard_map/all_to_all | solution.py:211
  162.8 0.0 collective-permute-done.3.twin_ref
  162.8 1.1 final.1
  (6 shorter events, 0.2 us)
Async XLA Ops:
  0.6 10.3 %collective-permute-start.2 = (bf16[512,2048]{1,0:T(8,128)(2,1)}, bf16[512,2048]{1,0:T(8,128)(2,1)S(1)}, u32[]{:S(2)}, u32[]{:S(2)}) collective-permute-start(bf16[512,2048]{1,0:T(8,128)(2,1)} %a_in.1), channel_id=1, source_target_pairs={{0,8},{8,0},{1,9},{9,1},{2,10},{10,2},{3,11},{11,3},{4,12},{12,4},... | collective-permute-start | bytes 6291464 | tf_op jit(solution)/shard_map/ppermute | solution.py:215
  3.9 7.0 %collective-permute-start.1 = (bf16[512,128]{1,0:T(8,128)(2,1)}, bf16[512,128]{1,0:T(8,128)(2,1)S(1)}, u32[]{:S(2)}, u32[]{:S(2)}) collective-permute-start(bf16[512,128]{1,0:T(8,128)(2,1)} %b_own.1), channel_id=1, source_target_pairs={{0,8},{8,0},{1,9},{9,1},{2,10},{10,2},{3,11},{11,3},{4,12},{12,4},... | collective-permute-start | bytes 393224 | tf_op jit(solution)/shard_map/ppermute | solution.py:215
  4.0 6.9 %collective-permute-start = (s32[1]{0:T(128)}, s32[1]{0:T(128)}, u32[]{:S(2)}, u32[]{:S(2)}) collective-permute-start(s32[1]{0:T(128)} %param.7), channel_id=1, source_target_pairs={{0,8},{8,0},{1,9},{9,1},{2,10},{10,2},{3,11},{11,3},{4,12},{12,4},... | collective-permute-start | bytes 20 | tf_op jit(solution)/shard_map/ppermute | solution.py:215
  5.1 1.6 copy-start
  6.7 4.3 %copy-start.1 = (bf16[512,128]{1,0:T(8,128)(2,1)S(1)}, bf16[512,128]{1,0:T(8,128)(2,1)}, u32[]{:S(2)}) copy-start(bf16[512,128]{1,0:T(8,128)(2,1)} %b_own.1) | copy-start | bytes 393220
  133.2 29.6 %collective-permute-start.3 = (f32[16,8576]{1,0:T(8,128)S(1)}, f32[16,8576]{1,0:T(8,128)S(1)}, u32[]{:S(2)}, u32[]{:S(2)}) collective-permute-start(f32[16,8576]{1,0:T(8,128)S(1)} %pack.1.mine_ref), channel_id=1, source_target_pairs={{0,8},{8,0},{1,9},{9,1},{2,10},{10,2},{3,11},{11,3},{4,12},{12,4},... | collective-permute-start | bytes 1646600 | tf_op jit(solution)/shard_map/ppermute | solution.py:215

commit v4 on v3

--- a/solution.py
+++ b/solution.py
@@ -54,21 +54,27 @@
     return jnp.dot(left, right, preferred_element_type=f32)
 
 
-def nt(left, right):
-    return lax.dot_general(left, right, (((1,), (1,)), ((), ())), preferred_element_type=f32)
-
-
-def write_tiles(residue, own_ref, twin_ref, tiles_ref, squares_ref):
-    rows = own_ref.shape[0]
-    rounded = residue.astype(bf16)
-    partial_value = nn(rounded[:, :rows], own_ref[...]) + nn(rounded[:, rows:], twin_ref[...])
-    kept = residue.shape[0]
-    squares = to_lanes(jnp.sum(residue * residue, axis=1, keepdims=True))
-    squares_ref[...] = jnp.broadcast_to(squares.reshape(1, 1, LANES), squares_ref.shape)
+def squares_of(residue):
+    return to_lanes(jnp.sum(residue * residue, axis=1, keepdims=True))
+
+
+def put_tiles(partial_value, squares, tiles_ref):
+    kept = partial_value.shape[0]
     extra = terms_of(squares).astype(bf16)
     for j in range(tiles_ref.shape[0]):
         tiles_ref[j, :kept, :] = partial_value[:, j * LANES : (j + 1) * LANES].astype(bf16)
         tiles_ref[j, kept:, :] = extra
+
+
+def write_tiles(residue, own_ref, twin_ref, tiles_ref):
+    rows = own_ref.shape[0]
+    rounded = residue.astype(bf16)
+    partial_value = nn(rounded[:, :rows], own_ref[...]) + nn(rounded[:, rows:], twin_ref[...])
+    put_tiles(partial_value, squares_of(residue), tiles_ref)
+
+
+def tiles_body(residue_ref, own_ref, twin_ref, tiles_ref):
+    write_tiles(residue_ref[...], own_ref, twin_ref, tiles_ref)
 
 
 def masked(residue, own_count, twin_count):
@@ -78,51 +84,57 @@
     return jnp.where(live, residue, 0.0)
 
 
-def load_body(n_in, a_in, n_ref, turned_n, a_ref, turned_a, arrived):
-    jobs = []
-    for source, target, turned in ((a_in, a_ref, turned_a), (n_in, n_ref, turned_n)):
-        for at in range(0, source.shape[0], LOAD_ROWS):
-            block = pl.ds(at, LOAD_ROWS)
-            copy = pltpu.make_async_copy(source.at[block], target.at[block], arrived.at[len(jobs)])
-            copy.start()
-            jobs.append((copy, target, turned, at))
-    for copy, target, turned, at in jobs:
+def load_body(source, held, turned, arrived):
+    copies = []
+    for at in range(0, source.shape[0], LOAD_ROWS):
+        block = pl.ds(at, LOAD_ROWS)
+        copy = pltpu.make_async_copy(source.at[block], held.at[block], arrived.at[len(copies)])
+        copy.start()
+        copies.append((copy, at))
+    for copy, at in copies:
         copy.wait()
-        turned[:, at : at + LOAD_ROWS] = target[at : at + LOAD_ROWS, :].T
-
-
-def start_body(own_count, twin_count, b_own, b_twin, a_own, a_twin, tiles_ref, squares_ref, residue_ref, turned):
+        turned[:, at : at + LOAD_ROWS] = held[at : at + LOAD_ROWS, :].T
+
+
+def start_body(own_count, twin_count, b_own, b_twin, a_own, a_twin, tiles_ref, residue_ref, turned_own, turned_twin, work):
     cols = residue_ref.shape[0]
     rows = b_own.shape[0]
-    turned[:, :rows] = b_own[...].astype(f32).T
-    turned[:, rows:] = b_twin[...].astype(f32).T
-    mine = turned[pl.ds(pl.multiple_of(lax.axis_index("core") * cols, cols), cols), :]
+    work[:, :rows] = b_own[...].astype(f32).T
+    work[:, rows:] = b_twin[...].astype(f32).T
+    mine = work[pl.ds(pl.multiple_of(lax.axis_index("core") * cols, cols), cols), :]
     residue = masked(mine, own_count[0], twin_count[0])
     residue_ref[...] = residue
-    write_tiles(residue, a_own, a_twin, tiles_ref, squares_ref)
-
-
-def turn_body(first, own_count, twin_count, half_ref, sq_ref, n_ref, turned_n, a_own, a_twin, turned_a, old_ref, *refs):
+    turned_own[...] = a_own[...].T
+    turned_twin[...] = a_twin[...].T
+    write_tiles(residue, a_own, a_twin, tiles_ref)
+
+
+def turn_body(first, last, own_count, twin_count, half_ref, sq_ref, n_ref, turned_n, a_own, a_twin, turned_own, turned_twin, old_ref, *refs):
     right_ref = None if first else refs[0]
-    tiles_ref, squares_ref, residue_ref, next_ref, image_ref, norms_ref = refs[-6:]
+    sent_ref, residue_ref, next_ref, image_ref, norms_ref = refs[-5:]
     cols = half_ref.shape[1]
     u_norm = to_column(jnp.sqrt(sq_ref[0:1] + floor_sq), cols)
+    per_u = 1.0 / u_norm
     total = jnp.concatenate([half_ref[j] for j in range(half_ref.shape[0])], axis=1)
-    raw_vec = nn(total, n_ref[...]) / u_norm
+    raw_vec = nn(total, n_ref[...]) * per_u
     if not first:
         raw_vec = raw_vec - u_norm * right_ref[...]
+    image = nn(raw_vec.astype(bf16), turned_n[...])
     v_norm = jnp.sqrt(jnp.sum(raw_vec * raw_vec, axis=1, keepdims=True) + floor_sq)
-    next_vec = raw_vec / v_norm
-    next_ref[...] = next_vec
-    image = nn(next_vec.astype(bf16), turned_n[...])
+    per_v = 1.0 / v_norm
+    next_ref[...] = raw_vec * per_v
+    image = image * per_v
     image_ref[...] = image
     pushed = image.astype(bf16)
-    ahead = jnp.concatenate([nn(pushed, turned_a[...]), nt(pushed, a_twin[...])], axis=1)
-    residue = masked(ahead - v_norm * (old_ref[...] / u_norm), own_count[0], twin_count[0])
+    ahead = jnp.concatenate([nn(pushed, turned_own[...]), nn(pushed, turned_twin[...])], axis=1)
+    residue = masked(ahead - (v_norm * per_u) * old_ref[...], own_count[0], twin_count[0])
     residue_ref[...] = residue
     norms_ref[:, :LANES] = jnp.broadcast_to(u_norm, (cols, LANES))
     norms_ref[:, LANES:] = jnp.broadcast_to(v_norm, (cols, LANES))
-    write_tiles(residue, a_own, a_twin, tiles_ref, squares_ref)
+    if last:
+        sent_ref[...] = jnp.broadcast_to(squares_of(residue).reshape(1, 1, LANES), sent_ref.shape)
+    else:
+        write_tiles(residue, a_own, a_twin, sent_ref)
 
 
 def block_sum(tiles_ref, kept):
@@ -185,12 +197,14 @@
 def final_body(everyone_ref, mine_ref, twin_ref, out_ref, coeffs_ref, ratio_ref, column):
     share = mine_ref.shape[0]
     width = out_ref.shape[1]
-    tiles = everyone_ref[...].reshape(everyone_ref.shape[0], LANES)
-    sender = lax.broadcasted_iota(jnp.int32, tiles.shape, 0)
     cols = column.shape[0]
     owner, at = own_place(cols, share)
-    wanted = sender // lax.axis_size("grp") % 2 == owner
-    squares = jnp.sum(jnp.where(wanted, tiles, 0.0), axis=0, keepdims=True)
+    lines = lax.axis_size("grp")
+    by_core = [jnp.zeros((1, LANES), f32), jnp.zeros((1, LANES), f32)]
+    for sender in range(0, everyone_ref.shape[0], lines):
+        half = sender // lines % 2
+        by_core[half] = by_core[half] + jnp.sum(everyone_ref[sender : sender + lines], axis=0)
+    squares = jnp.where(owner == 0, by_core[0], by_core[1])
     column[...] = jnp.broadcast_to(to_column(jnp.sqrt(squares + floor_sq), cols), column.shape)
     u_norm = column[pl.ds(at, share), :][:, 0:1]
     own = owner == lax.axis_index("core")
@@ -237,25 +251,28 @@
 def shards(matrix, right_side, precond, row_counts):
     local_rows, width = matrix.shape
     cols = right_side.shape[1] // 2
-    twin_matrix = swap_cores(matrix)
-    twin_side = swap_cores(right_side)
-    twin_counts = swap_cores(row_counts)
+    tiles_shape = (width // LANES, cols + SQ_ROWS, LANES)
+    twin_matrix, twin_side, twin_counts = (swap_cores(value) for value in (matrix, right_side, row_counts))
     counts = [row_counts, twin_counts]
-    anywhere = pl.BlockSpec(memory_space=pltpu.HBM)
-    held, turned, own, turned_own = run(
+    blocks = [matrix, twin_matrix]
+    held, turned = run(
         load_body,
-        [(precond.shape, bf16), (precond.shape[::-1], bf16), (matrix.shape, bf16), (matrix.shape[::-1], bf16)],
-        [precond, matrix],
-        [anywhere] * 2,
+        [(precond.shape, bf16), (precond.shape[::-1], bf16)],
+        [precond],
+        [pl.BlockSpec(memory_space=pltpu.HBM)],
         "load",
-        scratch=[pltpu.SemaphoreType.DMA(((width + local_rows) // LOAD_ROWS,))],
-        limit=24 * 1024 * 1024,
-    )
-    blocks = [own, twin_matrix]
-    tiles_shape = (width // LANES, cols + SQ_ROWS, LANES)
-    tiles, _, residue = run(
+        scratch=[pltpu.SemaphoreType.DMA((width // LOAD_ROWS,))],
+        limit=36 * 1024 * 1024,
+    )
+    right_side, turned = lax.optimization_barrier((right_side, turned))
+    tiles, residue, turned_own, turned_twin = run(
         start_body,
-        [(tiles_shape, bf16), ((1, 1, LANES), f32), ((cols, 2 * local_rows), f32)],
+        [
+            (tiles_shape, bf16),
+            ((cols, 2 * local_rows), f32),
+            (matrix.shape[::-1], bf16),
+            (matrix.shape[::-1], bf16),
+        ],
         [*counts, right_side, twin_side, *blocks],
         [SMEM] * 2 + [VMEM] * 4,
         "start",
@@ -263,19 +280,14 @@
         limit=12 * 1024 * 1024,
     )
 
-    def turn(first, half, squares, right_vec, residue, copies=1):
+    def turn(half, squares, right_vec, residue, last=False):
+        first = right_vec is None
+        sent = ((lax.axis_size(every), 1, LANES), f32) if last else (tiles_shape, bf16)
         return run(
-            functools.partial(turn_body, first),
-            [
-                (tiles_shape, bf16),
-                ((copies, 1, LANES), f32),
-                (residue.shape, f32),
-                ((cols, width), f32),
-                ((cols, width), f32),
-                ((cols, 2 * LANES), f32),
-            ],
-            [*counts, half, squares, held, turned, *blocks, turned_own, residue] + ([] if first else [right_vec]),
-            [SMEM] * 2 + [VMEM] * (8 if first else 9),
+            functools.partial(turn_body, first, last),
+            [sent, (residue.shape, f32), ((cols, width), f32), ((cols, width), f32), ((cols, 2 * LANES), f32)],
+            [*counts, half, squares, held, turned, *blocks, turned_own, turned_twin, residue] + ([] if first else [right_vec]),
+            [SMEM] * 2 + [VMEM] * (9 if first else 10),
             "turn",
             limit=20 * 1024 * 1024,
         )
@@ -283,21 +295,16 @@
     right_vec = None
     rights, images, norms = ([], [], [])
     for turn_index in range(ITERS):
+        last = turn_index + 1 == ITERS
         half, squares = sum_everywhere(tiles)
-        tiles, local_squares, residue, right_vec, image, norm_pair = turn(
-            turn_index == 0,
-            half,
-            squares,
-            right_vec,
-            residue,
-            lax.axis_size(every) if turn_index + 1 == ITERS else 1,
-        )
+        tiles, residue, right_vec, image, norm_pair = turn(half, squares, right_vec, residue, last)
         rights.append(right_vec)
         images.append(image)
         norms.append(norm_pair)
+    everyone = exchange(tiles, every)
+    (tiles,) = run(tiles_body, [(tiles_shape, bf16)], [residue, *blocks], [VMEM] * 3, "tiles", limit=20 * 1024 * 1024)
     half, squares = sum_everywhere(tiles)
-    turn(False, half, squares, right_vec, residue)
-    everyone = exchange(local_squares, every)
+    turn(half, squares, right_vec, residue)
 
     share = 2 * cols // lax.axis_size("grp")
     packed = run(

time: 164 us -> 161 us (0.982)
  Pallas kernels: 25.4 us -> 23.6 us
    pallas_call x13, Pallas kernels: 25.4 us -> 23.6 us  [run(): pl.pallas_call(body, out_shape=[jax.ShapeDtypeStruct(s, t) for s, t in sh...]
where the time goes in v4:
time: 161 us
  blocking collectives  120 us (75%)
  Pallas kernels  23.6 us (15%)
  starting transfers between devices  15.5 us (10%)
    all_to_all x10, blocking collectives, exchange(): return lax.all_to_all(tiles, axis, 0, 0, tiled=True)  120 us
    pallas_call x13, Pallas kernels, run(): pl.pallas_call(body, out_shape=[jax.ShapeDtypeStruct(s, t) for s, t in sh...  23.6 us
    ppermute x4, starting transfers between devices, swap_cores(): return lax.ppermute(value, 'core', [(0, 1), (1, 0)])  15.5 us
  transfers between devices with their start and end apart: 4, of which 0 were waited for; matrix products, arithmetic and copies ran while one was open for 0% of the time, Pallas kernels for 3%

profile of v4, /device:TPU:1, one launch (start us, length us, event | category | flops | bytes accessed | tf_op | source)
XLA Modules:
  0.0 160.7 jit_solution(600451044680799205)
XLA Ops:
  0.6 3.3 %collective-permute-start.2 = (bf16[512,2048]{1,0:T(8,128)(2,1)}, bf16[512,2048]{1,0:T(8,128)(2,1)S(1)}, u32[]{:S(2)}, u32[]{:S(2)}) collective-permute-start(bf16[512,2048]{1,0:T(8,128)(2,1)} %a_own.7), channel_id=1, source_target_pairs={{0,8},{8,0},{1,9},{9,1},{2,10},{10,2},{3,11},{11,3},{4,12},{12,4},... | collective-permute-start | bytes 6291464 | tf_op jit(solution)/shard_map/ppermute | solution.py:229
  3.9 0.1 collective-permute-start.1
  4.0 0.4 collective-permute-start
  5.1 0.0 copy-start
  5.1 0.0 copy-start.1
  5.1 4.3 %load.1 = (bf16[2048,2048]{1,0:T(8,128)(2,1)S(1)}, bf16[2048,2048]{1,0:T(8,128)(2,1)S(1)}) custom-call(bf16[2048,2048]{1,0:T(8,128)(2,1)} %source.1), custom_call_target="tpu_custom_call" | custom-call | tf_op jit(solution)/shard_map/load/pallas_call | solution.py:24
  9.4 0.0 collective-permute-done.twin_count
  9.4 0.0 collective-permute-done.1.b_twin
  9.4 0.0 collective-permute-done.2.a_twin
  9.4 0.0 copy-done
  9.4 0.0 copy-done.1
  9.4 2.2 %start.1 = (bf16[16,72,128]{2,1,0:T(8,128)(2,1)S(1)}, f32[64,1024]{1,0:T(8,128)S(1)}, bf16[2048,512]{1,0:T(8,128)(2,1)S(1)}, bf16[2048,512]{1,0:T(8,128)(2,1)S(1)}) custom-call(s32[1]{0:T(128)S(6)} %copy.7.own_count, s32[1]{0:T(128)} %collective-permute-done.twin_count, bf16[512,128]{1,0:T(8,128)(2,1)S(1)} %copy-done.1, ...), custom_call_target="tpu_custom_call" | custom-call | tf_op jit(solution)/shard_map/start/pallas_call | solution.py:24
  11.6 13.6 %all_to_all.53.tiles_ref = bf16[16,72,128]{2,1,0:T(8,128)(2,1)S(1)} all-to-all(bf16[16,72,128]{2,1,0:T(8,128)(2,1)S(1)} %get-tuple-element.36), channel_id=1, replica_groups=mesh['y'=4,'x'=4,'core'=2,'grp'=8] {'y','x'}, dimensions={0} | all-to-all | bytes 589824 | tf_op jit(solution)/shard_map/all_to_all | solution.py:225
  25.3 16.2 %all_to_all.54.tiles_ref = bf16[8,72,128]{2,1,0:T(8,128)(2,1)S(1)} all-to-all(bf16[8,72,128]{2,1,0:T(8,128)(2,1)S(1)} %plane_sum.3), channel_id=1, replica_groups=mesh['y'=4,'x'=4,'core'=2,'grp'=8] {'grp'}, dimensions={0} | all-to-all | bytes 294912 | tf_op jit(solution)/shard_map/all_to_all | solution.py:225
  41.5 10.2 %all_to_all.55.half_ref = bf16[16,64,128]{2,1,0:T(8,128)(2,1)S(1)} all-to-all(bf16[16,64,128]{2,1,0:T(8,128)(2,1)S(1)} %get-tuple-element.37), channel_id=1, replica_groups=mesh['y'=4,'x'=4,'core'=2,'grp'=8] {'y','x'}, dimensions={0} | all-to-all | bytes 524288 | tf_op jit(solution)/shard_map/all_to_all | solution.py:225
  51.7 5.2 %turn.3 = (bf16[16,72,128]{2,1,0:T(8,128)(2,1)S(1)}, f32[64,1024]{1,0:T(8,128)S(1)}, f32[64,2048]{1,0:T(8,128)S(1)}, f32[64,2048]{1,0:T(8,128)S(1)}, f32[64,256]{1,0:T(8,128)S(1)}) custom-call(s32[1]{0:T(128)S(6)} %copy.7.own_count, s32[1]{0:T(128)} %collective-permute-done.twin_count, bf16[16,64,128]{2,1,0:T(8,128)(2,1)S(1)} %all_to_all.55.half_ref, ...), custom_call_target="tpu_custom_call" | custom-call | tf_op jit(solution)/shard_map/turn/pallas_call | solution.py:24
  57.0 10.6 %all_to_all.56.tiles_ref = bf16[16,72,128]{2,1,0:T(8,128)(2,1)S(1)} all-to-all(bf16[16,72,128]{2,1,0:T(8,128)(2,1)S(1)} %get-tuple-element.44), channel_id=1, replica_groups=mesh['y'=4,'x'=4,'core'=2,'grp'=8] {'y','x'}, dimensions={0} | all-to-all | bytes 589824 | tf_op jit(solution)/shard_map/all_to_all | solution.py:225
  67.6 10.5 %all_to_all.57.tiles_ref = bf16[8,72,128]{2,1,0:T(8,128)(2,1)S(1)} all-to-all(bf16[8,72,128]{2,1,0:T(8,128)(2,1)S(1)} %plane_sum.4), channel_id=1, replica_groups=mesh['y'=4,'x'=4,'core'=2,'grp'=8] {'grp'}, dimensions={0} | all-to-all | bytes 294912 | tf_op jit(solution)/shard_map/all_to_all | solution.py:225
  78.1 10.1 %all_to_all.58.half_ref = bf16[16,64,128]{2,1,0:T(8,128)(2,1)S(1)} all-to-all(bf16[16,64,128]{2,1,0:T(8,128)(2,1)S(1)} %get-tuple-element.45), channel_id=1, replica_groups=mesh['y'=4,'x'=4,'core'=2,'grp'=8] {'y','x'}, dimensions={0} | all-to-all | bytes 524288 | tf_op jit(solution)/shard_map/all_to_all | solution.py:225
  88.3 5.3 %turn.4 = (bf16[16,72,128]{2,1,0:T(8,128)(2,1)S(1)}, f32[64,1024]{1,0:T(8,128)S(1)}, f32[64,2048]{1,0:T(8,128)S(1)}, f32[64,2048]{1,0:T(8,128)S(1)}, f32[64,256]{1,0:T(8,128)S(1)}) custom-call(s32[1]{0:T(128)S(6)} %copy.7.own_count, s32[1]{0:T(128)} %collective-permute-done.twin_count, bf16[16,64,128]{2,1,0:T(8,128)(2,1)S(1)} %all_to_all.58.half_ref, ...), custom_call_target="tpu_custom_call" | custom-call | tf_op jit(solution)/shard_map/turn/pallas_call | solution.py:24
  93.5 10.3 %all_to_all.59.tiles_ref = bf16[16,72,128]{2,1,0:T(8,128)(2,1)S(1)} all-to-all(bf16[16,72,128]{2,1,0:T(8,128)(2,1)S(1)} %get-tuple-element.49), channel_id=1, replica_groups=mesh['y'=4,'x'=4,'core'=2,'grp'=8] {'y','x'}, dimensions={0} | all-to-all | bytes 589824 | tf_op jit(solution)/shard_map/all_to_all | solution.py:225
  103.9 10.5 %all_to_all.60.tiles_ref = bf16[8,72,128]{2,1,0:T(8,128)(2,1)S(1)} all-to-all(bf16[8,72,128]{2,1,0:T(8,128)(2,1)S(1)} %plane_sum.5), channel_id=1, replica_groups=mesh['y'=4,'x'=4,'core'=2,'grp'=8] {'grp'}, dimensions={0} | all-to-all | bytes 294912 | tf_op jit(solution)/shard_map/all_to_all | solution.py:225
  114.5 10.1 %all_to_all.61.half_ref = bf16[16,64,128]{2,1,0:T(8,128)(2,1)S(1)} all-to-all(bf16[16,64,128]{2,1,0:T(8,128)(2,1)S(1)} %get-tuple-element.50), channel_id=1, replica_groups=mesh['y'=4,'x'=4,'core'=2,'grp'=8] {'y','x'}, dimensions={0} | all-to-all | bytes 524288 | tf_op jit(solution)/shard_map/all_to_all | solution.py:225
  124.6 5.2 %turn.5 = (f32[256,1,128]{2,1,0:T(1,128)S(1)}, f32[64,1024]{1,0:T(8,128)}, f32[64,2048]{1,0:T(8,128)S(1)}, f32[64,2048]{1,0:T(8,128)S(1)}, f32[64,256]{1,0:T(8,128)S(1)}) custom-call(s32[1]{0:T(128)S(6)} %copy.7.own_count, s32[1]{0:T(128)} %collective-permute-done.twin_count, bf16[16,64,128]{2,1,0:T(8,128)(2,1)S(1)} %all_to_all.61.half_ref, ...), custom_call_target="tpu_custom_call" | custom-call | tf_op jit(solution)/shard_map/turn/pallas_call | solution.py:24
  129.8 0.2 pack.1.mine_ref
  130.0 11.7 %collective-permute-start.3 = (f32[16,8576]{1,0:T(8,128)S(1)}, f32[16,8576]{1,0:T(8,128)S(1)}, u32[]{:S(2)}, u32[]{:S(2)}) collective-permute-start(f32[16,8576]{1,0:T(8,128)S(1)} %pack.1.mine_ref), channel_id=1, source_target_pairs={{0,8},{8,0},{1,9},{9,1},{2,10},{10,2},{3,11},{11,3},{4,12},{12,4},... | collective-permute-start | bytes 1646600 | tf_op jit(solution)/shard_map/ppermute | solution.py:229
  141.7 17.9 %all_to_all.62.everyone_ref = f32[256,1,128]{2,1,0:T(1,128)S(1)} all-to-all(f32[256,1,128]{2,1,0:T(1,128)S(1)} %get-tuple-element.54), channel_id=1, replica_groups=mesh['y'=4,'x'=4,'core'=2,'grp'=8] {'y','x','core','grp'}, dimensions={0} | all-to-all | bytes 262144 | tf_op jit(solution)/shard_map/all_to_all | solution.py:225
  159.6 0.0 collective-permute-done.3.twin_ref
  159.6 1.1 final.1
  (6 shorter events, 0.2 us)
Async XLA Ops:
  0.6 8.8 %collective-permute-start.2 = (bf16[512,2048]{1,0:T(8,128)(2,1)}, bf16[512,2048]{1,0:T(8,128)(2,1)S(1)}, u32[]{:S(2)}, u32[]{:S(2)}) collective-permute-start(bf16[512,2048]{1,0:T(8,128)(2,1)} %a_own.7), channel_id=1, source_target_pairs={{0,8},{8,0},{1,9},{9,1},{2,10},{10,2},{3,11},{11,3},{4,12},{12,4},... | collective-permute-start | bytes 6291464 | tf_op jit(solution)/shard_map/ppermute | solution.py:229
  3.9 5.5 %collective-permute-start.1 = (bf16[512,128]{1,0:T(8,128)(2,1)}, bf16[512,128]{1,0:T(8,128)(2,1)S(1)}, u32[]{:S(2)}, u32[]{:S(2)}) collective-permute-start(bf16[512,128]{1,0:T(8,128)(2,1)} %b_own), channel_id=1, source_target_pairs={{0,8},{8,0},{1,9},{9,1},{2,10},{10,2},{3,11},{11,3},{4,12},{12,4},... | collective-permute-start | bytes 393224 | tf_op jit(solution)/shard_map/ppermute | solution.py:229
  4.0 5.4 %collective-permute-start = (s32[1]{0:T(128)}, s32[1]{0:T(128)}, u32[]{:S(2)}, u32[]{:S(2)}) collective-permute-start(s32[1]{0:T(128)} %param.7), channel_id=1, source_target_pairs={{0,8},{8,0},{1,9},{9,1},{2,10},{10,2},{3,11},{11,3},{4,12},{12,4},... | collective-permute-start | bytes 20 | tf_op jit(solution)/shard_map/ppermute | solution.py:229
  5.1 4.3 %copy-start = (bf16[512,2048]{1,0:T(8,128)(2,1)S(1)}, bf16[512,2048]{1,0:T(8,128)(2,1)}, u32[]{:S(2)}) copy-start(bf16[512,2048]{1,0:T(8,128)(2,1)} %a_own.7) | copy-start | bytes 6291460
  5.1 4.3 %copy-start.1 = (bf16[512,128]{1,0:T(8,128)(2,1)S(1)}, bf16[512,128]{1,0:T(8,128)(2,1)}, u32[]{:S(2)}) copy-start(bf16[512,128]{1,0:T(8,128)(2,1)} %b_own) | copy-start | bytes 393220
  130.0 29.6 %collective-permute-start.3 = (f32[16,8576]{1,0:T(8,128)S(1)}, f32[16,8576]{1,0:T(8,128)S(1)}, u32[]{:S(2)}, u32[]{:S(2)}) collective-permute-start(f32[16,8576]{1,0:T(8,128)S(1)} %pack.1.mine_ref), channel_id=1, source_target_pairs={{0,8},{8,0},{1,9},{9,1},{2,10},{10,2},{3,11},{11,3},{4,12},{12,4},... | collective-permute-start | bytes 1646600 | tf_op jit(solution)/shard_map/ppermute | solution.py:229

commit v5 on v4

--- a/solution.py
+++ b/solution.py
@@ -1,4 +1,5 @@
 import functools
+import itertools
 
 import jax
 import jax.numpy as jnp
@@ -10,7 +11,6 @@
 ITERS = 3
 
 floor_sq = 0.01
-plane = ("y", "x")
 every = ("y", "x", "core", "grp")
 SQ_ROWS = 8
 LANES = 128
@@ -101,7 +101,7 @@
     rows = b_own.shape[0]
     work[:, :rows] = b_own[...].astype(f32).T
     work[:, rows:] = b_twin[...].astype(f32).T
-    mine = work[pl.ds(pl.multiple_of(lax.axis_index("core") * cols, cols), cols), :]
+    mine = work[pl.ds(pl.multiple_of(own_half() * cols, cols), cols), :]
     residue = masked(mine, own_count[0], twin_count[0])
     residue_ref[...] = residue
     turned_own[...] = a_own[...].T
@@ -199,15 +199,17 @@
     width = out_ref.shape[1]
     cols = column.shape[0]
     owner, at = own_place(cols, share)
-    lines = lax.axis_size("grp")
-    by_core = [jnp.zeros((1, LANES), f32), jnp.zeros((1, LANES), f32)]
-    for sender in range(0, everyone_ref.shape[0], lines):
-        half = sender // lines % 2
-        by_core[half] = by_core[half] + jnp.sum(everyone_ref[sender : sender + lines], axis=0)
-    squares = jnp.where(owner == 0, by_core[0], by_core[1])
+    sizes = [lax.axis_size(name) for name in every]
+    run_length = sizes[3] // 2
+    by_half = [jnp.zeros((1, LANES), f32), jnp.zeros((1, LANES), f32)]
+    for sender in range(0, everyone_ref.shape[0], run_length):
+        line, rest = sender % sizes[3], sender // sizes[3]
+        half = int(half_of(rest // 2 % sizes[1], rest % 2 == 1, line, sizes[1], sizes[3]))
+        by_half[half] = by_half[half] + jnp.sum(everyone_ref[sender : sender + run_length], axis=0)
+    squares = jnp.where(owner == 0, by_half[0], by_half[1])
     column[...] = jnp.broadcast_to(to_column(jnp.sqrt(squares + floor_sq), cols), column.shape)
     u_norm = column[pl.ds(at, share), :][:, 0:1]
-    own = owner == lax.axis_index("core")
+    own = owner == own_half()
 
     def piece(start, length):
         return jnp.where(own, mine_ref[:, start : start + length], twin_ref[:, start : start + length])
@@ -221,8 +223,33 @@
     ratio_ref[...] = to_lanes(phi_bar / start_norm)[:, :share]
 
 
-def exchange(tiles, axis):
-    return lax.all_to_all(tiles, axis, 0, 0, tiled=True)
+def half_of(x, core, line, x_size, lines):
+    far = (2 * x >= x_size) ^ (2 * line >= lines)
+    return core ^ far
+
+
+def own_half():
+    return half_of(
+        lax.axis_index("x"),
+        lax.axis_index("core") == 1,
+        lax.axis_index("grp"),
+        lax.axis_size("x"),
+        lax.axis_size("grp"),
+    ).astype(jnp.int32)
+
+
+def groups_of(kind):
+    sizes = [lax.axis_size(name) for name in every]
+    groups = {}
+    for number, (y, x, core, line) in enumerate(itertools.product(*map(range, sizes))):
+        half = half_of(x, core == 1, line, sizes[1], sizes[3])
+        key = (line, half) if kind == "plane" else (y, x, half)
+        groups.setdefault(key, []).append(number)
+    return list(groups.values())
+
+
+def exchange(tiles, groups=None):
+    return lax.all_to_all(tiles, every, 0, 0, axis_index_groups=groups, tiled=True)
 
 
 def swap_cores(value):
@@ -236,16 +263,17 @@
     peers, tall, _ = tiles.shape
     kept = tall - SQ_ROWS
     lines = lax.axis_size("grp")
-    (block,) = run(plane_sum_body, [((lines, tall, LANES), bf16)], [exchange(tiles, plane)], [VMEM], "plane_sum", limit=SMALL)
+    planes = groups_of("plane")
+    (block,) = run(plane_sum_body, [((lines, tall, LANES), bf16)], [exchange(tiles, planes)], [VMEM], "plane_sum", limit=SMALL)
     half, squares = run(
         line_sum_body,
         [((peers, kept, LANES), bf16), ((SQ_ROWS, LANES), f32)],
-        [exchange(block, "grp")],
+        [exchange(block, groups_of("line"))],
         [VMEM],
         "line_sum",
         limit=SMALL,
     )
-    return (exchange(half, plane), squares)
+    return (exchange(half, planes), squares)
 
 
 def shards(matrix, right_side, precond, row_counts):
@@ -301,7 +329,7 @@
         rights.append(right_vec)
         images.append(image)
         norms.append(norm_pair)
-    everyone = exchange(tiles, every)
+    everyone = exchange(tiles)
     (tiles,) = run(tiles_body, [(tiles_shape, bf16)], [residue, *blocks], [VMEM] * 3, "tiles", limit=20 * 1024 * 1024)
     half, squares = sum_everywhere(tiles)
     turn(half, squares, right_vec, residue)

time: 161 us -> 164 us (1.019)
  blocking collectives: 120 us -> 135 us
  starting transfers between devices: 15.5 us -> 3.89 us
    all_to_all x10, blocking collectives: 120 us -> 135 us  [exchange(): lax.all_to_all(tiles, every, 0, 0, axis_index_groups=groups, tiled=True)]
    ppermute x4, starting transfers between devices: 15.5 us -> 3.89 us  [swap_cores(): return lax.ppermute(value, 'core', [(0, 1), (1, 0)])]
where the time goes in v5:
time: 164 us
  blocking collectives  135 us (82%)
  Pallas kernels  23.6 us (14%)
  starting transfers between devices  3.89 us (2%)
    all_to_all x10, blocking collectives, exchange(): lax.all_to_all(tiles, every, 0, 0, axis_index_groups=groups, tiled=True)  135 us
    pallas_call x13, Pallas kernels, run(): pl.pallas_call(body, out_shape=[jax.ShapeDtypeStruct(s, t) for s, t in sh...  23.6 us
    ppermute x4, starting transfers between devices, swap_cores(): return lax.ppermute(value, 'core', [(0, 1), (1, 0)])  3.89 us
  transfers between devices with their start and end apart: 4, of which 0 were waited for; matrix products, arithmetic and copies ran while one was open for 0% of the time, Pallas kernels for 3%

profile of v5, /device:TPU:1, one launch (start us, length us, event | category | flops | bytes accessed | tf_op | source)
XLA Modules:
  0.0 163.7 jit_solution(12319018815458133330)
XLA Ops:
  0.6 3.3 %collective-permute-start.2 = (bf16[512,2048]{1,0:T(8,128)(2,1)}, bf16[512,2048]{1,0:T(8,128)(2,1)S(1)}, u32[]{:S(2)}, u32[]{:S(2)}) collective-permute-start(bf16[512,2048]{1,0:T(8,128)(2,1)} %a_own.7), channel_id=1, source_target_pairs={{0,8},{8,0},{1,9},{9,1},{2,10},{10,2},{3,11},{11,3},{4,12},{12,4},... | collective-permute-start | bytes 6291464 | tf_op jit(solution)/shard_map/ppermute | solution.py:256
  3.9 0.1 collective-permute-start.1
  4.0 0.4 collective-permute-start
  5.1 0.0 copy-start
  5.1 0.0 copy-start.1
  5.1 4.3 %load.1 = (bf16[2048,2048]{1,0:T(8,128)(2,1)S(1)}, bf16[2048,2048]{1,0:T(8,128)(2,1)S(1)}) custom-call(bf16[2048,2048]{1,0:T(8,128)(2,1)} %source.1), custom_call_target="tpu_custom_call" | custom-call | tf_op jit(solution)/shard_map/load/pallas_call | solution.py:24
  9.4 0.0 collective-permute-done.twin_count
  9.4 0.0 collective-permute-done.1.b_twin
  9.4 0.0 collective-permute-done.2.a_twin
  9.4 0.0 copy-done
  9.4 0.0 copy-done.1
  9.4 2.2 %start.1 = (bf16[16,72,128]{2,1,0:T(8,128)(2,1)S(1)}, f32[64,1024]{1,0:T(8,128)S(1)}, bf16[2048,512]{1,0:T(8,128)(2,1)S(1)}, bf16[2048,512]{1,0:T(8,128)(2,1)S(1)}) custom-call(s32[1]{0:T(128)S(6)} %copy.7.own_count, s32[1]{0:T(128)} %collective-permute-done.twin_count, bf16[512,128]{1,0:T(8,128)(2,1)S(1)} %copy-done.1, ...), custom_call_target="tpu_custom_call" | custom-call | tf_op jit(solution)/shard_map/start/pallas_call | solution.py:24
  11.6 14.4 %all_to_all.53.tiles_ref = bf16[16,72,128]{2,1,0:T(8,128)(2,1)S(1)} all-to-all(bf16[16,72,128]{2,1,0:T(8,128)(2,1)S(1)} %get-tuple-element.36), channel_id=1, replica_groups={{0,16,40,56,64,80,104,120,128,144,168,184,192,208,232,248},{1,17,41,57,..., dimensions={0} | all-to-all | bytes 589824 | tf_op jit(solution)/shard_map/all_to_all | solution.py:252
  26.1 15.4 %all_to_all.54.tiles_ref = bf16[8,72,128]{2,1,0:T(8,128)(2,1)S(1)} all-to-all(bf16[8,72,128]{2,1,0:T(8,128)(2,1)S(1)} %plane_sum.3), channel_id=1, replica_groups={{0,1,2,3,12,13,14,15},{4,5,6,7,8,9,10,11},{16,17,18,19,28,29,30,31},{20..., dimensions={0} | all-to-all | bytes 294912 | tf_op jit(solution)/shard_map/all_to_all | solution.py:252
  41.5 12.5 %all_to_all.55.half_ref = bf16[16,64,128]{2,1,0:T(8,128)(2,1)S(1)} all-to-all(bf16[16,64,128]{2,1,0:T(8,128)(2,1)S(1)} %get-tuple-element.37), channel_id=1, replica_groups={{0,16,40,56,64,80,104,120,128,144,168,184,192,208,232,248},{1,17,41,57,..., dimensions={0} | all-to-all | bytes 524288 | tf_op jit(solution)/shard_map/all_to_all | solution.py:252
  54.0 5.2 %turn.3 = (bf16[16,72,128]{2,1,0:T(8,128)(2,1)S(1)}, f32[64,1024]{1,0:T(8,128)S(1)}, f32[64,2048]{1,0:T(8,128)S(1)}, f32[64,2048]{1,0:T(8,128)S(1)}, f32[64,256]{1,0:T(8,128)S(1)}) custom-call(s32[1]{0:T(128)S(6)} %copy.7.own_count, s32[1]{0:T(128)} %collective-permute-done.twin_count, bf16[16,64,128]{2,1,0:T(8,128)(2,1)S(1)} %all_to_all.55.half_ref, ...), custom_call_target="tpu_custom_call" | custom-call | tf_op jit(solution)/shard_map/turn/pallas_call | solution.py:24
  59.3 12.1 %all_to_all.56.tiles_ref = bf16[16,72,128]{2,1,0:T(8,128)(2,1)S(1)} all-to-all(bf16[16,72,128]{2,1,0:T(8,128)(2,1)S(1)} %get-tuple-element.44), channel_id=1, replica_groups={{0,16,40,56,64,80,104,120,128,144,168,184,192,208,232,248},{1,17,41,57,..., dimensions={0} | all-to-all | bytes 589824 | tf_op jit(solution)/shard_map/all_to_all | solution.py:252
  71.4 11.9 %all_to_all.57.tiles_ref = bf16[8,72,128]{2,1,0:T(8,128)(2,1)S(1)} all-to-all(bf16[8,72,128]{2,1,0:T(8,128)(2,1)S(1)} %plane_sum.4), channel_id=1, replica_groups={{0,1,2,3,12,13,14,15},{4,5,6,7,8,9,10,11},{16,17,18,19,28,29,30,31},{20..., dimensions={0} | all-to-all | bytes 294912 | tf_op jit(solution)/shard_map/all_to_all | solution.py:252
  83.4 12.5 %all_to_all.58.half_ref = bf16[16,64,128]{2,1,0:T(8,128)(2,1)S(1)} all-to-all(bf16[16,64,128]{2,1,0:T(8,128)(2,1)S(1)} %get-tuple-element.45), channel_id=1, replica_groups={{0,16,40,56,64,80,104,120,128,144,168,184,192,208,232,248},{1,17,41,57,..., dimensions={0} | all-to-all | bytes 524288 | tf_op jit(solution)/shard_map/all_to_all | solution.py:252
  95.9 5.3 %turn.4 = (bf16[16,72,128]{2,1,0:T(8,128)(2,1)S(1)}, f32[64,1024]{1,0:T(8,128)S(1)}, f32[64,2048]{1,0:T(8,128)S(1)}, f32[64,2048]{1,0:T(8,128)S(1)}, f32[64,256]{1,0:T(8,128)S(1)}) custom-call(s32[1]{0:T(128)S(6)} %copy.7.own_count, s32[1]{0:T(128)} %collective-permute-done.twin_count, bf16[16,64,128]{2,1,0:T(8,128)(2,1)S(1)} %all_to_all.58.half_ref, ...), custom_call_target="tpu_custom_call" | custom-call | tf_op jit(solution)/shard_map/turn/pallas_call | solution.py:24
  101.1 12.1 %all_to_all.59.tiles_ref = bf16[16,72,128]{2,1,0:T(8,128)(2,1)S(1)} all-to-all(bf16[16,72,128]{2,1,0:T(8,128)(2,1)S(1)} %get-tuple-element.49), channel_id=1, replica_groups={{0,16,40,56,64,80,104,120,128,144,168,184,192,208,232,248},{1,17,41,57,..., dimensions={0} | all-to-all | bytes 589824 | tf_op jit(solution)/shard_map/all_to_all | solution.py:252
  113.3 12.0 %all_to_all.60.tiles_ref = bf16[8,72,128]{2,1,0:T(8,128)(2,1)S(1)} all-to-all(bf16[8,72,128]{2,1,0:T(8,128)(2,1)S(1)} %plane_sum.5), channel_id=1, replica_groups={{0,1,2,3,12,13,14,15},{4,5,6,7,8,9,10,11},{16,17,18,19,28,29,30,31},{20..., dimensions={0} | all-to-all | bytes 294912 | tf_op jit(solution)/shard_map/all_to_all | solution.py:252
  125.3 12.4 %all_to_all.61.half_ref = bf16[16,64,128]{2,1,0:T(8,128)(2,1)S(1)} all-to-all(bf16[16,64,128]{2,1,0:T(8,128)(2,1)S(1)} %get-tuple-element.50), channel_id=1, replica_groups={{0,16,40,56,64,80,104,120,128,144,168,184,192,208,232,248},{1,17,41,57,..., dimensions={0} | all-to-all | bytes 524288 | tf_op jit(solution)/shard_map/all_to_all | solution.py:252
  137.7 5.2 %turn.5 = (f32[256,1,128]{2,1,0:T(1,128)S(1)}, f32[64,1024]{1,0:T(8,128)}, f32[64,2048]{1,0:T(8,128)S(1)}, f32[64,2048]{1,0:T(8,128)S(1)}, f32[64,256]{1,0:T(8,128)S(1)}) custom-call(s32[1]{0:T(128)S(6)} %copy.7.own_count, s32[1]{0:T(128)} %collective-permute-done.twin_count, bf16[16,64,128]{2,1,0:T(8,128)(2,1)S(1)} %all_to_all.61.half_ref, ...), custom_call_target="tpu_custom_call" | custom-call | tf_op jit(solution)/shard_map/turn/pallas_call | solution.py:24
  142.9 0.2 pack.1.mine_ref
  143.0 0.1 collective-permute-start.3
  143.1 19.5 %all_to_all.62.everyone_ref = f32[256,1,128]{2,1,0:T(1,128)S(1)} all-to-all(f32[256,1,128]{2,1,0:T(1,128)S(1)} %get-tuple-element.54), channel_id=1, replica_groups=mesh['y'=4,'x'=4,'core'=2,'grp'=8] {'y','x','core','grp'}, dimensions={0} | all-to-all | bytes 262144 | tf_op jit(solution)/shard_map/all_to_all | solution.py:252
  162.6 0.0 collective-permute-done.3.twin_ref
  162.6 1.0 final.1
  (6 shorter events, 0.2 us)
Async XLA Ops:
  0.6 8.8 %collective-permute-start.2 = (bf16[512,2048]{1,0:T(8,128)(2,1)}, bf16[512,2048]{1,0:T(8,128)(2,1)S(1)}, u32[]{:S(2)}, u32[]{:S(2)}) collective-permute-start(bf16[512,2048]{1,0:T(8,128)(2,1)} %a_own.7), channel_id=1, source_target_pairs={{0,8},{8,0},{1,9},{9,1},{2,10},{10,2},{3,11},{11,3},{4,12},{12,4},... | collective-permute-start | bytes 6291464 | tf_op jit(solution)/shard_map/ppermute | solution.py:256
  3.9 5.5 %collective-permute-start.1 = (bf16[512,128]{1,0:T(8,128)(2,1)}, bf16[512,128]{1,0:T(8,128)(2,1)S(1)}, u32[]{:S(2)}, u32[]{:S(2)}) collective-permute-start(bf16[512,128]{1,0:T(8,128)(2,1)} %b_own), channel_id=1, source_target_pairs={{0,8},{8,0},{1,9},{9,1},{2,10},{10,2},{3,11},{11,3},{4,12},{12,4},... | collective-permute-start | bytes 393224 | tf_op jit(solution)/shard_map/ppermute | solution.py:256
  4.0 5.4 %collective-permute-start = (s32[1]{0:T(128)}, s32[1]{0:T(128)}, u32[]{:S(2)}, u32[]{:S(2)}) collective-permute-start(s32[1]{0:T(128)} %param.7), channel_id=1, source_target_pairs={{0,8},{8,0},{1,9},{9,1},{2,10},{10,2},{3,11},{11,3},{4,12},{12,4},... | collective-permute-start | bytes 20 | tf_op jit(solution)/shard_map/ppermute | solution.py:256
  5.1 4.3 %copy-start = (bf16[512,2048]{1,0:T(8,128)(2,1)S(1)}, bf16[512,2048]{1,0:T(8,128)(2,1)}, u32[]{:S(2)}) copy-start(bf16[512,2048]{1,0:T(8,128)(2,1)} %a_own.7) | copy-start | bytes 6291460
  5.1 4.3 %copy-start.1 = (bf16[512,128]{1,0:T(8,128)(2,1)S(1)}, bf16[512,128]{1,0:T(8,128)(2,1)}, u32[]{:S(2)}) copy-start(bf16[512,128]{1,0:T(8,128)(2,1)} %b_own) | copy-start | bytes 393220
  143.0 19.6 %collective-permute-start.3 = (f32[16,8576]{1,0:T(8,128)S(1)}, f32[16,8576]{1,0:T(8,128)S(1)}, u32[]{:S(2)}, u32[]{:S(2)}) collective-permute-start(f32[16,8576]{1,0:T(8,128)S(1)} %pack.1.mine_ref), channel_id=1, source_target_pairs={{0,8},{8,0},{1,9},{9,1},{2,10},{10,2},{3,11},{11,3},{4,12},{12,4},... | collective-permute-start | bytes 1646600 | tf_op jit(solution)/shard_map/ppermute | solution.py:256

commit v6 on v4

--- a/solution.py
+++ b/solution.py
@@ -17,7 +17,6 @@
 LOAD_ROWS = 256
 bf16, f32 = jnp.bfloat16, jnp.float32
 VMEM = pl.BlockSpec(memory_space=pltpu.VMEM)
-SMEM = pl.BlockSpec(memory_space=pltpu.SMEM)
 
 
 def run(body, shapes, operands, specs, name, scratch=(), limit=None):
@@ -77,13 +76,6 @@
     write_tiles(residue_ref[...], own_ref, twin_ref, tiles_ref)
 
 
-def masked(residue, own_count, twin_count):
-    rows = residue.shape[1] // 2
-    slot = lax.broadcasted_iota(jnp.int32, residue.shape, 1)
-    live = (slot < own_count) | ((slot >= rows) & (slot < rows + twin_count))
-    return jnp.where(live, residue, 0.0)
-
-
 def load_body(source, held, turned, arrived):
     copies = []
     for at in range(0, source.shape[0], LOAD_ROWS):
@@ -96,20 +88,23 @@
         turned[:, at : at + LOAD_ROWS] = held[at : at + LOAD_ROWS, :].T
 
 
-def start_body(own_count, twin_count, b_own, b_twin, a_own, a_twin, tiles_ref, residue_ref, turned_own, turned_twin, work):
+def start_body(own_count, twin_count, b_own, b_twin, a_own, a_twin, tiles_ref, residue_ref, live_ref, turned_own, turned_twin, work):
     cols = residue_ref.shape[0]
     rows = b_own.shape[0]
     work[:, :rows] = b_own[...].astype(f32).T
     work[:, rows:] = b_twin[...].astype(f32).T
     mine = work[pl.ds(pl.multiple_of(lax.axis_index("core") * cols, cols), cols), :]
-    residue = masked(mine, own_count[0], twin_count[0])
+    slot = lax.broadcasted_iota(jnp.int32, (1, rows), 1)
+    live = jnp.concatenate([slot < own_count[...], slot < twin_count[...]], axis=1).astype(f32)
+    live_ref[...] = live
+    residue = live * mine
     residue_ref[...] = residue
     turned_own[...] = a_own[...].T
     turned_twin[...] = a_twin[...].T
     write_tiles(residue, a_own, a_twin, tiles_ref)
 
 
-def turn_body(first, last, own_count, twin_count, half_ref, sq_ref, n_ref, turned_n, a_own, a_twin, turned_own, turned_twin, old_ref, *refs):
+def turn_body(first, last, live_ref, half_ref, sq_ref, n_ref, turned_n, a_own, a_twin, turned_own, turned_twin, old_ref, *refs):
     right_ref = None if first else refs[0]
     sent_ref, residue_ref, next_ref, image_ref, norms_ref = refs[-5:]
     cols = half_ref.shape[1]
@@ -119,15 +114,14 @@
     raw_vec = nn(total, n_ref[...]) * per_u
     if not first:
         raw_vec = raw_vec - u_norm * right_ref[...]
-    image = nn(raw_vec.astype(bf16), turned_n[...])
     v_norm = jnp.sqrt(jnp.sum(raw_vec * raw_vec, axis=1, keepdims=True) + floor_sq)
-    per_v = 1.0 / v_norm
-    next_ref[...] = raw_vec * per_v
-    image = image * per_v
+    next_vec = raw_vec * (1.0 / v_norm)
+    next_ref[...] = next_vec
+    image = nn(next_vec.astype(bf16), turned_n[...])
     image_ref[...] = image
     pushed = image.astype(bf16)
     ahead = jnp.concatenate([nn(pushed, turned_own[...]), nn(pushed, turned_twin[...])], axis=1)
-    residue = masked(ahead - (v_norm * per_u) * old_ref[...], own_count[0], twin_count[0])
+    residue = live_ref[...] * (ahead - (v_norm * per_u) * old_ref[...])
     residue_ref[...] = residue
     norms_ref[:, :LANES] = jnp.broadcast_to(u_norm, (cols, LANES))
     norms_ref[:, LANES:] = jnp.broadcast_to(v_norm, (cols, LANES))
@@ -253,7 +247,6 @@
     cols = right_side.shape[1] // 2
     tiles_shape = (width // LANES, cols + SQ_ROWS, LANES)
     twin_matrix, twin_side, twin_counts = (swap_cores(value) for value in (matrix, right_side, row_counts))
-    counts = [row_counts, twin_counts]
     blocks = [matrix, twin_matrix]
     held, turned = run(
         load_body,
@@ -264,17 +257,19 @@
         scratch=[pltpu.SemaphoreType.DMA((width // LOAD_ROWS,))],
         limit=36 * 1024 * 1024,
     )
+    counts = [row_counts.reshape(1, 1), twin_counts.reshape(1, 1)]
     right_side, turned = lax.optimization_barrier((right_side, turned))
-    tiles, residue, turned_own, turned_twin = run(
+    tiles, residue, live, turned_own, turned_twin = run(
         start_body,
         [
             (tiles_shape, bf16),
             ((cols, 2 * local_rows), f32),
+            ((1, 2 * local_rows), f32),
             (matrix.shape[::-1], bf16),
             (matrix.shape[::-1], bf16),
         ],
         [*counts, right_side, twin_side, *blocks],
-        [SMEM] * 2 + [VMEM] * 4,
+        [VMEM] * 6,
         "start",
         scratch=[pltpu.VMEM((2 * cols, 2 * local_rows), f32)],
         limit=12 * 1024 * 1024,
@@ -286,8 +281,8 @@
         return run(
             functools.partial(turn_body, first, last),
             [sent, (residue.shape, f32), ((cols, width), f32), ((cols, width), f32), ((cols, 2 * LANES), f32)],
-            [*counts, half, squares, held, turned, *blocks, turned_own, turned_twin, residue] + ([] if first else [right_vec]),
-            [SMEM] * 2 + [VMEM] * (9 if first else 10),
+            [live, half, squares, held, turned, *blocks, turned_own, turned_twin, residue] + ([] if first else [right_vec]),
+            [VMEM] * (10 if first else 11),
             "turn",
             limit=20 * 1024 * 1024,
         )

time: 161 us -> 160 us (level)
  no operation moved by 1% of the time
where the time goes in v6:
time: 160 us; the launch traced here: 159 us
  blocking collectives  120 us (75%)
  Pallas kernels  22.2 us (14%)
  starting transfers between devices  15.5 us (10%)
    all_to_all x10, blocking collectives, exchange(): return lax.all_to_all(tiles, axis, 0, 0, tiled=True)  120 us
    pallas_call x13, Pallas kernels, run(): pl.pallas_call(body, out_shape=[jax.ShapeDtypeStruct(s, t) for s, t in sh...  22.2 us
    ppermute x4, starting transfers between devices, swap_cores(): return lax.ppermute(value, 'core', [(0, 1), (1, 0)])  15.5 us
  transfers between devices with their start and end apart: 4, of which 0 were waited for; matrix products, arithmetic and copies ran while one was open for 0% of the time, Pallas kernels for 3%

profile of v6, /device:TPU:1, one launch (start us, length us, event | category | flops | bytes accessed | tf_op | source)
XLA Modules:
  0.0 159.3 jit_solution(10814903192777450299)
XLA Ops:
  0.6 3.3 %collective-permute-start.2 = (bf16[512,2048]{1,0:T(8,128)(2,1)}, bf16[512,2048]{1,0:T(8,128)(2,1)S(1)}, u32[]{:S(2)}, u32[]{:S(2)}) collective-permute-start(bf16[512,2048]{1,0:T(8,128)(2,1)} %a_own.7), channel_id=1, source_target_pairs={{0,8},{8,0},{1,9},{9,1},{2,10},{10,2},{3,11},{11,3},{4,12},{12,4},... | collective-permute-start | bytes 6291464 | tf_op jit(solution)/shard_map/ppermute | solution.py:223
  3.9 0.1 collective-permute-start.1
  4.0 0.4 collective-permute-start
  5.1 0.0 copy-start
  5.1 0.0 copy-start.1
  5.1 4.3 %load.1 = (bf16[2048,2048]{1,0:T(8,128)(2,1)S(1)}, bf16[2048,2048]{1,0:T(8,128)(2,1)S(1)}) custom-call(bf16[2048,2048]{1,0:T(8,128)(2,1)} %source.1), custom_call_target="tpu_custom_call" | custom-call | tf_op jit(solution)/shard_map/load/pallas_call | solution.py:23
  9.4 0.0 collective-permute-done
  9.4 0.0 collective-permute-done.1.b_twin
  9.4 0.0 collective-permute-done.2.a_twin
  9.4 0.0 copy-done
  9.4 0.0 copy-done.1
  9.4 2.3 %start.1 = (bf16[16,72,128]{2,1,0:T(8,128)(2,1)S(1)}, f32[64,1024]{1,0:T(8,128)S(1)}, f32[1,1024]{1,0:T(1,128)S(1)}, bf16[2048,512]{1,0:T(8,128)(2,1)S(1)}, bf16[2048,512]{1,0:T(8,128)(2,1)S(1)}) custom-call(s32[1,1]{1,0:T(1,128)} %bitcast.5.own_count, s32[1,1]{1,0:T(1,128)} %bitcast.1.twin_count, bf16[512,128]{1,0:T(8,128)(2,1)S(1)} %copy-done.1, ...), custom_call_target="tpu_custom_call" | custom-call | tf_op jit(solution)/shard_map/start/pallas_call | solution.py:23
  11.7 13.6 %all_to_all.53.tiles_ref = bf16[16,72,128]{2,1,0:T(8,128)(2,1)S(1)} all-to-all(bf16[16,72,128]{2,1,0:T(8,128)(2,1)S(1)} %get-tuple-element.38), channel_id=1, replica_groups=mesh['y'=4,'x'=4,'core'=2,'grp'=8] {'y','x'}, dimensions={0} | all-to-all | bytes 589824 | tf_op jit(solution)/shard_map/all_to_all | solution.py:219
  25.3 16.2 %all_to_all.54.tiles_ref = bf16[8,72,128]{2,1,0:T(8,128)(2,1)S(1)} all-to-all(bf16[8,72,128]{2,1,0:T(8,128)(2,1)S(1)} %plane_sum.3), channel_id=1, replica_groups=mesh['y'=4,'x'=4,'core'=2,'grp'=8] {'grp'}, dimensions={0} | all-to-all | bytes 294912 | tf_op jit(solution)/shard_map/all_to_all | solution.py:219
  41.6 10.2 %all_to_all.55.half_ref = bf16[16,64,128]{2,1,0:T(8,128)(2,1)S(1)} all-to-all(bf16[16,64,128]{2,1,0:T(8,128)(2,1)S(1)} %get-tuple-element.39), channel_id=1, replica_groups=mesh['y'=4,'x'=4,'core'=2,'grp'=8] {'y','x'}, dimensions={0} | all-to-all | bytes 524288 | tf_op jit(solution)/shard_map/all_to_all | solution.py:219
  51.8 4.8 %turn.3 = (bf16[16,72,128]{2,1,0:T(8,128)(2,1)S(1)}, f32[64,1024]{1,0:T(8,128)S(1)}, f32[64,2048]{1,0:T(8,128)S(1)}, f32[64,2048]{1,0:T(8,128)S(1)}, f32[64,256]{1,0:T(8,128)S(1)}) custom-call(f32[1,1024]{1,0:T(1,128)S(1)} %get-tuple-element.37.live_ref, bf16[16,64,128]{2,1,0:T(8,128)(2,1)S(1)} %all_to_all.55.half_ref, ...), custom_call_target="tpu_custom_call" | custom-call | tf_op jit(solution)/shard_map/turn/pallas_call | solution.py:23
  56.6 10.6 %all_to_all.56.tiles_ref = bf16[16,72,128]{2,1,0:T(8,128)(2,1)S(1)} all-to-all(bf16[16,72,128]{2,1,0:T(8,128)(2,1)S(1)} %get-tuple-element.46), channel_id=1, replica_groups=mesh['y'=4,'x'=4,'core'=2,'grp'=8] {'y','x'}, dimensions={0} | all-to-all | bytes 589824 | tf_op jit(solution)/shard_map/all_to_all | solution.py:219
  67.2 10.5 %all_to_all.57.tiles_ref = bf16[8,72,128]{2,1,0:T(8,128)(2,1)S(1)} all-to-all(bf16[8,72,128]{2,1,0:T(8,128)(2,1)S(1)} %plane_sum.4), channel_id=1, replica_groups=mesh['y'=4,'x'=4,'core'=2,'grp'=8] {'grp'}, dimensions={0} | all-to-all | bytes 294912 | tf_op jit(solution)/shard_map/all_to_all | solution.py:219
  77.7 10.1 %all_to_all.58.half_ref = bf16[16,64,128]{2,1,0:T(8,128)(2,1)S(1)} all-to-all(bf16[16,64,128]{2,1,0:T(8,128)(2,1)S(1)} %get-tuple-element.47), channel_id=1, replica_groups=mesh['y'=4,'x'=4,'core'=2,'grp'=8] {'y','x'}, dimensions={0} | all-to-all | bytes 524288 | tf_op jit(solution)/shard_map/all_to_all | solution.py:219
  87.8 4.8 %turn.4 = (bf16[16,72,128]{2,1,0:T(8,128)(2,1)S(1)}, f32[64,1024]{1,0:T(8,128)S(1)}, f32[64,2048]{1,0:T(8,128)S(1)}, f32[64,2048]{1,0:T(8,128)S(1)}, f32[64,256]{1,0:T(8,128)S(1)}) custom-call(f32[1,1024]{1,0:T(1,128)S(1)} %get-tuple-element.37.live_ref, bf16[16,64,128]{2,1,0:T(8,128)(2,1)S(1)} %all_to_all.58.half_ref, ...), custom_call_target="tpu_custom_call" | custom-call | tf_op jit(solution)/shard_map/turn/pallas_call | solution.py:23
  92.6 10.3 %all_to_all.59.tiles_ref = bf16[16,72,128]{2,1,0:T(8,128)(2,1)S(1)} all-to-all(bf16[16,72,128]{2,1,0:T(8,128)(2,1)S(1)} %get-tuple-element.51), channel_id=1, replica_groups=mesh['y'=4,'x'=4,'core'=2,'grp'=8] {'y','x'}, dimensions={0} | all-to-all | bytes 589824 | tf_op jit(solution)/shard_map/all_to_all | solution.py:219
  103.0 10.5 %all_to_all.60.tiles_ref = bf16[8,72,128]{2,1,0:T(8,128)(2,1)S(1)} all-to-all(bf16[8,72,128]{2,1,0:T(8,128)(2,1)S(1)} %plane_sum.5), channel_id=1, replica_groups=mesh['y'=4,'x'=4,'core'=2,'grp'=8] {'grp'}, dimensions={0} | all-to-all | bytes 294912 | tf_op jit(solution)/shard_map/all_to_all | solution.py:219
  113.5 10.1 %all_to_all.61.half_ref = bf16[16,64,128]{2,1,0:T(8,128)(2,1)S(1)} all-to-all(bf16[16,64,128]{2,1,0:T(8,128)(2,1)S(1)} %get-tuple-element.52), channel_id=1, replica_groups=mesh['y'=4,'x'=4,'core'=2,'grp'=8] {'y','x'}, dimensions={0} | all-to-all | bytes 524288 | tf_op jit(solution)/shard_map/all_to_all | solution.py:219
  123.7 4.7 %turn.5 = (f32[256,1,128]{2,1,0:T(1,128)S(1)}, f32[64,1024]{1,0:T(8,128)}, f32[64,2048]{1,0:T(8,128)S(1)}, f32[64,2048]{1,0:T(8,128)S(1)}, f32[64,256]{1,0:T(8,128)S(1)}) custom-call(f32[1,1024]{1,0:T(1,128)S(1)} %get-tuple-element.37.live_ref, bf16[16,64,128]{2,1,0:T(8,128)(2,1)S(1)} %all_to_all.61.half_ref, f32[8,128]{1,0:T(8,128)S(1)} %get-tuple-element.53.sq_ref, ...), custom_call_target="tpu_custom_call" | custom-call | tf_op jit(solution)/shard_map/turn/pallas_call | solution.py:23
  128.4 0.2 pack.1.mine_ref
  128.6 11.7 %collective-permute-start.3 = (f32[16,8576]{1,0:T(8,128)S(1)}, f32[16,8576]{1,0:T(8,128)S(1)}, u32[]{:S(2)}, u32[]{:S(2)}) collective-permute-start(f32[16,8576]{1,0:T(8,128)S(1)} %pack.1.mine_ref), channel_id=1, source_target_pairs={{0,8},{8,0},{1,9},{9,1},{2,10},{10,2},{3,11},{11,3},{4,12},{12,4},... | collective-permute-start | bytes 1646600 | tf_op jit(solution)/shard_map/ppermute | solution.py:223
  140.3 17.9 %all_to_all.62.everyone_ref = f32[256,1,128]{2,1,0:T(1,128)S(1)} all-to-all(f32[256,1,128]{2,1,0:T(1,128)S(1)} %get-tuple-element.56), channel_id=1, replica_groups=mesh['y'=4,'x'=4,'core'=2,'grp'=8] {'y','x','core','grp'}, dimensions={0} | all-to-all | bytes 262144 | tf_op jit(solution)/shard_map/all_to_all | solution.py:219
  158.2 0.0 collective-permute-done.3.twin_ref
  158.2 1.1 final.1
  (6 shorter events, 0.2 us)
Async XLA Ops:
  0.6 8.8 %collective-permute-start.2 = (bf16[512,2048]{1,0:T(8,128)(2,1)}, bf16[512,2048]{1,0:T(8,128)(2,1)S(1)}, u32[]{:S(2)}, u32[]{:S(2)}) collective-permute-start(bf16[512,2048]{1,0:T(8,128)(2,1)} %a_own.7), channel_id=1, source_target_pairs={{0,8},{8,0},{1,9},{9,1},{2,10},{10,2},{3,11},{11,3},{4,12},{12,4},... | collective-permute-start | bytes 6291464 | tf_op jit(solution)/shard_map/ppermute | solution.py:223
  3.9 5.5 %collective-permute-start.1 = (bf16[512,128]{1,0:T(8,128)(2,1)}, bf16[512,128]{1,0:T(8,128)(2,1)S(1)}, u32[]{:S(2)}, u32[]{:S(2)}) collective-permute-start(bf16[512,128]{1,0:T(8,128)(2,1)} %b_own), channel_id=1, source_target_pairs={{0,8},{8,0},{1,9},{9,1},{2,10},{10,2},{3,11},{11,3},{4,12},{12,4},... | collective-permute-start | bytes 393224 | tf_op jit(solution)/shard_map/ppermute | solution.py:223
  4.0 5.4 %collective-permute-start = (s32[1]{0:T(128)}, s32[1]{0:T(128)}, u32[]{:S(2)}, u32[]{:S(2)}) collective-permute-start(s32[1]{0:T(128)} %param.7), channel_id=1, source_target_pairs={{0,8},{8,0},{1,9},{9,1},{2,10},{10,2},{3,11},{11,3},{4,12},{12,4},... | collective-permute-start | bytes 20 | tf_op jit(solution)/shard_map/ppermute | solution.py:223
  5.1 4.3 %copy-start = (bf16[512,2048]{1,0:T(8,128)(2,1)S(1)}, bf16[512,2048]{1,0:T(8,128)(2,1)}, u32[]{:S(2)}) copy-start(bf16[512,2048]{1,0:T(8,128)(2,1)} %a_own.7) | copy-start | bytes 6291460
  5.1 4.3 %copy-start.1 = (bf16[512,128]{1,0:T(8,128)(2,1)S(1)}, bf16[512,128]{1,0:T(8,128)(2,1)}, u32[]{:S(2)}) copy-start(bf16[512,128]{1,0:T(8,128)(2,1)} %b_own) | copy-start | bytes 393220
  128.6 29.6 %collective-permute-start.3 = (f32[16,8576]{1,0:T(8,128)S(1)}, f32[16,8576]{1,0:T(8,128)S(1)}, u32[]{:S(2)}, u32[]{:S(2)}) collective-permute-start(f32[16,8576]{1,0:T(8,128)S(1)} %pack.1.mine_ref), channel_id=1, source_target_pairs={{0,8},{8,0},{1,9},{9,1},{2,10},{10,2},{3,11},{11,3},{4,12},{12,4},... | collective-permute-start | bytes 1646600 | tf_op jit(solution)/shard_map/ppermute | solution.py:223

commit v7 on v6

--- a/solution.py
+++ b/solution.py
@@ -50,7 +50,10 @@
 
 
 def nn(left, right):
-    return jnp.dot(left, right, preferred_element_type=f32)
+    rows = left.shape[0]
+    if rows < LANES:
+        left = jnp.concatenate([left] * (LANES // rows))
+    return jnp.dot(left, right, preferred_element_type=f32)[:rows]
 
 
 def squares_of(residue):
@@ -88,18 +91,21 @@
         turned[:, at : at + LOAD_ROWS] = held[at : at + LOAD_ROWS, :].T
 
 
-def start_body(own_count, twin_count, b_own, b_twin, a_own, a_twin, tiles_ref, residue_ref, live_ref, turned_own, turned_twin, work):
+def start_body(own_count, twin_count, b_own, b_twin, a_own, a_twin, tiles_ref, residue_ref, live_ref, turned_own, turned_twin, work, count, arrived):
+    counting = pltpu.make_async_copy(twin_count, count, arrived)
+    counting.start()
     cols = residue_ref.shape[0]
     rows = b_own.shape[0]
     work[:, :rows] = b_own[...].astype(f32).T
     work[:, rows:] = b_twin[...].astype(f32).T
     mine = work[pl.ds(pl.multiple_of(lax.axis_index("core") * cols, cols), cols), :]
+    turned_own[...] = a_own[...].T
+    counting.wait()
     slot = lax.broadcasted_iota(jnp.int32, (1, rows), 1)
-    live = jnp.concatenate([slot < own_count[...], slot < twin_count[...]], axis=1).astype(f32)
+    live = jnp.concatenate([slot < own_count[0], slot < count[0]], axis=1).astype(f32)
     live_ref[...] = live
     residue = live * mine
     residue_ref[...] = residue
-    turned_own[...] = a_own[...].T
     turned_twin[...] = a_twin[...].T
     write_tiles(residue, a_own, a_twin, tiles_ref)
 
@@ -257,7 +263,6 @@
         scratch=[pltpu.SemaphoreType.DMA((width // LOAD_ROWS,))],
         limit=36 * 1024 * 1024,
     )
-    counts = [row_counts.reshape(1, 1), twin_counts.reshape(1, 1)]
     right_side, turned = lax.optimization_barrier((right_side, turned))
     tiles, residue, live, turned_own, turned_twin = run(
         start_body,
@@ -268,10 +273,14 @@
             (matrix.shape[::-1], bf16),
             (matrix.shape[::-1], bf16),
         ],
-        [*counts, right_side, twin_side, *blocks],
-        [VMEM] * 6,
+        [row_counts, twin_counts, right_side, twin_side, *blocks],
+        [pl.BlockSpec(memory_space=pltpu.SMEM), pl.BlockSpec(memory_space=pltpu.HBM)] + [VMEM] * 4,
         "start",
-        scratch=[pltpu.VMEM((2 * cols, 2 * local_rows), f32)],
+        scratch=[
+            pltpu.VMEM((2 * cols, 2 * local_rows), f32),
+            pltpu.SMEM((1,), jnp.int32),
+            pltpu.SemaphoreType.DMA(()),
+        ],
         limit=12 * 1024 * 1024,
     )
 

time: 160 us -> 157 us (0.981)
  Pallas kernels: 22.2 us -> 19.7 us
    pallas_call x13, Pallas kernels: 22.2 us -> 19.7 us  [run(): pl.pallas_call(body, out_shape=[jax.ShapeDtypeStruct(s, t) for s, t in sh...]
where the time goes in v7:
time: 157 us
  blocking collectives  120 us (76%)
  Pallas kernels  19.7 us (13%)
  starting transfers between devices  15.5 us (10%)
    all_to_all x10, blocking collectives, exchange(): return lax.all_to_all(tiles, axis, 0, 0, tiled=True)  120 us
    pallas_call x13, Pallas kernels, run(): pl.pallas_call(body, out_shape=[jax.ShapeDtypeStruct(s, t) for s, t in sh...  19.7 us
    ppermute x4, starting transfers between devices, swap_cores(): return lax.ppermute(value, 'core', [(0, 1), (1, 0)])  15.5 us
  transfers between devices with their start and end apart: 4, of which 0 were waited for; matrix products, arithmetic and copies ran while one was open for 0% of the time, Pallas kernels for 3%

profile of v7, /device:TPU:1, one launch (start us, length us, event | category | flops | bytes accessed | tf_op | source)
XLA Modules:
  0.0 156.7 jit_solution(6918513660951078008)
XLA Ops:
  0.6 3.3 %collective-permute-start.2 = (bf16[512,2048]{1,0:T(8,128)(2,1)}, bf16[512,2048]{1,0:T(8,128)(2,1)S(1)}, u32[]{:S(2)}, u32[]{:S(2)}) collective-permute-start(bf16[512,2048]{1,0:T(8,128)(2,1)} %a_own.7), channel_id=1, source_target_pairs={{0,8},{8,0},{1,9},{9,1},{2,10},{10,2},{3,11},{11,3},{4,12},{12,4},... | collective-permute-start | bytes 6291464 | tf_op jit(solution)/shard_map/ppermute | solution.py:229
  3.9 0.1 collective-permute-start.1
  4.0 0.4 collective-permute-start
  5.1 0.0 copy-start
  5.1 0.0 copy-start.1
  5.1 4.3 %load.1 = (bf16[2048,2048]{1,0:T(8,128)(2,1)S(1)}, bf16[2048,2048]{1,0:T(8,128)(2,1)S(1)}) custom-call(bf16[2048,2048]{1,0:T(8,128)(2,1)} %source.1), custom_call_target="tpu_custom_call" | custom-call | tf_op jit(solution)/shard_map/load/pallas_call | solution.py:23
  9.4 0.0 collective-permute-done.twin_count
  9.4 0.0 collective-permute-done.1.b_twin
  9.4 0.0 collective-permute-done.2.a_twin
  9.4 0.0 copy-done
  9.4 0.0 copy-done.1
  9.4 2.6 %start.1 = (bf16[16,72,128]{2,1,0:T(8,128)(2,1)S(1)}, f32[64,1024]{1,0:T(8,128)S(1)}, f32[1,1024]{1,0:T(1,128)S(1)}, bf16[2048,512]{1,0:T(8,128)(2,1)S(1)}, bf16[2048,512]{1,0:T(8,128)(2,1)S(1)}) custom-call(s32[1]{0:T(128)S(6)} %copy.7.own_count, s32[1]{0:T(128)} %collective-permute-done.twin_count, bf16[512,128]{1,0:T(8,128)(2,1)S(1)} %copy-done.1, ...), custom_call_target="tpu_custom_call" | custom-call | tf_op jit(solution)/shard_map/start/pallas_call | solution.py:23
  12.1 13.6 %all_to_all.53.tiles_ref = bf16[16,72,128]{2,1,0:T(8,128)(2,1)S(1)} all-to-all(bf16[16,72,128]{2,1,0:T(8,128)(2,1)S(1)} %get-tuple-element.38), channel_id=1, replica_groups=mesh['y'=4,'x'=4,'core'=2,'grp'=8] {'y','x'}, dimensions={0} | all-to-all | bytes 589824 | tf_op jit(solution)/shard_map/all_to_all | solution.py:225
  25.7 16.2 %all_to_all.54.tiles_ref = bf16[8,72,128]{2,1,0:T(8,128)(2,1)S(1)} all-to-all(bf16[8,72,128]{2,1,0:T(8,128)(2,1)S(1)} %plane_sum.3), channel_id=1, replica_groups=mesh['y'=4,'x'=4,'core'=2,'grp'=8] {'grp'}, dimensions={0} | all-to-all | bytes 294912 | tf_op jit(solution)/shard_map/all_to_all | solution.py:225
  41.9 10.2 %all_to_all.55.half_ref = bf16[16,64,128]{2,1,0:T(8,128)(2,1)S(1)} all-to-all(bf16[16,64,128]{2,1,0:T(8,128)(2,1)S(1)} %get-tuple-element.39), channel_id=1, replica_groups=mesh['y'=4,'x'=4,'core'=2,'grp'=8] {'y','x'}, dimensions={0} | all-to-all | bytes 524288 | tf_op jit(solution)/shard_map/all_to_all | solution.py:225
  52.2 3.7 %turn.3 = (bf16[16,72,128]{2,1,0:T(8,128)(2,1)S(1)}, f32[64,1024]{1,0:T(8,128)S(1)}, f32[64,2048]{1,0:T(8,128)S(1)}, f32[64,2048]{1,0:T(8,128)S(1)}, f32[64,256]{1,0:T(8,128)S(1)}) custom-call(f32[1,1024]{1,0:T(1,128)S(1)} %get-tuple-element.37.live_ref, bf16[16,64,128]{2,1,0:T(8,128)(2,1)S(1)} %all_to_all.55.half_ref, ...), custom_call_target="tpu_custom_call" | custom-call | tf_op jit(solution)/shard_map/turn/pallas_call | solution.py:23
  55.9 10.6 %all_to_all.56.tiles_ref = bf16[16,72,128]{2,1,0:T(8,128)(2,1)S(1)} all-to-all(bf16[16,72,128]{2,1,0:T(8,128)(2,1)S(1)} %get-tuple-element.46), channel_id=1, replica_groups=mesh['y'=4,'x'=4,'core'=2,'grp'=8] {'y','x'}, dimensions={0} | all-to-all | bytes 589824 | tf_op jit(solution)/shard_map/all_to_all | solution.py:225
  66.5 10.5 %all_to_all.57.tiles_ref = bf16[8,72,128]{2,1,0:T(8,128)(2,1)S(1)} all-to-all(bf16[8,72,128]{2,1,0:T(8,128)(2,1)S(1)} %plane_sum.4), channel_id=1, replica_groups=mesh['y'=4,'x'=4,'core'=2,'grp'=8] {'grp'}, dimensions={0} | all-to-all | bytes 294912 | tf_op jit(solution)/shard_map/all_to_all | solution.py:225
  77.0 10.1 %all_to_all.58.half_ref = bf16[16,64,128]{2,1,0:T(8,128)(2,1)S(1)} all-to-all(bf16[16,64,128]{2,1,0:T(8,128)(2,1)S(1)} %get-tuple-element.47), channel_id=1, replica_groups=mesh['y'=4,'x'=4,'core'=2,'grp'=8] {'y','x'}, dimensions={0} | all-to-all | bytes 524288 | tf_op jit(solution)/shard_map/all_to_all | solution.py:225
  87.2 3.7 %turn.4 = (bf16[16,72,128]{2,1,0:T(8,128)(2,1)S(1)}, f32[64,1024]{1,0:T(8,128)S(1)}, f32[64,2048]{1,0:T(8,128)S(1)}, f32[64,2048]{1,0:T(8,128)S(1)}, f32[64,256]{1,0:T(8,128)S(1)}) custom-call(f32[1,1024]{1,0:T(1,128)S(1)} %get-tuple-element.37.live_ref, bf16[16,64,128]{2,1,0:T(8,128)(2,1)S(1)} %all_to_all.58.half_ref, ...), custom_call_target="tpu_custom_call" | custom-call | tf_op jit(solution)/shard_map/turn/pallas_call | solution.py:23
  90.9 10.4 %all_to_all.59.tiles_ref = bf16[16,72,128]{2,1,0:T(8,128)(2,1)S(1)} all-to-all(bf16[16,72,128]{2,1,0:T(8,128)(2,1)S(1)} %get-tuple-element.51), channel_id=1, replica_groups=mesh['y'=4,'x'=4,'core'=2,'grp'=8] {'y','x'}, dimensions={0} | all-to-all | bytes 589824 | tf_op jit(solution)/shard_map/all_to_all | solution.py:225
  101.3 10.5 %all_to_all.60.tiles_ref = bf16[8,72,128]{2,1,0:T(8,128)(2,1)S(1)} all-to-all(bf16[8,72,128]{2,1,0:T(8,128)(2,1)S(1)} %plane_sum.5), channel_id=1, replica_groups=mesh['y'=4,'x'=4,'core'=2,'grp'=8] {'grp'}, dimensions={0} | all-to-all | bytes 294912 | tf_op jit(solution)/shard_map/all_to_all | solution.py:225
  111.8 10.1 %all_to_all.61.half_ref = bf16[16,64,128]{2,1,0:T(8,128)(2,1)S(1)} all-to-all(bf16[16,64,128]{2,1,0:T(8,128)(2,1)S(1)} %get-tuple-element.52), channel_id=1, replica_groups=mesh['y'=4,'x'=4,'core'=2,'grp'=8] {'y','x'}, dimensions={0} | all-to-all | bytes 524288 | tf_op jit(solution)/shard_map/all_to_all | solution.py:225
  122.0 3.9 %turn.5 = (f32[256,1,128]{2,1,0:T(1,128)S(1)}, f32[64,1024]{1,0:T(8,128)}, f32[64,2048]{1,0:T(8,128)S(1)}, f32[64,2048]{1,0:T(8,128)S(1)}, f32[64,256]{1,0:T(8,128)S(1)}) custom-call(f32[1,1024]{1,0:T(1,128)S(1)} %get-tuple-element.37.live_ref, bf16[16,64,128]{2,1,0:T(8,128)(2,1)S(1)} %all_to_all.61.half_ref, f32[8,128]{1,0:T(8,128)S(1)} %get-tuple-element.53.sq_ref, ...), custom_call_target="tpu_custom_call" | custom-call | tf_op jit(solution)/shard_map/turn/pallas_call | solution.py:23
  125.9 0.2 pack.1.mine_ref
  126.0 11.7 %collective-permute-start.3 = (f32[16,8576]{1,0:T(8,128)S(1)}, f32[16,8576]{1,0:T(8,128)S(1)}, u32[]{:S(2)}, u32[]{:S(2)}) collective-permute-start(f32[16,8576]{1,0:T(8,128)S(1)} %pack.1.mine_ref), channel_id=1, source_target_pairs={{0,8},{8,0},{1,9},{9,1},{2,10},{10,2},{3,11},{11,3},{4,12},{12,4},... | collective-permute-start | bytes 1646600 | tf_op jit(solution)/shard_map/ppermute | solution.py:229
  137.8 17.9 %all_to_all.62.everyone_ref = f32[256,1,128]{2,1,0:T(1,128)S(1)} all-to-all(f32[256,1,128]{2,1,0:T(1,128)S(1)} %get-tuple-element.56), channel_id=1, replica_groups=mesh['y'=4,'x'=4,'core'=2,'grp'=8] {'y','x','core','grp'}, dimensions={0} | all-to-all | bytes 262144 | tf_op jit(solution)/shard_map/all_to_all | solution.py:225
  155.7 0.0 collective-permute-done.3.twin_ref
  155.7 1.1 final.1
  (6 shorter events, 0.2 us)
Async XLA Ops:
  0.6 8.8 %collective-permute-start.2 = (bf16[512,2048]{1,0:T(8,128)(2,1)}, bf16[512,2048]{1,0:T(8,128)(2,1)S(1)}, u32[]{:S(2)}, u32[]{:S(2)}) collective-permute-start(bf16[512,2048]{1,0:T(8,128)(2,1)} %a_own.7), channel_id=1, source_target_pairs={{0,8},{8,0},{1,9},{9,1},{2,10},{10,2},{3,11},{11,3},{4,12},{12,4},... | collective-permute-start | bytes 6291464 | tf_op jit(solution)/shard_map/ppermute | solution.py:229
  3.9 5.5 %collective-permute-start.1 = (bf16[512,128]{1,0:T(8,128)(2,1)}, bf16[512,128]{1,0:T(8,128)(2,1)S(1)}, u32[]{:S(2)}, u32[]{:S(2)}) collective-permute-start(bf16[512,128]{1,0:T(8,128)(2,1)} %b_own), channel_id=1, source_target_pairs={{0,8},{8,0},{1,9},{9,1},{2,10},{10,2},{3,11},{11,3},{4,12},{12,4},... | collective-permute-start | bytes 393224 | tf_op jit(solution)/shard_map/ppermute | solution.py:229
  4.0 5.4 %collective-permute-start = (s32[1]{0:T(128)}, s32[1]{0:T(128)}, u32[]{:S(2)}, u32[]{:S(2)}) collective-permute-start(s32[1]{0:T(128)} %param.7), channel_id=1, source_target_pairs={{0,8},{8,0},{1,9},{9,1},{2,10},{10,2},{3,11},{11,3},{4,12},{12,4},... | collective-permute-start | bytes 20 | tf_op jit(solution)/shard_map/ppermute | solution.py:229
  5.1 4.3 %copy-start = (bf16[512,2048]{1,0:T(8,128)(2,1)S(1)}, bf16[512,2048]{1,0:T(8,128)(2,1)}, u32[]{:S(2)}) copy-start(bf16[512,2048]{1,0:T(8,128)(2,1)} %a_own.7) | copy-start | bytes 6291460
  5.1 4.3 %copy-start.1 = (bf16[512,128]{1,0:T(8,128)(2,1)S(1)}, bf16[512,128]{1,0:T(8,128)(2,1)}, u32[]{:S(2)}) copy-start(bf16[512,128]{1,0:T(8,128)(2,1)} %b_own) | copy-start | bytes 393220
  126.0 29.6 %collective-permute-start.3 = (f32[16,8576]{1,0:T(8,128)S(1)}, f32[16,8576]{1,0:T(8,128)S(1)}, u32[]{:S(2)}, u32[]{:S(2)}) collective-permute-start(f32[16,8576]{1,0:T(8,128)S(1)} %pack.1.mine_ref), channel_id=1, source_target_pairs={{0,8},{8,0},{1,9},{9,1},{2,10},{10,2},{3,11},{11,3},{4,12},{12,4},... | collective-permute-start | bytes 1646600 | tf_op jit(solution)/shard_map/ppermute | solution.py:229

commit v8 on v7

--- a/solution.py
+++ b/solution.py
@@ -96,18 +96,22 @@
     counting.start()
     cols = residue_ref.shape[0]
     rows = b_own.shape[0]
-    work[:, :rows] = b_own[...].astype(f32).T
-    work[:, rows:] = b_twin[...].astype(f32).T
-    mine = work[pl.ds(pl.multiple_of(lax.axis_index("core") * cols, cols), cols), :]
-    turned_own[...] = a_own[...].T
+    mine = pl.ds(pl.multiple_of(lax.axis_index("core") * cols, cols), cols)
+
+    def rows_of(count_value, b_ref, a_ref, turned, at):
+        work[:, at : at + rows] = b_ref[...].astype(f32).T
+        live = (lax.broadcasted_iota(jnp.int32, (1, rows), 1) < count_value).astype(f32)
+        live_ref[:, at : at + rows] = live
+        residue = live * work[mine, at : at + rows]
+        residue_ref[:, at : at + rows] = residue
+        turned[...] = a_ref[...].T
+        squares = jnp.sum(residue * residue, axis=1, keepdims=True)
+        return (nn(residue.astype(bf16), a_ref[...]), squares)
+
+    own_part, own_squares = rows_of(own_count[0], b_own, a_own, turned_own, 0)
     counting.wait()
-    slot = lax.broadcasted_iota(jnp.int32, (1, rows), 1)
-    live = jnp.concatenate([slot < own_count[0], slot < count[0]], axis=1).astype(f32)
-    live_ref[...] = live
-    residue = live * mine
-    residue_ref[...] = residue
-    turned_twin[...] = a_twin[...].T
-    write_tiles(residue, a_own, a_twin, tiles_ref)
+    twin_part, twin_squares = rows_of(count[0], b_twin, a_twin, turned_twin, rows)
+    put_tiles(own_part + twin_part, to_lanes(own_squares + twin_squares), tiles_ref)
 
 
 def turn_body(first, last, live_ref, half_ref, sq_ref, n_ref, turned_n, a_own, a_twin, turned_own, turned_twin, old_ref, *refs):

time: 157 us -> 157 us (level)
  no operation moved by 1% of the time
where the time goes in v8:
time: 157 us
  blocking collectives  120 us (76%)
  Pallas kernels  19.8 us (13%)
  starting transfers between devices  15.5 us (10%)
    all_to_all x10, blocking collectives, exchange(): return lax.all_to_all(tiles, axis, 0, 0, tiled=True)  120 us
    pallas_call x13, Pallas kernels, run(): pl.pallas_call(body, out_shape=[jax.ShapeDtypeStruct(s, t) for s, t in sh...  19.8 us
    ppermute x4, starting transfers between devices, swap_cores(): return lax.ppermute(value, 'core', [(0, 1), (1, 0)])  15.5 us
  transfers between devices with their start and end apart: 4, of which 0 were waited for; matrix products, arithmetic and copies ran while one was open for 0% of the time, Pallas kernels for 3%

profile of v8, /device:TPU:1, one launch (start us, length us, event | category | flops | bytes accessed | tf_op | source)
XLA Modules:
  0.0 156.8 jit_solution(1655260571980283037)
XLA Ops:
  0.6 3.3 %collective-permute-start.2 = (bf16[512,2048]{1,0:T(8,128)(2,1)}, bf16[512,2048]{1,0:T(8,128)(2,1)S(1)}, u32[]{:S(2)}, u32[]{:S(2)}) collective-permute-start(bf16[512,2048]{1,0:T(8,128)(2,1)} %a_own.7), channel_id=1, source_target_pairs={{0,8},{8,0},{1,9},{9,1},{2,10},{10,2},{3,11},{11,3},{4,12},{12,4},... | collective-permute-start | bytes 6291464 | tf_op jit(solution)/shard_map/ppermute | solution.py:233
  3.9 0.1 collective-permute-start.1
  4.0 0.4 collective-permute-start
  5.1 0.0 copy-start
  5.1 0.0 copy-start.1
  5.1 4.3 %load.1 = (bf16[2048,2048]{1,0:T(8,128)(2,1)S(1)}, bf16[2048,2048]{1,0:T(8,128)(2,1)S(1)}) custom-call(bf16[2048,2048]{1,0:T(8,128)(2,1)} %source.1), custom_call_target="tpu_custom_call" | custom-call | tf_op jit(solution)/shard_map/load/pallas_call | solution.py:23
  9.4 0.0 collective-permute-done.twin_count
  9.4 0.0 collective-permute-done.1.b_twin
  9.4 0.0 collective-permute-done.2.a_twin
  9.4 0.0 copy-done
  9.4 0.0 copy-done.1
  9.4 2.7 %start.1 = (bf16[16,72,128]{2,1,0:T(8,128)(2,1)S(1)}, f32[64,1024]{1,0:T(8,128)S(1)}, f32[1,1024]{1,0:T(1,128)S(1)}, bf16[2048,512]{1,0:T(8,128)(2,1)S(1)}, bf16[2048,512]{1,0:T(8,128)(2,1)S(1)}) custom-call(s32[1]{0:T(128)S(6)} %copy.7.own_count, s32[1]{0:T(128)} %collective-permute-done.twin_count, bf16[512,128]{1,0:T(8,128)(2,1)S(1)} %copy-done.1, ...), custom_call_target="tpu_custom_call" | custom-call | tf_op jit(solution)/shard_map/start/pallas_call | solution.py:23
  12.2 13.6 %all_to_all.53.tiles_ref = bf16[16,72,128]{2,1,0:T(8,128)(2,1)S(1)} all-to-all(bf16[16,72,128]{2,1,0:T(8,128)(2,1)S(1)} %get-tuple-element.38), channel_id=1, replica_groups=mesh['y'=4,'x'=4,'core'=2,'grp'=8] {'y','x'}, dimensions={0} | all-to-all | bytes 589824 | tf_op jit(solution)/shard_map/all_to_all | solution.py:229
  25.8 16.2 %all_to_all.54.tiles_ref = bf16[8,72,128]{2,1,0:T(8,128)(2,1)S(1)} all-to-all(bf16[8,72,128]{2,1,0:T(8,128)(2,1)S(1)} %plane_sum.3), channel_id=1, replica_groups=mesh['y'=4,'x'=4,'core'=2,'grp'=8] {'grp'}, dimensions={0} | all-to-all | bytes 294912 | tf_op jit(solution)/shard_map/all_to_all | solution.py:229
  42.0 10.2 %all_to_all.55.half_ref = bf16[16,64,128]{2,1,0:T(8,128)(2,1)S(1)} all-to-all(bf16[16,64,128]{2,1,0:T(8,128)(2,1)S(1)} %get-tuple-element.39), channel_id=1, replica_groups=mesh['y'=4,'x'=4,'core'=2,'grp'=8] {'y','x'}, dimensions={0} | all-to-all | bytes 524288 | tf_op jit(solution)/shard_map/all_to_all | solution.py:229
  52.3 3.7 %turn.3 = (bf16[16,72,128]{2,1,0:T(8,128)(2,1)S(1)}, f32[64,1024]{1,0:T(8,128)S(1)}, f32[64,2048]{1,0:T(8,128)S(1)}, f32[64,2048]{1,0:T(8,128)S(1)}, f32[64,256]{1,0:T(8,128)S(1)}) custom-call(f32[1,1024]{1,0:T(1,128)S(1)} %get-tuple-element.37.live_ref, bf16[16,64,128]{2,1,0:T(8,128)(2,1)S(1)} %all_to_all.55.half_ref, ...), custom_call_target="tpu_custom_call" | custom-call | tf_op jit(solution)/shard_map/turn/pallas_call | solution.py:23
  56.0 10.6 %all_to_all.56.tiles_ref = bf16[16,72,128]{2,1,0:T(8,128)(2,1)S(1)} all-to-all(bf16[16,72,128]{2,1,0:T(8,128)(2,1)S(1)} %get-tuple-element.46), channel_id=1, replica_groups=mesh['y'=4,'x'=4,'core'=2,'grp'=8] {'y','x'}, dimensions={0} | all-to-all | bytes 589824 | tf_op jit(solution)/shard_map/all_to_all | solution.py:229
  66.6 10.5 %all_to_all.57.tiles_ref = bf16[8,72,128]{2,1,0:T(8,128)(2,1)S(1)} all-to-all(bf16[8,72,128]{2,1,0:T(8,128)(2,1)S(1)} %plane_sum.4), channel_id=1, replica_groups=mesh['y'=4,'x'=4,'core'=2,'grp'=8] {'grp'}, dimensions={0} | all-to-all | bytes 294912 | tf_op jit(solution)/shard_map/all_to_all | solution.py:229
  77.1 10.1 %all_to_all.58.half_ref = bf16[16,64,128]{2,1,0:T(8,128)(2,1)S(1)} all-to-all(bf16[16,64,128]{2,1,0:T(8,128)(2,1)S(1)} %get-tuple-element.47), channel_id=1, replica_groups=mesh['y'=4,'x'=4,'core'=2,'grp'=8] {'y','x'}, dimensions={0} | all-to-all | bytes 524288 | tf_op jit(solution)/shard_map/all_to_all | solution.py:229
  87.3 3.7 %turn.4 = (bf16[16,72,128]{2,1,0:T(8,128)(2,1)S(1)}, f32[64,1024]{1,0:T(8,128)S(1)}, f32[64,2048]{1,0:T(8,128)S(1)}, f32[64,2048]{1,0:T(8,128)S(1)}, f32[64,256]{1,0:T(8,128)S(1)}) custom-call(f32[1,1024]{1,0:T(1,128)S(1)} %get-tuple-element.37.live_ref, bf16[16,64,128]{2,1,0:T(8,128)(2,1)S(1)} %all_to_all.58.half_ref, ...), custom_call_target="tpu_custom_call" | custom-call | tf_op jit(solution)/shard_map/turn/pallas_call | solution.py:23
  91.0 10.3 %all_to_all.59.tiles_ref = bf16[16,72,128]{2,1,0:T(8,128)(2,1)S(1)} all-to-all(bf16[16,72,128]{2,1,0:T(8,128)(2,1)S(1)} %get-tuple-element.51), channel_id=1, replica_groups=mesh['y'=4,'x'=4,'core'=2,'grp'=8] {'y','x'}, dimensions={0} | all-to-all | bytes 589824 | tf_op jit(solution)/shard_map/all_to_all | solution.py:229
  101.4 10.5 %all_to_all.60.tiles_ref = bf16[8,72,128]{2,1,0:T(8,128)(2,1)S(1)} all-to-all(bf16[8,72,128]{2,1,0:T(8,128)(2,1)S(1)} %plane_sum.5), channel_id=1, replica_groups=mesh['y'=4,'x'=4,'core'=2,'grp'=8] {'grp'}, dimensions={0} | all-to-all | bytes 294912 | tf_op jit(solution)/shard_map/all_to_all | solution.py:229
  111.9 10.1 %all_to_all.61.half_ref = bf16[16,64,128]{2,1,0:T(8,128)(2,1)S(1)} all-to-all(bf16[16,64,128]{2,1,0:T(8,128)(2,1)S(1)} %get-tuple-element.52), channel_id=1, replica_groups=mesh['y'=4,'x'=4,'core'=2,'grp'=8] {'y','x'}, dimensions={0} | all-to-all | bytes 524288 | tf_op jit(solution)/shard_map/all_to_all | solution.py:229
  122.1 3.9 %turn.5 = (f32[256,1,128]{2,1,0:T(1,128)S(1)}, f32[64,1024]{1,0:T(8,128)}, f32[64,2048]{1,0:T(8,128)S(1)}, f32[64,2048]{1,0:T(8,128)S(1)}, f32[64,256]{1,0:T(8,128)S(1)}) custom-call(f32[1,1024]{1,0:T(1,128)S(1)} %get-tuple-element.37.live_ref, bf16[16,64,128]{2,1,0:T(8,128)(2,1)S(1)} %all_to_all.61.half_ref, f32[8,128]{1,0:T(8,128)S(1)} %get-tuple-element.53.sq_ref, ...), custom_call_target="tpu_custom_call" | custom-call | tf_op jit(solution)/shard_map/turn/pallas_call | solution.py:23
  125.9 0.2 pack.1.mine_ref
  126.1 11.7 %collective-permute-start.3 = (f32[16,8576]{1,0:T(8,128)S(1)}, f32[16,8576]{1,0:T(8,128)S(1)}, u32[]{:S(2)}, u32[]{:S(2)}) collective-permute-start(f32[16,8576]{1,0:T(8,128)S(1)} %pack.1.mine_ref), channel_id=1, source_target_pairs={{0,8},{8,0},{1,9},{9,1},{2,10},{10,2},{3,11},{11,3},{4,12},{12,4},... | collective-permute-start | bytes 1646600 | tf_op jit(solution)/shard_map/ppermute | solution.py:233
  137.9 17.9 %all_to_all.62.everyone_ref = f32[256,1,128]{2,1,0:T(1,128)S(1)} all-to-all(f32[256,1,128]{2,1,0:T(1,128)S(1)} %get-tuple-element.56), channel_id=1, replica_groups=mesh['y'=4,'x'=4,'core'=2,'grp'=8] {'y','x','core','grp'}, dimensions={0} | all-to-all | bytes 262144 | tf_op jit(solution)/shard_map/all_to_all | solution.py:229
  155.8 0.0 collective-permute-done.3.twin_ref
  155.8 1.1 final.1
  (6 shorter events, 0.2 us)
Async XLA Ops:
  0.6 8.8 %collective-permute-start.2 = (bf16[512,2048]{1,0:T(8,128)(2,1)}, bf16[512,2048]{1,0:T(8,128)(2,1)S(1)}, u32[]{:S(2)}, u32[]{:S(2)}) collective-permute-start(bf16[512,2048]{1,0:T(8,128)(2,1)} %a_own.7), channel_id=1, source_target_pairs={{0,8},{8,0},{1,9},{9,1},{2,10},{10,2},{3,11},{11,3},{4,12},{12,4},... | collective-permute-start | bytes 6291464 | tf_op jit(solution)/shard_map/ppermute | solution.py:233
  3.9 5.5 %collective-permute-start.1 = (bf16[512,128]{1,0:T(8,128)(2,1)}, bf16[512,128]{1,0:T(8,128)(2,1)S(1)}, u32[]{:S(2)}, u32[]{:S(2)}) collective-permute-start(bf16[512,128]{1,0:T(8,128)(2,1)} %b_own), channel_id=1, source_target_pairs={{0,8},{8,0},{1,9},{9,1},{2,10},{10,2},{3,11},{11,3},{4,12},{12,4},... | collective-permute-start | bytes 393224 | tf_op jit(solution)/shard_map/ppermute | solution.py:233
  4.0 5.4 %collective-permute-start = (s32[1]{0:T(128)}, s32[1]{0:T(128)}, u32[]{:S(2)}, u32[]{:S(2)}) collective-permute-start(s32[1]{0:T(128)} %param.7), channel_id=1, source_target_pairs={{0,8},{8,0},{1,9},{9,1},{2,10},{10,2},{3,11},{11,3},{4,12},{12,4},... | collective-permute-start | bytes 20 | tf_op jit(solution)/shard_map/ppermute | solution.py:233
  5.1 4.3 %copy-start = (bf16[512,2048]{1,0:T(8,128)(2,1)S(1)}, bf16[512,2048]{1,0:T(8,128)(2,1)}, u32[]{:S(2)}) copy-start(bf16[512,2048]{1,0:T(8,128)(2,1)} %a_own.7) | copy-start | bytes 6291460
  5.1 4.3 %copy-start.1 = (bf16[512,128]{1,0:T(8,128)(2,1)S(1)}, bf16[512,128]{1,0:T(8,128)(2,1)}, u32[]{:S(2)}) copy-start(bf16[512,128]{1,0:T(8,128)(2,1)} %b_own) | copy-start | bytes 393220
  126.1 29.6 %collective-permute-start.3 = (f32[16,8576]{1,0:T(8,128)S(1)}, f32[16,8576]{1,0:T(8,128)S(1)}, u32[]{:S(2)}, u32[]{:S(2)}) collective-permute-start(f32[16,8576]{1,0:T(8,128)S(1)} %pack.1.mine_ref), channel_id=1, source_target_pairs={{0,8},{8,0},{1,9},{9,1},{2,10},{10,2},{3,11},{11,3},{4,12},{12,4},... | collective-permute-start | bytes 1646600 | tf_op jit(solution)/shard_map/ppermute | solution.py:233

commit v9 on v8

--- a/solution.py
+++ b/solution.py
@@ -1,4 +1,5 @@
 import functools
+import itertools
 
 import jax
 import jax.numpy as jnp
@@ -10,7 +11,6 @@
 ITERS = 3
 
 floor_sq = 0.01
-plane = ("y", "x")
 every = ("y", "x", "core", "grp")
 SQ_ROWS = 8
 LANES = 128
@@ -225,8 +225,23 @@
     ratio_ref[...] = to_lanes(phi_bar / start_norm)[:, :share]
 
 
-def exchange(tiles, axis):
-    return lax.all_to_all(tiles, axis, 0, 0, tiled=True)
+def groups_of(kind):
+    y_size, x_size, cores, lines = (lax.axis_size(name) for name in every)
+
+    def number(y, x, core, line):
+        return ((y * x_size + x) * cores + core) * lines + line
+
+    if kind == "plane":
+        steps = itertools.product(range(2), range(2), range(0, x_size, 2), range(0, y_size, 2))
+        spots = [(y + up, x + across) for x, y, across, up in steps]
+        return [[number(y, x, core, line) for y, x in spots] for core in range(cores) for line in range(lines)]
+    spots = [*range(0, lines, 2), *range(lines - 1, 0, -2)]
+    planes = itertools.product(range(y_size), range(x_size), range(cores))
+    return [[number(y, x, core, line) for line in spots] for y, x, core in planes]
+
+
+def exchange(tiles, groups=None):
+    return lax.all_to_all(tiles, every, 0, 0, axis_index_groups=groups, tiled=True)
 
 
 def swap_cores(value):
@@ -240,16 +255,17 @@
     peers, tall, _ = tiles.shape
     kept = tall - SQ_ROWS
     lines = lax.axis_size("grp")
-    (block,) = run(plane_sum_body, [((lines, tall, LANES), bf16)], [exchange(tiles, plane)], [VMEM], "plane_sum", limit=SMALL)
+    planes = groups_of("plane")
+    (block,) = run(plane_sum_body, [((lines, tall, LANES), bf16)], [exchange(tiles, planes)], [VMEM], "plane_sum", limit=SMALL)
     half, squares = run(
         line_sum_body,
         [((peers, kept, LANES), bf16), ((SQ_ROWS, LANES), f32)],
-        [exchange(block, "grp")],
+        [exchange(block, groups_of("line"))],
         [VMEM],
         "line_sum",
         limit=SMALL,
     )
-    return (exchange(half, plane), squares)
+    return (exchange(half, planes), squares)
 
 
 def shards(matrix, right_side, precond, row_counts):
@@ -309,7 +325,7 @@
         rights.append(right_vec)
         images.append(image)
         norms.append(norm_pair)
-    everyone = exchange(tiles, every)
+    everyone = exchange(tiles)
     (tiles,) = run(tiles_body, [(tiles_shape, bf16)], [residue, *blocks], [VMEM] * 3, "tiles", limit=20 * 1024 * 1024)
     half, squares = sum_everywhere(tiles)
     turn(half, squares, right_vec, residue)

time: 157 us -> 156 us (level)
  blocking collectives: 120 us -> 118 us
    all_to_all x10, blocking collectives: 120 us -> 118 us  [exchange(): lax.all_to_all(tiles, every, 0, 0, axis_index_groups=groups, tiled=True)]
where the time goes in v9:
time: 156 us; the launch traced here: 155 us
  blocking collectives  118 us (76%)
  Pallas kernels  19.8 us (13%)
  starting transfers between devices  16 us (10%)
    all_to_all x10, blocking collectives, exchange(): lax.all_to_all(tiles, every, 0, 0, axis_index_groups=groups, tiled=True)  118 us
    pallas_call x13, Pallas kernels, run(): pl.pallas_call(body, out_shape=[jax.ShapeDtypeStruct(s, t) for s, t in sh...  19.8 us
    ppermute x4, starting transfers between devices, swap_cores(): return lax.ppermute(value, 'core', [(0, 1), (1, 0)])  16 us
  transfers between devices with their start and end apart: 4, of which 0 were waited for; matrix products, arithmetic and copies ran while one was open for 0% of the time, Pallas kernels for 3%

profile of v9, /device:TPU:1, one launch (start us, length us, event | category | flops | bytes accessed | tf_op | source)
XLA Modules:
  0.0 155.2 jit_solution(14819323291325744069)
XLA Ops:
  0.6 3.3 %collective-permute-start.2 = (bf16[512,2048]{1,0:T(8,128)(2,1)}, bf16[512,2048]{1,0:T(8,128)(2,1)S(1)}, u32[]{:S(2)}, u32[]{:S(2)}) collective-permute-start(bf16[512,2048]{1,0:T(8,128)(2,1)} %a_own.7), channel_id=1, source_target_pairs={{0,8},{8,0},{1,9},{9,1},{2,10},{10,2},{3,11},{11,3},{4,12},{12,4},... | collective-permute-start | bytes 6291464 | tf_op jit(solution)/shard_map/ppermute | solution.py:248
  3.9 0.1 collective-permute-start.1
  4.0 0.4 collective-permute-start
  5.1 0.0 copy-start
  5.1 0.0 copy-start.1
  5.1 4.3 %load.1 = (bf16[2048,2048]{1,0:T(8,128)(2,1)S(1)}, bf16[2048,2048]{1,0:T(8,128)(2,1)S(1)}) custom-call(bf16[2048,2048]{1,0:T(8,128)(2,1)} %source.1), custom_call_target="tpu_custom_call" | custom-call | tf_op jit(solution)/shard_map/load/pallas_call | solution.py:23
  9.4 0.0 collective-permute-done.twin_count
  9.4 0.0 collective-permute-done.1.b_twin
  9.4 0.0 collective-permute-done.2.a_twin
  9.4 0.0 copy-done
  9.4 0.0 copy-done.1
  9.4 2.7 %start.1 = (bf16[16,72,128]{2,1,0:T(8,128)(2,1)S(1)}, f32[64,1024]{1,0:T(8,128)S(1)}, f32[1,1024]{1,0:T(1,128)S(1)}, bf16[2048,512]{1,0:T(8,128)(2,1)S(1)}, bf16[2048,512]{1,0:T(8,128)(2,1)S(1)}) custom-call(s32[1]{0:T(128)S(6)} %copy.7.own_count, s32[1]{0:T(128)} %collective-permute-done.twin_count, bf16[512,128]{1,0:T(8,128)(2,1)S(1)} %copy-done.1, ...), custom_call_target="tpu_custom_call" | custom-call | tf_op jit(solution)/shard_map/start/pallas_call | solution.py:23
  12.2 13.2 %all_to_all.53.tiles_ref = bf16[16,72,128]{2,1,0:T(8,128)(2,1)S(1)} all-to-all(bf16[16,72,128]{2,1,0:T(8,128)(2,1)S(1)} %get-tuple-element.38), channel_id=1, replica_groups={{0,128,32,160,64,192,96,224,16,144,48,176,80,208,112,240},{1,129,33,161..., dimensions={0} | all-to-all | bytes 589824 | tf_op jit(solution)/shard_map/all_to_all | solution.py:244
  25.4 15.5 %all_to_all.54.tiles_ref = bf16[8,72,128]{2,1,0:T(8,128)(2,1)S(1)} all-to-all(bf16[8,72,128]{2,1,0:T(8,128)(2,1)S(1)} %plane_sum.3), channel_id=1, replica_groups={{0,2,4,6,7,5,3,1},{8,10,12,14,15,13,11,9},{16,18,20,22,23,21,19,17},{24..., dimensions={0} | all-to-all | bytes 294912 | tf_op jit(solution)/shard_map/all_to_all | solution.py:244
  41.0 10.5 %all_to_all.55.half_ref = bf16[16,64,128]{2,1,0:T(8,128)(2,1)S(1)} all-to-all(bf16[16,64,128]{2,1,0:T(8,128)(2,1)S(1)} %get-tuple-element.39), channel_id=1, replica_groups={{0,128,32,160,64,192,96,224,16,144,48,176,80,208,112,240},{1,129,33,161..., dimensions={0} | all-to-all | bytes 524288 | tf_op jit(solution)/shard_map/all_to_all | solution.py:244
  51.5 3.7 %turn.3 = (bf16[16,72,128]{2,1,0:T(8,128)(2,1)S(1)}, f32[64,1024]{1,0:T(8,128)S(1)}, f32[64,2048]{1,0:T(8,128)S(1)}, f32[64,2048]{1,0:T(8,128)S(1)}, f32[64,256]{1,0:T(8,128)S(1)}) custom-call(f32[1,1024]{1,0:T(1,128)S(1)} %get-tuple-element.37.live_ref, bf16[16,64,128]{2,1,0:T(8,128)(2,1)S(1)} %all_to_all.55.half_ref, ...), custom_call_target="tpu_custom_call" | custom-call | tf_op jit(solution)/shard_map/turn/pallas_call | solution.py:23
  55.2 10.3 %all_to_all.56.tiles_ref = bf16[16,72,128]{2,1,0:T(8,128)(2,1)S(1)} all-to-all(bf16[16,72,128]{2,1,0:T(8,128)(2,1)S(1)} %get-tuple-element.46), channel_id=1, replica_groups={{0,128,32,160,64,192,96,224,16,144,48,176,80,208,112,240},{1,129,33,161..., dimensions={0} | all-to-all | bytes 589824 | tf_op jit(solution)/shard_map/all_to_all | solution.py:244
  65.6 9.8 %all_to_all.57.tiles_ref = bf16[8,72,128]{2,1,0:T(8,128)(2,1)S(1)} all-to-all(bf16[8,72,128]{2,1,0:T(8,128)(2,1)S(1)} %plane_sum.4), channel_id=1, replica_groups={{0,2,4,6,7,5,3,1},{8,10,12,14,15,13,11,9},{16,18,20,22,23,21,19,17},{24..., dimensions={0} | all-to-all | bytes 294912 | tf_op jit(solution)/shard_map/all_to_all | solution.py:244
  75.4 10.2 %all_to_all.58.half_ref = bf16[16,64,128]{2,1,0:T(8,128)(2,1)S(1)} all-to-all(bf16[16,64,128]{2,1,0:T(8,128)(2,1)S(1)} %get-tuple-element.47), channel_id=1, replica_groups={{0,128,32,160,64,192,96,224,16,144,48,176,80,208,112,240},{1,129,33,161..., dimensions={0} | all-to-all | bytes 524288 | tf_op jit(solution)/shard_map/all_to_all | solution.py:244
  85.7 3.8 %turn.4 = (bf16[16,72,128]{2,1,0:T(8,128)(2,1)S(1)}, f32[64,1024]{1,0:T(8,128)S(1)}, f32[64,2048]{1,0:T(8,128)S(1)}, f32[64,2048]{1,0:T(8,128)S(1)}, f32[64,256]{1,0:T(8,128)S(1)}) custom-call(f32[1,1024]{1,0:T(1,128)S(1)} %get-tuple-element.37.live_ref, bf16[16,64,128]{2,1,0:T(8,128)(2,1)S(1)} %all_to_all.58.half_ref, ...), custom_call_target="tpu_custom_call" | custom-call | tf_op jit(solution)/shard_map/turn/pallas_call | solution.py:23
  89.4 10.4 %all_to_all.59.tiles_ref = bf16[16,72,128]{2,1,0:T(8,128)(2,1)S(1)} all-to-all(bf16[16,72,128]{2,1,0:T(8,128)(2,1)S(1)} %get-tuple-element.51), channel_id=1, replica_groups={{0,128,32,160,64,192,96,224,16,144,48,176,80,208,112,240},{1,129,33,161..., dimensions={0} | all-to-all | bytes 589824 | tf_op jit(solution)/shard_map/all_to_all | solution.py:244
  99.8 9.8 %all_to_all.60.tiles_ref = bf16[8,72,128]{2,1,0:T(8,128)(2,1)S(1)} all-to-all(bf16[8,72,128]{2,1,0:T(8,128)(2,1)S(1)} %plane_sum.5), channel_id=1, replica_groups={{0,2,4,6,7,5,3,1},{8,10,12,14,15,13,11,9},{16,18,20,22,23,21,19,17},{24..., dimensions={0} | all-to-all | bytes 294912 | tf_op jit(solution)/shard_map/all_to_all | solution.py:244
  109.7 10.2 %all_to_all.61.half_ref = bf16[16,64,128]{2,1,0:T(8,128)(2,1)S(1)} all-to-all(bf16[16,64,128]{2,1,0:T(8,128)(2,1)S(1)} %get-tuple-element.52), channel_id=1, replica_groups={{0,128,32,160,64,192,96,224,16,144,48,176,80,208,112,240},{1,129,33,161..., dimensions={0} | all-to-all | bytes 524288 | tf_op jit(solution)/shard_map/all_to_all | solution.py:244
  119.9 3.9 %turn.5 = (f32[256,1,128]{2,1,0:T(1,128)S(1)}, f32[64,1024]{1,0:T(8,128)}, f32[64,2048]{1,0:T(8,128)S(1)}, f32[64,2048]{1,0:T(8,128)S(1)}, f32[64,256]{1,0:T(8,128)S(1)}) custom-call(f32[1,1024]{1,0:T(1,128)S(1)} %get-tuple-element.37.live_ref, bf16[16,64,128]{2,1,0:T(8,128)(2,1)S(1)} %all_to_all.61.half_ref, f32[8,128]{1,0:T(8,128)S(1)} %get-tuple-element.53.sq_ref, ...), custom_call_target="tpu_custom_call" | custom-call | tf_op jit(solution)/shard_map/turn/pallas_call | solution.py:23
  123.8 0.2 pack.1.mine_ref
  124.0 12.2 %collective-permute-start.3 = (f32[16,8576]{1,0:T(8,128)S(1)}, f32[16,8576]{1,0:T(8,128)S(1)}, u32[]{:S(2)}, u32[]{:S(2)}) collective-permute-start(f32[16,8576]{1,0:T(8,128)S(1)} %pack.1.mine_ref), channel_id=1, source_target_pairs={{0,8},{8,0},{1,9},{9,1},{2,10},{10,2},{3,11},{11,3},{4,12},{12,4},... | collective-permute-start | bytes 1646600 | tf_op jit(solution)/shard_map/ppermute | solution.py:248
  136.2 17.9 %all_to_all.62.everyone_ref = f32[256,1,128]{2,1,0:T(1,128)S(1)} all-to-all(f32[256,1,128]{2,1,0:T(1,128)S(1)} %get-tuple-element.56), channel_id=1, replica_groups=mesh['y'=4,'x'=4,'core'=2,'grp'=8] {'y','x','core','grp'}, dimensions={0} | all-to-all | bytes 262144 | tf_op jit(solution)/shard_map/all_to_all | solution.py:244
  154.1 0.0 collective-permute-done.3.twin_ref
  154.1 1.1 final.1
  (6 shorter events, 0.2 us)
Async XLA Ops:
  0.6 8.8 %collective-permute-start.2 = (bf16[512,2048]{1,0:T(8,128)(2,1)}, bf16[512,2048]{1,0:T(8,128)(2,1)S(1)}, u32[]{:S(2)}, u32[]{:S(2)}) collective-permute-start(bf16[512,2048]{1,0:T(8,128)(2,1)} %a_own.7), channel_id=1, source_target_pairs={{0,8},{8,0},{1,9},{9,1},{2,10},{10,2},{3,11},{11,3},{4,12},{12,4},... | collective-permute-start | bytes 6291464 | tf_op jit(solution)/shard_map/ppermute | solution.py:248
  3.9 5.5 %collective-permute-start.1 = (bf16[512,128]{1,0:T(8,128)(2,1)}, bf16[512,128]{1,0:T(8,128)(2,1)S(1)}, u32[]{:S(2)}, u32[]{:S(2)}) collective-permute-start(bf16[512,128]{1,0:T(8,128)(2,1)} %b_own), channel_id=1, source_target_pairs={{0,8},{8,0},{1,9},{9,1},{2,10},{10,2},{3,11},{11,3},{4,12},{12,4},... | collective-permute-start | bytes 393224 | tf_op jit(solution)/shard_map/ppermute | solution.py:248
  4.0 5.4 %collective-permute-start = (s32[1]{0:T(128)}, s32[1]{0:T(128)}, u32[]{:S(2)}, u32[]{:S(2)}) collective-permute-start(s32[1]{0:T(128)} %param.7), channel_id=1, source_target_pairs={{0,8},{8,0},{1,9},{9,1},{2,10},{10,2},{3,11},{11,3},{4,12},{12,4},... | collective-permute-start | bytes 20 | tf_op jit(solution)/shard_map/ppermute | solution.py:248
  5.1 4.3 %copy-start = (bf16[512,2048]{1,0:T(8,128)(2,1)S(1)}, bf16[512,2048]{1,0:T(8,128)(2,1)}, u32[]{:S(2)}) copy-start(bf16[512,2048]{1,0:T(8,128)(2,1)} %a_own.7) | copy-start | bytes 6291460
  5.1 4.3 %copy-start.1 = (bf16[512,128]{1,0:T(8,128)(2,1)S(1)}, bf16[512,128]{1,0:T(8,128)(2,1)}, u32[]{:S(2)}) copy-start(bf16[512,128]{1,0:T(8,128)(2,1)} %b_own) | copy-start | bytes 393220
  124.0 30.1 %collective-permute-start.3 = (f32[16,8576]{1,0:T(8,128)S(1)}, f32[16,8576]{1,0:T(8,128)S(1)}, u32[]{:S(2)}, u32[]{:S(2)}) collective-permute-start(f32[16,8576]{1,0:T(8,128)S(1)} %pack.1.mine_ref), channel_id=1, source_target_pairs={{0,8},{8,0},{1,9},{9,1},{2,10},{10,2},{3,11},{11,3},{4,12},{12,4},... | collective-permute-start | bytes 1646600 | tf_op jit(solution)/shard_map/ppermute | solution.py:248

commit v10 on v8

--- a/solution.py
+++ b/solution.py
@@ -225,8 +225,14 @@
     ratio_ref[...] = to_lanes(phi_bar / start_norm)[:, :share]
 
 
-def exchange(tiles, axis):
-    return lax.all_to_all(tiles, axis, 0, 0, tiled=True)
+def line_groups():
+    y_size, x_size, cores, lines = (lax.axis_size(name) for name in every)
+    spots = [*range(0, lines, 2), *range(lines - 1, 0, -2)]
+    return [[line * lines + spot for spot in spots] for line in range(y_size * x_size * cores)]
+
+
+def exchange(tiles, axis, groups=None):
+    return lax.all_to_all(tiles, axis, 0, 0, axis_index_groups=groups, tiled=True)
 
 
 def swap_cores(value):
@@ -244,7 +250,7 @@
     half, squares = run(
         line_sum_body,
         [((peers, kept, LANES), bf16), ((SQ_ROWS, LANES), f32)],
-        [exchange(block, "grp")],
+        [exchange(block, every, line_groups())],
         [VMEM],
         "line_sum",
         limit=SMALL,

time: 157 us -> 155 us (0.987)
  blocking collectives: 120 us -> 118 us
    all_to_all x10, blocking collectives: 120 us -> 118 us  [exchange(): lax.all_to_all(tiles, axis, 0, 0, axis_index_groups=groups, tiled=True)]
where the time goes in v10:
time: 155 us
  blocking collectives  118 us (76%)
  Pallas kernels  19.8 us (13%)
  starting transfers between devices  15.7 us (10%)
    all_to_all x10, blocking collectives, exchange(): lax.all_to_all(tiles, axis, 0, 0, axis_index_groups=groups, tiled=True)  118 us
    pallas_call x13, Pallas kernels, run(): pl.pallas_call(body, out_shape=[jax.ShapeDtypeStruct(s, t) for s, t in sh...  19.8 us
    ppermute x4, starting transfers between devices, swap_cores(): return lax.ppermute(value, 'core', [(0, 1), (1, 0)])  15.7 us
  transfers between devices with their start and end apart: 4, of which 0 were waited for; matrix products, arithmetic and copies ran while one was open for 0% of the time, Pallas kernels for 3%

profile of v10, /device:TPU:1, one launch (start us, length us, event | category | flops | bytes accessed | tf_op | source)
XLA Modules:
  0.0 155.0 jit_solution(490300562347936775)
XLA Ops:
  0.6 3.3 %collective-permute-start.2 = (bf16[512,2048]{1,0:T(8,128)(2,1)}, bf16[512,2048]{1,0:T(8,128)(2,1)S(1)}, u32[]{:S(2)}, u32[]{:S(2)}) collective-permute-start(bf16[512,2048]{1,0:T(8,128)(2,1)} %a_own.7), channel_id=1, source_target_pairs={{0,8},{8,0},{1,9},{9,1},{2,10},{10,2},{3,11},{11,3},{4,12},{12,4},... | collective-permute-start | bytes 6291464 | tf_op jit(solution)/shard_map/ppermute | solution.py:239
  3.9 0.1 collective-permute-start.1
  4.0 0.4 collective-permute-start
  5.1 0.0 copy-start
  5.1 0.0 copy-start.1
  5.1 4.3 %load.1 = (bf16[2048,2048]{1,0:T(8,128)(2,1)S(1)}, bf16[2048,2048]{1,0:T(8,128)(2,1)S(1)}) custom-call(bf16[2048,2048]{1,0:T(8,128)(2,1)} %source.1), custom_call_target="tpu_custom_call" | custom-call | tf_op jit(solution)/shard_map/load/pallas_call | solution.py:23
  9.4 0.0 collective-permute-done.twin_count
  9.4 0.0 collective-permute-done.1.b_twin
  9.4 0.0 collective-permute-done.2.a_twin
  9.4 0.0 copy-done
  9.4 0.0 copy-done.1
  9.4 2.7 %start.1 = (bf16[16,72,128]{2,1,0:T(8,128)(2,1)S(1)}, f32[64,1024]{1,0:T(8,128)S(1)}, f32[1,1024]{1,0:T(1,128)S(1)}, bf16[2048,512]{1,0:T(8,128)(2,1)S(1)}, bf16[2048,512]{1,0:T(8,128)(2,1)S(1)}) custom-call(s32[1]{0:T(128)S(6)} %copy.7.own_count, s32[1]{0:T(128)} %collective-permute-done.twin_count, bf16[512,128]{1,0:T(8,128)(2,1)S(1)} %copy-done.1, ...), custom_call_target="tpu_custom_call" | custom-call | tf_op jit(solution)/shard_map/start/pallas_call | solution.py:23
  12.2 13.6 %all_to_all.53.tiles_ref = bf16[16,72,128]{2,1,0:T(8,128)(2,1)S(1)} all-to-all(bf16[16,72,128]{2,1,0:T(8,128)(2,1)S(1)} %get-tuple-element.38), channel_id=1, replica_groups=mesh['y'=4,'x'=4,'core'=2,'grp'=8] {'y','x'}, dimensions={0} | all-to-all | bytes 589824 | tf_op jit(solution)/shard_map/all_to_all | solution.py:235
  25.8 15.5 %all_to_all.54.tiles_ref = bf16[8,72,128]{2,1,0:T(8,128)(2,1)S(1)} all-to-all(bf16[8,72,128]{2,1,0:T(8,128)(2,1)S(1)} %plane_sum.3), channel_id=1, replica_groups={{0,2,4,6,7,5,3,1},{8,10,12,14,15,13,11,9},{16,18,20,22,23,21,19,17},{24..., dimensions={0} | all-to-all | bytes 294912 | tf_op jit(solution)/shard_map/all_to_all | solution.py:235
  41.4 10.2 %all_to_all.55.half_ref = bf16[16,64,128]{2,1,0:T(8,128)(2,1)S(1)} all-to-all(bf16[16,64,128]{2,1,0:T(8,128)(2,1)S(1)} %get-tuple-element.39), channel_id=1, replica_groups=mesh['y'=4,'x'=4,'core'=2,'grp'=8] {'y','x'}, dimensions={0} | all-to-all | bytes 524288 | tf_op jit(solution)/shard_map/all_to_all | solution.py:235
  51.5 3.7 %turn.3 = (bf16[16,72,128]{2,1,0:T(8,128)(2,1)S(1)}, f32[64,1024]{1,0:T(8,128)S(1)}, f32[64,2048]{1,0:T(8,128)S(1)}, f32[64,2048]{1,0:T(8,128)S(1)}, f32[64,256]{1,0:T(8,128)S(1)}) custom-call(f32[1,1024]{1,0:T(1,128)S(1)} %get-tuple-element.37.live_ref, bf16[16,64,128]{2,1,0:T(8,128)(2,1)S(1)} %all_to_all.55.half_ref, ...), custom_call_target="tpu_custom_call" | custom-call | tf_op jit(solution)/shard_map/turn/pallas_call | solution.py:23
  55.2 10.6 %all_to_all.56.tiles_ref = bf16[16,72,128]{2,1,0:T(8,128)(2,1)S(1)} all-to-all(bf16[16,72,128]{2,1,0:T(8,128)(2,1)S(1)} %get-tuple-element.46), channel_id=1, replica_groups=mesh['y'=4,'x'=4,'core'=2,'grp'=8] {'y','x'}, dimensions={0} | all-to-all | bytes 589824 | tf_op jit(solution)/shard_map/all_to_all | solution.py:235
  65.9 9.8 %all_to_all.57.tiles_ref = bf16[8,72,128]{2,1,0:T(8,128)(2,1)S(1)} all-to-all(bf16[8,72,128]{2,1,0:T(8,128)(2,1)S(1)} %plane_sum.4), channel_id=1, replica_groups={{0,2,4,6,7,5,3,1},{8,10,12,14,15,13,11,9},{16,18,20,22,23,21,19,17},{24..., dimensions={0} | all-to-all | bytes 294912 | tf_op jit(solution)/shard_map/all_to_all | solution.py:235
  75.8 10.1 %all_to_all.58.half_ref = bf16[16,64,128]{2,1,0:T(8,128)(2,1)S(1)} all-to-all(bf16[16,64,128]{2,1,0:T(8,128)(2,1)S(1)} %get-tuple-element.47), channel_id=1, replica_groups=mesh['y'=4,'x'=4,'core'=2,'grp'=8] {'y','x'}, dimensions={0} | all-to-all | bytes 524288 | tf_op jit(solution)/shard_map/all_to_all | solution.py:235
  85.9 3.7 %turn.4 = (bf16[16,72,128]{2,1,0:T(8,128)(2,1)S(1)}, f32[64,1024]{1,0:T(8,128)S(1)}, f32[64,2048]{1,0:T(8,128)S(1)}, f32[64,2048]{1,0:T(8,128)S(1)}, f32[64,256]{1,0:T(8,128)S(1)}) custom-call(f32[1,1024]{1,0:T(1,128)S(1)} %get-tuple-element.37.live_ref, bf16[16,64,128]{2,1,0:T(8,128)(2,1)S(1)} %all_to_all.58.half_ref, ...), custom_call_target="tpu_custom_call" | custom-call | tf_op jit(solution)/shard_map/turn/pallas_call | solution.py:23
  89.7 10.4 %all_to_all.59.tiles_ref = bf16[16,72,128]{2,1,0:T(8,128)(2,1)S(1)} all-to-all(bf16[16,72,128]{2,1,0:T(8,128)(2,1)S(1)} %get-tuple-element.51), channel_id=1, replica_groups=mesh['y'=4,'x'=4,'core'=2,'grp'=8] {'y','x'}, dimensions={0} | all-to-all | bytes 589824 | tf_op jit(solution)/shard_map/all_to_all | solution.py:235
  100.1 9.8 %all_to_all.60.tiles_ref = bf16[8,72,128]{2,1,0:T(8,128)(2,1)S(1)} all-to-all(bf16[8,72,128]{2,1,0:T(8,128)(2,1)S(1)} %plane_sum.5), channel_id=1, replica_groups={{0,2,4,6,7,5,3,1},{8,10,12,14,15,13,11,9},{16,18,20,22,23,21,19,17},{24..., dimensions={0} | all-to-all | bytes 294912 | tf_op jit(solution)/shard_map/all_to_all | solution.py:235
  109.9 10.1 %all_to_all.61.half_ref = bf16[16,64,128]{2,1,0:T(8,128)(2,1)S(1)} all-to-all(bf16[16,64,128]{2,1,0:T(8,128)(2,1)S(1)} %get-tuple-element.52), channel_id=1, replica_groups=mesh['y'=4,'x'=4,'core'=2,'grp'=8] {'y','x'}, dimensions={0} | all-to-all | bytes 524288 | tf_op jit(solution)/shard_map/all_to_all | solution.py:235
  120.1 3.9 %turn.5 = (f32[256,1,128]{2,1,0:T(1,128)S(1)}, f32[64,1024]{1,0:T(8,128)}, f32[64,2048]{1,0:T(8,128)S(1)}, f32[64,2048]{1,0:T(8,128)S(1)}, f32[64,256]{1,0:T(8,128)S(1)}) custom-call(f32[1,1024]{1,0:T(1,128)S(1)} %get-tuple-element.37.live_ref, bf16[16,64,128]{2,1,0:T(8,128)(2,1)S(1)} %all_to_all.61.half_ref, f32[8,128]{1,0:T(8,128)S(1)} %get-tuple-element.53.sq_ref, ...), custom_call_target="tpu_custom_call" | custom-call | tf_op jit(solution)/shard_map/turn/pallas_call | solution.py:23
  124.0 0.2 pack.1.mine_ref
  124.1 11.9 %collective-permute-start.3 = (f32[16,8576]{1,0:T(8,128)S(1)}, f32[16,8576]{1,0:T(8,128)S(1)}, u32[]{:S(2)}, u32[]{:S(2)}) collective-permute-start(f32[16,8576]{1,0:T(8,128)S(1)} %pack.1.mine_ref), channel_id=1, source_target_pairs={{0,8},{8,0},{1,9},{9,1},{2,10},{10,2},{3,11},{11,3},{4,12},{12,4},... | collective-permute-start | bytes 1646600 | tf_op jit(solution)/shard_map/ppermute | solution.py:239
  136.1 17.9 %all_to_all.62.everyone_ref = f32[256,1,128]{2,1,0:T(1,128)S(1)} all-to-all(f32[256,1,128]{2,1,0:T(1,128)S(1)} %get-tuple-element.56), channel_id=1, replica_groups=mesh['y'=4,'x'=4,'core'=2,'grp'=8] {'y','x','core','grp'}, dimensions={0} | all-to-all | bytes 262144 | tf_op jit(solution)/shard_map/all_to_all | solution.py:235
  154.0 0.0 collective-permute-done.3.twin_ref
  154.0 1.1 final.1
  (6 shorter events, 0.2 us)
Async XLA Ops:
  0.6 8.8 %collective-permute-start.2 = (bf16[512,2048]{1,0:T(8,128)(2,1)}, bf16[512,2048]{1,0:T(8,128)(2,1)S(1)}, u32[]{:S(2)}, u32[]{:S(2)}) collective-permute-start(bf16[512,2048]{1,0:T(8,128)(2,1)} %a_own.7), channel_id=1, source_target_pairs={{0,8},{8,0},{1,9},{9,1},{2,10},{10,2},{3,11},{11,3},{4,12},{12,4},... | collective-permute-start | bytes 6291464 | tf_op jit(solution)/shard_map/ppermute | solution.py:239
  3.9 5.5 %collective-permute-start.1 = (bf16[512,128]{1,0:T(8,128)(2,1)}, bf16[512,128]{1,0:T(8,128)(2,1)S(1)}, u32[]{:S(2)}, u32[]{:S(2)}) collective-permute-start(bf16[512,128]{1,0:T(8,128)(2,1)} %b_own), channel_id=1, source_target_pairs={{0,8},{8,0},{1,9},{9,1},{2,10},{10,2},{3,11},{11,3},{4,12},{12,4},... | collective-permute-start | bytes 393224 | tf_op jit(solution)/shard_map/ppermute | solution.py:239
  4.0 5.4 %collective-permute-start = (s32[1]{0:T(128)}, s32[1]{0:T(128)}, u32[]{:S(2)}, u32[]{:S(2)}) collective-permute-start(s32[1]{0:T(128)} %param.7), channel_id=1, source_target_pairs={{0,8},{8,0},{1,9},{9,1},{2,10},{10,2},{3,11},{11,3},{4,12},{12,4},... | collective-permute-start | bytes 20 | tf_op jit(solution)/shard_map/ppermute | solution.py:239
  5.1 4.3 %copy-start = (bf16[512,2048]{1,0:T(8,128)(2,1)S(1)}, bf16[512,2048]{1,0:T(8,128)(2,1)}, u32[]{:S(2)}) copy-start(bf16[512,2048]{1,0:T(8,128)(2,1)} %a_own.7) | copy-start | bytes 6291460
  5.1 4.3 %copy-start.1 = (bf16[512,128]{1,0:T(8,128)(2,1)S(1)}, bf16[512,128]{1,0:T(8,128)(2,1)}, u32[]{:S(2)}) copy-start(bf16[512,128]{1,0:T(8,128)(2,1)} %b_own) | copy-start | bytes 393220
  124.1 29.8 %collective-permute-start.3 = (f32[16,8576]{1,0:T(8,128)S(1)}, f32[16,8576]{1,0:T(8,128)S(1)}, u32[]{:S(2)}, u32[]{:S(2)}) collective-permute-start(f32[16,8576]{1,0:T(8,128)S(1)} %pack.1.mine_ref), channel_id=1, source_target_pairs={{0,8},{8,0},{1,9},{9,1},{2,10},{10,2},{3,11},{11,3},{4,12},{12,4},... | collective-permute-start | bytes 1646600 | tf_op jit(solution)/shard_map/ppermute | solution.py:239
